TPU v7x, 512 devices: a whole 4x8x8 slice. The times are simulated.
512 devices in a mesh: dp: 16 (over y, x_lo), seq: 32 (over x_hi, z, core).
Axes of the slice: x: 4 (x_hi: 2, x_lo: 2; x = x_hi * 2 + x_lo), y: 8, z: 8, core: 2. Of those that a mesh axis runs over, the one named last changes fastest.
Arguments:
- queries: bfloat16 [16, 8192, 16, 128], P('dp', 'seq'), may hold values from -9 to 9
- keys: bfloat16 [16, 8192, 8, 128], P('dp', 'seq'), may hold values from -9 to 9
- values: bfloat16 [16, 8192, 8, 128], P('dp', 'seq'), may hold values from -6 to 6
- doc_lengths: int32 [16, 8], P('dp'), may hold values from 1 to 6144, 8192 in all within a row
Outputs:
- attended: bfloat16 [16, 8192, 16, 128], P('dp', 'seq')
- z_loss: float32 [], replicated
Inputs may be any that keep to these rules, and one draw needn't show every extreme that they name: `doc_lengths`: each row's 8 lengths add up to 8192, and its longest document has exactly 6144 tokens.
All inputs are finite; a program needn't handle non-finite values.
Results may differ from a plain program's by a relative error of at most 0.012.
Values may be sent and summed in bfloat16 or wider, within the bound.
No kernel may reach another device: no remote copies, remote signals or barrier semaphores. Data moves between devices by JAX's collectives and lax.ppermute only.
A program may use at most 64 MiB of HBM per device.

v0:
```python
import functools

import jax
import jax.numpy as jnp
from jax import lax
from jax.sharding import Mesh
from jax.sharding import PartitionSpec as P

WINDOW = 1024
SEQ = ("seq_0", "seq_1", "seq_2")
DP_SEQ = ("dp_0", "dp_1", "seq_0", "seq_1", "seq_2")
DP = ("dp_0", "dp_1")


rope_base = 500000.0
score_scale = 1.0 / 12.0
masked = -1e30


def shifted(block, axis, distance):
    devices = range(lax.axis_size(axis))
    route = [(i - distance, i) for i in devices if i - distance in devices]
    return lax.ppermute(block, axis, route)


def over_axes(shard, axes):
    return functools.reduce(lax.psum, axes, shard)


def rotate(tensor, places):
    half = tensor.shape[-1] // 2
    frequency = rope_base ** (-2.0 * jnp.arange(half, dtype=jnp.float32) / tensor.shape[-1])
    angles = places.astype(jnp.float32)[..., None, None] * frequency
    cos_table = jnp.cos(angles)
    sin_table = jnp.sin(angles)
    widened = tensor.astype(jnp.float32)
    front_half = widened[..., :half]
    back_half = widened[..., half:]
    joined = jnp.concatenate(
        [
            front_half * cos_table - back_half * sin_table,
            back_half * cos_table + front_half * sin_table,
        ],
        axis=-1,
    )
    return joined.astype(jnp.bfloat16)


def doc_index(doc_ends, where_at):
    return jnp.sum((doc_ends[None, :] <= where_at[:, None]).astype(jnp.int32), axis=1)


def shards(queries, keys, values, doc_lengths):
    block_rows = queries.shape[1]
    query_heads = queries.shape[2]
    head_width = queries.shape[3]
    key_heads = keys.shape[2]
    group_size = query_heads // key_heads
    seq_shards = lax.axis_size(SEQ)
    seq_index = lax.axis_index(SEQ)
    reach_blocks = min(WINDOW // block_rows, seq_shards - 1)
    doc_sizes = doc_lengths[0]
    doc_ends = jnp.cumsum(doc_sizes)
    doc_starts = doc_ends - doc_sizes
    own_rows = seq_index * block_rows + jnp.arange(block_rows, dtype=jnp.int32)
    own_doc = doc_index(doc_ends, own_rows)
    chosen = own_doc[:, None] == jnp.arange(doc_sizes.shape[0], dtype=jnp.int32)[None, :]
    own_start = jnp.sum(jnp.where(chosen, doc_starts[None, :], 0), axis=1)
    query_rot = rotate(queries[0], own_rows - own_start)
    key_rot = jnp.transpose(rotate(keys[0], own_rows - own_start), (1, 0, 2))
    value_own = jnp.transpose(values[0], (1, 0, 2))
    grouped = jnp.transpose(
        query_rot.reshape(block_rows, key_heads, group_size, head_width), (1, 0, 2, 3)
    )
    key_list = [key_rot]
    value_list = [value_own]
    current = (key_rot, value_own)
    for hop_index in range(reach_blocks):
        current = shifted((current[0], current[1]), SEQ, 1)
        key_list.append(current[0])
        value_list.append(current[1])
    near_keys = jnp.concatenate(key_list, axis=1)
    near_values = jnp.concatenate(value_list, axis=1)
    per_step = max(1, 512 // block_rows)
    step_count = -(-(reach_blocks + 1) // per_step)
    step_rows = per_step * block_rows
    extra_rows = step_count * step_rows - near_keys.shape[1]
    padded_keys = jnp.pad(near_keys, ((0, 0), (0, extra_rows), (0, 0)))
    padded_values = jnp.pad(near_values, ((0, 0), (0, extra_rows), (0, 0)))
    stack_rows = jnp.arange(step_count * step_rows, dtype=jnp.int32)
    key_at = (seq_index - stack_rows // block_rows) * block_rows + stack_rows % block_rows
    key_doc = doc_index(doc_ends, key_at)
    visible_all = (
        (own_doc[:, None] == key_doc[None, :])
        & (key_at[None, :] <= own_rows[:, None])
        & (own_rows[:, None] - key_at[None, :] < WINDOW)
        & (key_at[None, :] >= 0)
    )

    def visit(step_index, carry):
        begin = step_index * step_rows
        keys_step = lax.dynamic_slice_in_dim(padded_keys, begin, step_rows, 1)
        values_step = lax.dynamic_slice_in_dim(padded_values, begin, step_rows, 1)
        visible_step = lax.dynamic_slice_in_dim(visible_all, begin, step_rows, 1)

        def update(state):
            old_peak, old_total, old_summed = state
            scores = (
                jnp.einsum("ktgd,kud->kgtu", grouped, keys_step, preferred_element_type=jnp.float32)
                * score_scale
            )
            scores = jnp.where(visible_step[None, None], scores, masked)
            new_peak = jnp.maximum(old_peak, jnp.max(scores, axis=-1))
            weights = jnp.where(
                visible_step[None, None], jnp.exp(scores - new_peak[..., None]), 0.0
            )
            rescale = jnp.exp(old_peak - new_peak)
            new_total = old_total * rescale + jnp.sum(weights, axis=-1)
            product = jnp.einsum(
                "kgtu,kud->kgtd",
                weights.astype(jnp.bfloat16),
                values_step,
                preferred_element_type=jnp.float32,
            )
            return (new_peak, new_total, old_summed * rescale[..., None] + product)

        def unchanged(state):
            return state

        return lax.cond(jnp.any(visible_step), update, unchanged, carry)

    start_peak = jnp.full((key_heads, group_size, block_rows), masked, jnp.float32)
    start_total = jnp.zeros((key_heads, group_size, block_rows), jnp.float32)
    start_summed = jnp.zeros((key_heads, group_size, block_rows, head_width), jnp.float32)
    peak, total, summed = lax.fori_loop(
        0, step_count, visit, (start_peak, start_total, start_summed)
    )
    mixed = summed / total[..., None]
    normalizers = peak + jnp.log(total)
    attended = (
        jnp.transpose(mixed, (2, 0, 1, 3))
        .reshape(block_rows, query_heads, head_width)
        .astype(jnp.bfloat16)
    )
    local_squares = jnp.sum(normalizers * normalizers)
    all_squares = over_axes(local_squares, DP_SEQ)
    z_loss = all_squares / (lax.axis_size(DP) * seq_shards * block_rows * query_heads)
    return (attended[None], z_loss)


def solution(mesh):
    torus = Mesh(mesh.devices.reshape(8, 2, 2, 8, 2), ("dp_0", "dp_1", "seq_0", "seq_1", "seq_2"))
    in_specs = (P(DP, SEQ, None, None), P(DP, SEQ, None, None), P(DP, SEQ, None, None), P(DP, None))
    out_specs = (P(DP, SEQ, None, None), P())
    return jax.shard_map(
        shards, mesh=torus, in_specs=in_specs, out_specs=out_specs, check_vma=False
    )
```

profile of v0, /device:TPU:7, one launch (start us, length us, event | category | flops | bytes accessed | tf_op | source)
XLA Modules:
  0.0 163.2 jit_solution(11019048035592917869)
XLA Ops:
  0.7 0.8 reduce-window.4
  1.5 0.7 fusion.31
  2.1 0.1 convert_reduce_fusion.1
  2.2 0.1 select_reduce_fusion
  2.3 1.1 bitcast_convert_fusion.1
  3.4 0.5 multiply_cosine_fusion
  4.0 0.4 subtract_convert_fusion.1
  4.4 1.2 constant_dynamic-update-slice_fusion.4
  5.6 4.5 %collective-permute-start = (bf16[8,256,128]{2,1,0:T(8,128)(2,1)S(1)}, bf16[8,256,128]{2,1,0:T(8,128)(2,1)S(1)}, u32[]{:S(2)}, u32[]{:S(2)}) collective-permute-start(bf16[8,256,128]{2,1,0:T(8,128)(2,1)S(1)} %get-tuple-element.247), channel_id=1, source_target_pairs={{0,1},{1,2},{2,3},{3,4},{4,5},{5,6},{6,7},{7,8},{8,9},{9,10},{10,1... | collective-permute-start | bytes 1572872 | tf_op jit(solution)/shard_map/ppermute | solution.py:23
  10.2 0.1 copy.25
  10.3 1.9 %collective-permute-start.4 = (bf16[8,256,128]{2,1,0:T(8,128)(2,1)S(1)}, bf16[8,256,128]{2,1,0:T(8,128)(2,1)S(1)}, u32[]{:S(2)}, u32[]{:S(2)}) collective-permute-start(bf16[8,256,128]{2,1,0:T(8,128)(2,1)S(1)} %bitcast.71), channel_id=1, source_target_pairs={{0,1},{1,2},{2,3},{3,4},{4,5},{5,6},{6,7},{7,8},{8,9},{9,10},{10,1... | collective-permute-start | bytes 1572872 | tf_op jit(solution)/shard_map/ppermute | solution.py:23
  12.2 0.1 convert_reduce_fusion
  12.3 4.0 %collective-permute-done = bf16[8,256,128]{2,1,0:T(8,128)(2,1)S(1)} collective-permute-done((bf16[8,256,128]{2,1,0:T(8,128)(2,1)S(1)}, bf16[8,256,128]{2,1,0:T(8,128)(2,1)S(1)}, u32[]{:S(2)}, u32[]{:S(2)}) %collective-permute-start) | collective-permute-done | bytes 524320 | tf_op jit(solution)/shard_map/ppermute | solution.py:23
  16.3 4.4 %collective-permute-start.1 = (bf16[8,256,128]{2,1,0:T(8,128)(2,1)S(1)}, bf16[8,256,128]{2,1,0:T(8,128)(2,1)S(1)}, u32[]{:S(2)}, u32[]{:S(2)}) collective-permute-start(bf16[8,256,128]{2,1,0:T(8,128)(2,1)S(1)} %collective-permute-done), channel_id=1, source_target_pairs={{0,1},{1,2},{2,3},{3,4},{4,5},{5,6},{6,7},{7,8},{8,9},{9,10},{10,1... | collective-permute-start | bytes 1572872 | tf_op jit(solution)/shard_map/ppermute | solution.py:23
  20.7 2.4 %fusion.19 = pred[256,1536]{0,1:T(8,128)(4,1)} fusion(s32[256]{0:T(256)S(1)} %iota_add_fusion, s32[256]{0:T(256)S(1)} %convert_reduce_fusion.1, s32[1536]{0:T(1024)S(1)} %fusion.29, s32[1536]{0:T(1024)S(1)} %convert_reduce_fusion, pred[1536]{0:T(1024)(128)(4,1)S(1)} %broadcast_compare_fusion), kind=kLoop, calls=%fused_computation.26 | loop fusion | flops 2752512 | bytes 409088 | tf_op jit(solution)/shard_map/and | solution.py:94
  23.0 3.2 %collective-permute-start.5 = (bf16[8,256,128]{2,1,0:T(8,128)(2,1)S(1)}, bf16[8,256,128]{2,1,0:T(8,128)(2,1)}, u32[]{:S(2)}, u32[]{:S(2)}) collective-permute-start(bf16[8,256,128]{2,1,0:T(8,128)(2,1)S(1)} %collective-permute-done.4), channel_id=1, source_target_pairs={{0,1},{1,2},{2,3},{3,4},{4,5},{5,6},{6,7},{7,8},{8,9},{9,10},{10,1... | collective-permute-start | bytes 1572872 | tf_op jit(solution)/shard_map/ppermute | solution.py:23
  26.3 0.2 bitcast_convert_fusion
  26.5 1.2 collective-permute-done.1
  27.7 4.2 %collective-permute-start.2 = (bf16[8,256,128]{2,1,0:T(8,128)(2,1)S(1)}, bf16[8,256,128]{2,1,0:T(8,128)(2,1)}, u32[]{:S(2)}, u32[]{:S(2)}) collective-permute-start(bf16[8,256,128]{2,1,0:T(8,128)(2,1)S(1)} %collective-permute-done.1), channel_id=1, source_target_pairs={{0,1},{1,2},{2,3},{3,4},{4,5},{5,6},{6,7},{7,8},{8,9},{9,10},{10,1... | collective-permute-start | bytes 1572872 | tf_op jit(solution)/shard_map/ppermute | solution.py:23
  31.9 0.8 subtract_convert_fusion
  32.7 0.3 copy.14
  33.0 0.3 copy.15
  33.2 0.2 collective-permute-done.5
  33.4 4.2 %collective-permute-start.6 = (bf16[8,256,128]{2,1,0:T(8,128)(2,1)}, bf16[8,256,128]{2,1,0:T(8,128)(2,1)}, u32[]{:S(2)}, u32[]{:S(2)}) collective-permute-start(bf16[8,256,128]{2,1,0:T(8,128)(2,1)} %collective-permute-done.5), channel_id=1, source_target_pairs={{0,1},{1,2},{2,3},{3,4},{4,5},{5,6},{6,7},{7,8},{8,9},{9,10},{10,1... | collective-permute-start | bytes 1572872 | tf_op jit(solution)/shard_map/ppermute | solution.py:23
  37.6 0.6 maximum_bitcast_fusion
  38.3 0.9 constant_dynamic-update-slice_fusion.3
  39.2 2.7 %collective-permute-done.2 = bf16[8,256,128]{2,1,0:T(8,128)(2,1)} collective-permute-done((bf16[8,256,128]{2,1,0:T(8,128)(2,1)S(1)}, bf16[8,256,128]{2,1,0:T(8,128)(2,1)}, u32[]{:S(2)}, u32[]{:S(2)}) %collective-permute-start.2) | collective-permute-done | bytes 524320 | tf_op jit(solution)/shard_map/ppermute | solution.py:23
  41.9 1.9 %collective-permute-start.3 = (bf16[8,256,128]{2,1,0:T(8,128)(2,1)}, bf16[8,256,128]{2,1,0:T(8,128)(2,1)S(1)}, u32[]{:S(2)}, u32[]{:S(2)}) collective-permute-start(bf16[8,256,128]{2,1,0:T(8,128)(2,1)} %collective-permute-done.2), channel_id=1, source_target_pairs={{0,1},{1,2},{2,3},{3,4},{4,5},{5,6},{6,7},{7,8},{8,9},{9,10},{10,1... | collective-permute-start | bytes 1572872 | tf_op jit(solution)/shard_map/ppermute | solution.py:23
  43.9 3.9 %collective-permute-done.6 = bf16[8,256,128]{2,1,0:T(8,128)(2,1)} collective-permute-done((bf16[8,256,128]{2,1,0:T(8,128)(2,1)}, bf16[8,256,128]{2,1,0:T(8,128)(2,1)}, u32[]{:S(2)}, u32[]{:S(2)}) %collective-permute-start.6) | collective-permute-done | bytes 524320 | tf_op jit(solution)/shard_map/ppermute | solution.py:23
  47.9 1.9 %collective-permute-start.7 = (bf16[8,256,128]{2,1,0:T(8,128)(2,1)}, bf16[8,256,128]{2,1,0:T(8,128)(2,1)S(1)}, u32[]{:S(2)}, u32[]{:S(2)}) collective-permute-start(bf16[8,256,128]{2,1,0:T(8,128)(2,1)} %collective-permute-done.6), channel_id=1, source_target_pairs={{0,1},{1,2},{2,3},{3,4},{4,5},{5,6},{6,7},{7,8},{8,9},{9,10},{10,1... | collective-permute-start | bytes 1572872 | tf_op jit(solution)/shard_map/ppermute | solution.py:23
  49.8 0.9 constant_dynamic-update-slice_fusion.2
  50.6 1.1 constant_dynamic-update-slice_fusion.7
  51.8 2.0 %constant_dynamic-update-slice_fusion.1 = bf16[8,1280,128]{2,1,0:T(8,128)(2,1)} fusion(bf16[8,1280,128]{2,1,0:T(8,128)(2,1)} %constant_dynamic-update-slice_fusion.2, bf16[8,256,128]{2,1,0:T(8,128)(2,1)} %collective-permute-done.2), kind=kLoop, calls=%fused_computation.39 | loop fusion | bytes 1048576
  53.7 1.1 constant_dynamic-update-slice_fusion.6
  54.8 1.4 collective-permute-done.3
  56.2 0.9 constant_dynamic-update-slice_fusion
  57.1 3.7 %pad.7 = bf16[8,1536,128]{2,1,0:T(8,128)(2,1)} pad(bf16[8,1280,128]{2,1,0:T(8,128)(2,1)} %constant_dynamic-update-slice_fusion, bf16[]{:T(256)} %constant.130.clone.1), padding=0_0x0_256x0_0 | pad | bytes 5767170 | tf_op jit(solution)/shard_map/jit(_pad)/pad | solution.py:88
  60.8 1.4 collective-permute-done.7
  62.2 2.0 %pad.8 = bf16[8,1536,128]{2,1,0:T(8,128)(2,1)} pad(bf16[8,1280,128]{2,1,0:T(8,128)(2,1)S(1)} %constant_dynamic-update-slice_fusion.5, bf16[]{:T(256)} %constant.130.clone.1), padding=0_0x0_256x0_0 | pad | bytes 5767170 | tf_op jit(solution)/shard_map/jit(_pad)/pad | solution.py:89
  64.2 0.2 broadcast_in_dim.73
  64.4 34.5 %while.17 = (s32[]{:T(128)}, f32[8,2,256]{2,1,0:T(2,128)S(1)}, f32[8,2,256]{2,1,0:T(2,128)S(1)}, f32[8,2,256,128]{3,2,1,0:T(8,128)S(1)}, pred[256,1536]{0,1:T(8,...) while((s32[]{:T(128)}, f32[8,2,256]{2,1,0:T(2,128)S(1)}, ...), condition=%wide.region_10.11_spmd, body=%wide.region_4.10_spmd.sunk | while | flops 1102192640 | bytes 33424676 | solution.py:135
  64.4 1.7 %fusion.35 = (pred[]{:T(512)}, pred[256,512]{0,1:T(8,128)(4,1)S(1)}) fusion(pred[256,1536]{0,1:T(8,128)(4,1)} %get-tuple-element.351, s32[]{:T(128)} %select_n.97), kind=kLoop, calls=%fused_computation.72.clone.1 | loop fusion | flops 131071 | bytes 262149 | tf_op jit(solution)/shard_map/while/body/eval_jaxpr/reduce_or | solution.py:130
  66.8 9.1 %conditional.2 = ((f32[8,2,256]{2,1,0:T(2,128)S(1)}, f32[8,2,256]{2,1,0:T(2,128)S(1)}, f32[8,2,256,128]{3,2,1,0:T(8,128)S(1)})) conditional(s32[]{:T(128)} %convert_element_type.83, (f32[8,2,256]{2,1,0:T(2,128)S(1)}, f32[8,2,256]{2,1,0:T(2,128)S(1)}, f32[8,2,256,128]{3,2,1,0:T(8,128)S(1)}) %tuple.55, (pred[256,512]{0,1:T(8,128)(4,1)S(1)}, ...), branch_computations={%region_6.6_spmd, %region_7.9_spmd} | conditional | flops 1102061568 | bytes 33162272 | solution.py:130
  66.8 2.6 %fusion = (f32[8,2,256]{2,1,0:T(2,128)S(1)}, f32[8,512,256,2]{2,1,3,0:T(8,128)S(1)}) fusion(pred[256,512]{0,1:T(8,128)(4,1)S(1)} %get-tuple-element.199, bf16[8,256,2,128]{3,1,2,0:T(8,128)(2,1)S(1)} %get-tuple-element.202, bf16[8,1536,128]{2,1,0:T(8,128)(2,1)} %get-tuple-element.200, s32[]{:T(128)} %get-tuple-element.201), kind=kOutput, calls=%fused_computation.2 | convolution fusion | flops 543158272 | bytes 10633728 | tf_op jit(solution)/shard_map/while/body/eval_jaxpr/cond/branch_1_fun/ktgd,kud->kgtu/dot_general | solution.py:109
  69.5 2.0 %fusion.2 = f32[8,2,256]{2,1,0:T(2,128)S(1)} fusion(f32[8,512,256,2]{2,1,3,0:T(8,128)S(1)} %get-tuple-element.249, f32[8,2,256]{2,1,0:T(2,128)S(1)} %max.4, pred[256,512]{0,1:T(8,128)(4,1)S(1)} %get-tuple-element.199), kind=kLoop, calls=%fused_computation.4 | loop fusion | flops 10481664 | bytes 8552448 | tf_op jit(solution)/shard_map/while/body/eval_jaxpr/cond/branch_1_fun/reduce_sum | solution.py:118
  71.5 4.4 %multiply_add_fusion = f32[8,2,256,128]{3,2,1,0:T(8,128)S(1)} fusion(f32[8,2,256,128]{3,2,1,0:T(8,128)S(1)} %get-tuple-element.204, f32[8,512,256,2]{2,1,3,0:T(8,128)S(1)} %get-tuple-element.249, f32[8,2,256]{2,1,0:T(2,128)S(1)} %max.4, pred[256,512]{0,1:T(8,128)(4,1)S(1)} %get-tuple-element.199, bf16[8,1536,128]{2,1,0:T(8,128)(2,1)} %get-tuple-element.205, ...), kind=kOutput, calls=%fused_computation.7 | convolution fusion | flops 548405248 | bytes 13795840 | tf_op jit(solution)/shard_map/while/body/eval_jaxpr/cond/branch_1_fun/kgtu,kud->kgtd/dot_general | solution.py:119
  75.9 1.7 %fusion.35 = (pred[]{:T(512)}, pred[256,512]{0,1:T(8,128)(4,1)S(1)}) fusion(pred[256,1536]{0,1:T(8,128)(4,1)} %get-tuple-element.351, s32[]{:T(128)} %select_n.97), kind=kLoop, calls=%fused_computation.72.clone.1 | loop fusion | flops 131071 | bytes 262149 | tf_op jit(solution)/shard_map/while/body/eval_jaxpr/reduce_or | solution.py:130
  78.3 9.1 %conditional.2 = ((f32[8,2,256]{2,1,0:T(2,128)S(1)}, f32[8,2,256]{2,1,0:T(2,128)S(1)}, f32[8,2,256,128]{3,2,1,0:T(8,128)S(1)})) conditional(s32[]{:T(128)} %convert_element_type.83, (f32[8,2,256]{2,1,0:T(2,128)S(1)}, f32[8,2,256]{2,1,0:T(2,128)S(1)}, f32[8,2,256,128]{3,2,1,0:T(8,128)S(1)}) %tuple.55, (pred[256,512]{0,1:T(8,128)(4,1)S(1)}, ...), branch_computations={%region_6.6_spmd, %region_7.9_spmd} | conditional | flops 1102061568 | bytes 33162272 | solution.py:130
  78.3 2.6 %fusion = (f32[8,2,256]{2,1,0:T(2,128)S(1)}, f32[8,512,256,2]{2,1,3,0:T(8,128)S(1)}) fusion(pred[256,512]{0,1:T(8,128)(4,1)S(1)} %get-tuple-element.199, bf16[8,256,2,128]{3,1,2,0:T(8,128)(2,1)S(1)} %get-tuple-element.202, bf16[8,1536,128]{2,1,0:T(8,128)(2,1)} %get-tuple-element.200, s32[]{:T(128)} %get-tuple-element.201), kind=kOutput, calls=%fused_computation.2 | convolution fusion | flops 543158272 | bytes 10633728 | tf_op jit(solution)/shard_map/while/body/eval_jaxpr/cond/branch_1_fun/ktgd,kud->kgtu/dot_general | solution.py:109
  81.0 2.0 %fusion.2 = f32[8,2,256]{2,1,0:T(2,128)S(1)} fusion(f32[8,512,256,2]{2,1,3,0:T(8,128)S(1)} %get-tuple-element.249, f32[8,2,256]{2,1,0:T(2,128)S(1)} %max.4, pred[256,512]{0,1:T(8,128)(4,1)S(1)} %get-tuple-element.199), kind=kLoop, calls=%fused_computation.4 | loop fusion | flops 10481664 | bytes 8552448 | tf_op jit(solution)/shard_map/while/body/eval_jaxpr/cond/branch_1_fun/reduce_sum | solution.py:118
  83.0 4.4 %multiply_add_fusion = f32[8,2,256,128]{3,2,1,0:T(8,128)S(1)} fusion(f32[8,2,256,128]{3,2,1,0:T(8,128)S(1)} %get-tuple-element.204, f32[8,512,256,2]{2,1,3,0:T(8,128)S(1)} %get-tuple-element.249, f32[8,2,256]{2,1,0:T(2,128)S(1)} %max.4, pred[256,512]{0,1:T(8,128)(4,1)S(1)} %get-tuple-element.199, bf16[8,1536,128]{2,1,0:T(8,128)(2,1)} %get-tuple-element.205, ...), kind=kOutput, calls=%fused_computation.7 | convolution fusion | flops 548405248 | bytes 13795840 | tf_op jit(solution)/shard_map/while/body/eval_jaxpr/cond/branch_1_fun/kgtu,kud->kgtd/dot_general | solution.py:119
  87.4 1.7 %fusion.35 = (pred[]{:T(512)}, pred[256,512]{0,1:T(8,128)(4,1)S(1)}) fusion(pred[256,1536]{0,1:T(8,128)(4,1)} %get-tuple-element.351, s32[]{:T(128)} %select_n.97), kind=kLoop, calls=%fused_computation.72.clone.1 | loop fusion | flops 131071 | bytes 262149 | tf_op jit(solution)/shard_map/while/body/eval_jaxpr/reduce_or | solution.py:130
  89.8 9.1 %conditional.2 = ((f32[8,2,256]{2,1,0:T(2,128)S(1)}, f32[8,2,256]{2,1,0:T(2,128)S(1)}, f32[8,2,256,128]{3,2,1,0:T(8,128)S(1)})) conditional(s32[]{:T(128)} %convert_element_type.83, (f32[8,2,256]{2,1,0:T(2,128)S(1)}, f32[8,2,256]{2,1,0:T(2,128)S(1)}, f32[8,2,256,128]{3,2,1,0:T(8,128)S(1)}) %tuple.55, (pred[256,512]{0,1:T(8,128)(4,1)S(1)}, ...), branch_computations={%region_6.6_spmd, %region_7.9_spmd} | conditional | flops 1102061568 | bytes 33162272 | solution.py:130
  89.8 2.6 %fusion = (f32[8,2,256]{2,1,0:T(2,128)S(1)}, f32[8,512,256,2]{2,1,3,0:T(8,128)S(1)}) fusion(pred[256,512]{0,1:T(8,128)(4,1)S(1)} %get-tuple-element.199, bf16[8,256,2,128]{3,1,2,0:T(8,128)(2,1)S(1)} %get-tuple-element.202, bf16[8,1536,128]{2,1,0:T(8,128)(2,1)} %get-tuple-element.200, s32[]{:T(128)} %get-tuple-element.201), kind=kOutput, calls=%fused_computation.2 | convolution fusion | flops 543158272 | bytes 10633728 | tf_op jit(solution)/shard_map/while/body/eval_jaxpr/cond/branch_1_fun/ktgd,kud->kgtu/dot_general | solution.py:109
  92.5 2.0 %fusion.2 = f32[8,2,256]{2,1,0:T(2,128)S(1)} fusion(f32[8,512,256,2]{2,1,3,0:T(8,128)S(1)} %get-tuple-element.249, f32[8,2,256]{2,1,0:T(2,128)S(1)} %max.4, pred[256,512]{0,1:T(8,128)(4,1)S(1)} %get-tuple-element.199), kind=kLoop, calls=%fused_computation.4 | loop fusion | flops 10481664 | bytes 8552448 | tf_op jit(solution)/shard_map/while/body/eval_jaxpr/cond/branch_1_fun/reduce_sum | solution.py:118
  94.5 4.4 %multiply_add_fusion = f32[8,2,256,128]{3,2,1,0:T(8,128)S(1)} fusion(f32[8,2,256,128]{3,2,1,0:T(8,128)S(1)} %get-tuple-element.204, f32[8,512,256,2]{2,1,3,0:T(8,128)S(1)} %get-tuple-element.249, f32[8,2,256]{2,1,0:T(2,128)S(1)} %max.4, pred[256,512]{0,1:T(8,128)(4,1)S(1)} %get-tuple-element.199, bf16[8,1536,128]{2,1,0:T(8,128)(2,1)} %get-tuple-element.205, ...), kind=kOutput, calls=%fused_computation.7 | convolution fusion | flops 548405248 | bytes 13795840 | tf_op jit(solution)/shard_map/while/body/eval_jaxpr/cond/branch_1_fun/kgtu,kud->kgtd/dot_general | solution.py:119
  98.9 0.6 multiply_reduce_fusion
  99.5 14.5 %psum.35 = f32[]{:T(128)} all-reduce(f32[]{:T(128)} %multiply_reduce_fusion), channel_id=1, replica_groups=mesh['dp_0'=8,'dp_1'=2,'seq_0'=2,'seq_1'=8,'seq_2'=2] {'dp_0'}, use_global_device_ids=true, to_apply=%region_12.13 | all-reduce | flops 1 | bytes 8 | tf_op jit(solution)/shard_map/psum | solution.py:27
  114.0 4.4 %psum.36 = f32[]{:T(128)} all-reduce(f32[]{:T(128)} %psum.35), channel_id=1, replica_groups=mesh['dp_0'=8,'dp_1'=2,'seq_0'=2,'seq_1'=8,'seq_2'=2] {'dp_1'}, use_global_device_ids=true, to_apply=%region_13.14 | all-reduce | flops 1 | bytes 8 | tf_op jit(solution)/shard_map/psum | solution.py:27
  118.4 5.9 %psum.37 = f32[]{:T(128)} all-reduce(f32[]{:T(128)} %psum.36), channel_id=1, replica_groups=mesh['dp_0'=8,'dp_1'=2,'seq_0'=2,'seq_1'=8,'seq_2'=2] {'seq_0'}, use_global_device_ids=true, to_apply=%region_14.15 | all-reduce | flops 1 | bytes 8 | tf_op jit(solution)/shard_map/psum | solution.py:27
  124.3 21.9 %psum.38 = f32[]{:T(128)} all-reduce(f32[]{:T(128)} %psum.37), channel_id=1, replica_groups=mesh['dp_0'=8,'dp_1'=2,'seq_0'=2,'seq_1'=8,'seq_2'=2] {'seq_1'}, use_global_device_ids=true, to_apply=%region_15.16 | all-reduce | flops 1 | bytes 8 | tf_op jit(solution)/shard_map/psum | solution.py:27
  146.2 12.5 %psum.39 = f32[]{:T(128)} all-reduce(f32[]{:T(128)} %psum.38), channel_id=1, replica_groups=mesh['dp_0'=8,'dp_1'=2,'seq_0'=2,'seq_1'=8,'seq_2'=2] {'seq_2'}, use_global_device_ids=true, to_apply=%region_16.17 | all-reduce | flops 1 | bytes 8 | tf_op jit(solution)/shard_map/psum | solution.py:27
  158.7 0.7 fusion.20
  159.4 2.0 %copy.17 = bf16[256,8,2,128]{3,2,1,0:T(2,128)(2,1)} copy(bf16[256,8,2,128]{3,0,2,1:T(8,128)(2,1)S(1)} %fusion.20) | data formatting | bytes 2097152 | tf_op jit(solution)/shard_map/convert_element_type | solution.py:143
  (24 shorter events, 0.4 us)
Async XLA Ops:
  4.0 6.2 %copy-start = (bf16[1,256,8,128]{3,2,1,0:T(8,128)(2,1)S(1)}, bf16[1,256,8,128]{3,2,1,0:T(8,128)(2,1)}, u32[]{:S(2)}) copy-start(bf16[1,256,8,128]{3,2,1,0:T(8,128)(2,1)} %param.10) | copy-start | bytes 1572868
  4.4 21.9 %copy-start.1 = (bf16[1,256,16,128]{3,2,1,0:T(8,128)(2,1)S(1)}, bf16[1,256,16,128]{3,2,1,0:T(8,128)(2,1)}, u32[]{:S(2)}) copy-start(bf16[1,256,16,128]{3,2,1,0:T(8,128)(2,1)} %param.8) | copy-start | bytes 3145732
  5.6 10.7 %collective-permute-start = (bf16[8,256,128]{2,1,0:T(8,128)(2,1)S(1)}, bf16[8,256,128]{2,1,0:T(8,128)(2,1)S(1)}, u32[]{:S(2)}, u32[]{:S(2)}) collective-permute-start(bf16[8,256,128]{2,1,0:T(8,128)(2,1)S(1)} %get-tuple-element.247), channel_id=1, source_target_pairs={{0,1},{1,2},{2,3},{3,4},{4,5},{5,6},{6,7},{7,8},{8,9},{9,10},{10,1... | collective-permute-start | bytes 1572872 | tf_op jit(solution)/shard_map/ppermute | solution.py:23
  10.3 12.8 %collective-permute-start.4 = (bf16[8,256,128]{2,1,0:T(8,128)(2,1)S(1)}, bf16[8,256,128]{2,1,0:T(8,128)(2,1)S(1)}, u32[]{:S(2)}, u32[]{:S(2)}) collective-permute-start(bf16[8,256,128]{2,1,0:T(8,128)(2,1)S(1)} %bitcast.71), channel_id=1, source_target_pairs={{0,1},{1,2},{2,3},{3,4},{4,5},{5,6},{6,7},{7,8},{8,9},{9,10},{10,1... | collective-permute-start | bytes 1572872 | tf_op jit(solution)/shard_map/ppermute | solution.py:23
  16.3 11.4 %collective-permute-start.1 = (bf16[8,256,128]{2,1,0:T(8,128)(2,1)S(1)}, bf16[8,256,128]{2,1,0:T(8,128)(2,1)S(1)}, u32[]{:S(2)}, u32[]{:S(2)}) collective-permute-start(bf16[8,256,128]{2,1,0:T(8,128)(2,1)S(1)} %collective-permute-done), channel_id=1, source_target_pairs={{0,1},{1,2},{2,3},{3,4},{4,5},{5,6},{6,7},{7,8},{8,9},{9,10},{10,1... | collective-permute-start | bytes 1572872 | tf_op jit(solution)/shard_map/ppermute | solution.py:23
  23.0 10.4 %collective-permute-start.5 = (bf16[8,256,128]{2,1,0:T(8,128)(2,1)S(1)}, bf16[8,256,128]{2,1,0:T(8,128)(2,1)}, u32[]{:S(2)}, u32[]{:S(2)}) collective-permute-start(bf16[8,256,128]{2,1,0:T(8,128)(2,1)S(1)} %collective-permute-done.4), channel_id=1, source_target_pairs={{0,1},{1,2},{2,3},{3,4},{4,5},{5,6},{6,7},{7,8},{8,9},{9,10},{10,1... | collective-permute-start | bytes 1572872 | tf_op jit(solution)/shard_map/ppermute | solution.py:23
  27.7 14.2 %collective-permute-start.2 = (bf16[8,256,128]{2,1,0:T(8,128)(2,1)S(1)}, bf16[8,256,128]{2,1,0:T(8,128)(2,1)}, u32[]{:S(2)}, u32[]{:S(2)}) collective-permute-start(bf16[8,256,128]{2,1,0:T(8,128)(2,1)S(1)} %collective-permute-done.1), channel_id=1, source_target_pairs={{0,1},{1,2},{2,3},{3,4},{4,5},{5,6},{6,7},{7,8},{8,9},{9,10},{10,1... | collective-permute-start | bytes 1572872 | tf_op jit(solution)/shard_map/ppermute | solution.py:23
  33.4 14.4 %collective-permute-start.6 = (bf16[8,256,128]{2,1,0:T(8,128)(2,1)}, bf16[8,256,128]{2,1,0:T(8,128)(2,1)}, u32[]{:S(2)}, u32[]{:S(2)}) collective-permute-start(bf16[8,256,128]{2,1,0:T(8,128)(2,1)} %collective-permute-done.5), channel_id=1, source_target_pairs={{0,1},{1,2},{2,3},{3,4},{4,5},{5,6},{6,7},{7,8},{8,9},{9,10},{10,1... | collective-permute-start | bytes 1572872 | tf_op jit(solution)/shard_map/ppermute | solution.py:23
  41.9 14.3 %collective-permute-start.3 = (bf16[8,256,128]{2,1,0:T(8,128)(2,1)}, bf16[8,256,128]{2,1,0:T(8,128)(2,1)S(1)}, u32[]{:S(2)}, u32[]{:S(2)}) collective-permute-start(bf16[8,256,128]{2,1,0:T(8,128)(2,1)} %collective-permute-done.2), channel_id=1, source_target_pairs={{0,1},{1,2},{2,3},{3,4},{4,5},{5,6},{6,7},{7,8},{8,9},{9,10},{10,1... | collective-permute-start | bytes 1572872 | tf_op jit(solution)/shard_map/ppermute | solution.py:23
  47.9 14.3 %collective-permute-start.7 = (bf16[8,256,128]{2,1,0:T(8,128)(2,1)}, bf16[8,256,128]{2,1,0:T(8,128)(2,1)S(1)}, u32[]{:S(2)}, u32[]{:S(2)}) collective-permute-start(bf16[8,256,128]{2,1,0:T(8,128)(2,1)} %collective-permute-done.6), channel_id=1, source_target_pairs={{0,1},{1,2},{2,3},{3,4},{4,5},{5,6},{6,7},{7,8},{8,9},{9,10},{10,1... | collective-permute-start | bytes 1572872 | tf_op jit(solution)/shard_map/ppermute | solution.py:23
where the time goes:
time: 164 us; the launch traced here: 163 us
  blocking collectives  59.1 us (36%)
  starting transfers between devices  26.3 us (16%)
  other arithmetic  21.6 us (13%)
  matrix products  20.9 us (13%)
  local copies, waits for them, and re-layouts  15.6 us (10%)
  waiting for transfers between devices  14.8 us (9%)
  between operations  2.67 us (2%)
  loops' own time  2.19 us (1%)
    psum x5, blocking collectives, over_axes(): return functools.reduce(lax.psum, axes, shard)  59.1 us
    ppermute x8, starting transfers between devices, shifted(): return lax.ppermute(block, axis, route)  26.3 us
    ppermute x8, waiting for transfers between devices, shifted(): return lax.ppermute(block, axis, route)  14.8 us
    dot_general x3, matrix products, update(): jnp.einsum('kgtu,kud->kgtd', weights.astype(jnp.bfloat16), values_step, p...  13.1 us
    dot_general x3, matrix products, update(): jnp.einsum('ktgd,kud->kgtu', grouped, keys_step, preferred_element_type=j...  7.83 us
    unnamed x12, local copies, waits for them, and re-layouts  6.16 us
    reduce_sum x3, other arithmetic, update(): new_total = old_total * rescale + jnp.sum(weights, axis=-1)  6.06 us
    reduce_or x3, other arithmetic, visit(): return lax.cond(jnp.any(visible_step), update, unchanged, carry)  5.23 us
  transfers between devices with their start and end apart: 8, of which 7 were waited for; matrix products, arithmetic and copies ran while one was open for 9% of the time, Pallas kernels for 0%

commit v1 on v0

v1 whole, which is shorter than its diff:
```python
import functools
import math

import jax
import jax.numpy as jnp
from jax import lax
from jax.experimental import pallas as pl
from jax.experimental.pallas import tpu as pltpu
from jax.sharding import Mesh
from jax.sharding import PartitionSpec as P

WINDOW = 1024
SEQ = ("seq_0", "seq_1", "seq_2")
CHIP = ("seq_0", "seq_1")
DP_SEQ = ("dp_0", "dp_1", "seq_0", "seq_1", "seq_2")
DP = ("dp_0", "dp_1")
CORES = 2


rope_base = 500000.0
score_scale = 1.0 / 12.0
masked = -1e30
log2_e = 1.0 / math.log(2.0)
unit = score_scale * log2_e

VMEM = pl.BlockSpec(memory_space=pltpu.VMEM)
SMEM = pl.BlockSpec(memory_space=pltpu.SMEM)
NT = (((1,), (1,)), ((), ()))
TN = (((0,), (0,)), ((), ()))


def up_chip(block):
    count = lax.axis_size(SEQ)
    return lax.ppermute(block, SEQ, [(i, i + CORES) for i in range(count - CORES)])


def swapped(block):
    return lax.ppermute(block, "seq_2", [(0, 1), (1, 0)])


def rotated(block, cos_table, sin_table):
    wide = block.astype(jnp.float32)
    half = wide.shape[-1] // 2
    return (wide * cos_table + pltpu.roll(wide, half, 1) * sin_table).astype(jnp.bfloat16)


def doc_ends(lengths_ref):
    ends = [lengths_ref[0, 0]]
    for i in range(1, lengths_ref.shape[1]):
        ends.append(ends[-1] + lengths_ref[0, i])
    return ends


def doc_start(ends, at, low):
    for end in ends:
        low = jnp.maximum(low, jnp.where(at >= end, end, 0))
    return low


def block_start(spot_ref, rows, group, parity):
    core = spot_ref[1]
    place = core if parity == 0 else 1 - core
    return ((spot_ref[0] - group) * CORES + place) * rows


def single_slots(group, core):
    flip = core if group == 0 else 1 - core
    return [(0, 0, 0, None), (1, 1, 1, None), (0, 1, 2, flip == 1), (1, 0, 2, flip == 0)]


def guarded(condition, body):
    if condition is None:
        body()
    else:
        pl.when(condition)(body)


def table_kernel(lengths_ref, spot_ref, cos_ref, sin_ref):
    rows, width = cos_ref.shape[1:]
    half = width // 2
    pairs = rows // 2
    ends = doc_ends(lengths_ref)
    lane = lax.broadcasted_iota(jnp.int32, (pairs, width), 1)
    upper = lane >= half
    slot = jnp.where(upper, lane - half, lane).astype(jnp.float32)
    frequency = jnp.exp2(slot * (-2.0 * math.log2(rope_base) / width))
    sign = jnp.where(upper, 1.0, -1.0)
    for index in range(cos_ref.shape[0]):
        begin = block_start(spot_ref, rows, index // CORES, index % CORES)
        at = begin + lax.broadcasted_iota(jnp.int32, (pairs, width), 0)
        at = at + jnp.where(upper, pairs, 0)
        places = at - doc_start(ends, at, jnp.zeros_like(at))
        angles = places.astype(jnp.float32) * frequency
        for out_ref, table, factor in (
            (cos_ref, jnp.cos(angles), None),
            (sin_ref, jnp.sin(angles), sign),
        ):
            turned = pltpu.roll(table, half, 1)
            first = jnp.where(upper, turned, table)
            second = jnp.where(upper, table, turned)
            if factor is not None:
                first = first * factor
                second = second * factor
            out_ref[index, pl.ds(0, pairs), :] = first
            out_ref[index, pl.ds(pairs, pairs), :] = second


def bias_of(ends, spot_ref, rows, group, q_side, k_side):
    query_at = block_start(spot_ref, rows, 0, q_side) + lax.broadcasted_iota(
        jnp.int32, (1, rows), 1
    )
    key_at = block_start(spot_ref, rows, group, k_side) + lax.broadcasted_iota(
        jnp.int32, (rows, rows), 0
    )
    low = doc_start(ends, query_at, jnp.maximum(query_at - (WINDOW - 1), 0))
    bias = jnp.where((key_at >= low) & (key_at <= query_at), 0.0, masked)
    return jnp.concatenate([bias, bias], axis=1)


def gather_stats(
    group, lengths_ref, spot_ref, query_ref, key_of, weight_ref, mark_ref, peak_ref, total_ref
):
    heads = query_ref.shape[1]
    rows = weight_ref.shape[2]
    ends = doc_ends(lengths_ref)

    def visit(q_side, sides):
        biases = [bias_of(ends, spot_ref, rows, group, q_side, k_side) for k_side, _ in sides]
        for head in range(heads):
            row = pl.ds(q_side * heads + head, 1)
            old_peak = peak_ref[row, :]
            new_peak = old_peak
            parts = []
            for (k_side, _), bias in zip(sides, biases):
                scores = lax.dot_general(
                    key_of(k_side, head),
                    query_ref[q_side, head],
                    NT,
                    preferred_element_type=jnp.float32,
                )
                scores = scores + bias
                parts.append(scores)
                new_peak = jnp.maximum(new_peak, jnp.max(scores, axis=0, keepdims=True))
            total = total_ref[row, :] * jnp.exp2((old_peak - new_peak) * unit)
            for (_, slot), scores in zip(sides, parts):
                weights = jnp.exp2((scores - new_peak) * unit)
                total = total + jnp.sum(weights, axis=0, keepdims=True)
                weight_ref[slot, head] = weights.astype(jnp.bfloat16)
                mark_ref[slot, pl.ds(head, 1), :] = new_peak
            peak_ref[row, :] = new_peak
            total_ref[row, :] = total

    if group == 1:
        visit(0, [(0, 0), (1, 1)])
        visit(1, [(0, 2), (1, 3)])
        return
    for q_side, k_side, slot, condition in single_slots(group, spot_ref[1]):
        guarded(condition, functools.partial(visit, q_side, [(k_side, slot)]))


def rotate_keys(group, raw, cos_ref, sin_ref, key_ref):
    for side in range(CORES):
        cos_table = cos_ref[group * CORES + side]
        sin_table = sin_ref[group * CORES + side]
        for head in range(key_ref.shape[1]):
            key_ref[side, head] = rotated(raw(side, head), cos_table, sin_table)


def first_kernel(
    lengths_ref, spot_ref, cos_ref, sin_ref, k_own, k_other, q_own, q_other,
    query_ref, weight_ref, mark_ref, peak_ref, total_ref, key_ref,
):
    heads, rows = k_own.shape[:2]
    for side, raw_ref in enumerate((q_own, q_other)):
        cos_table = cos_ref[side]
        sin_table = sin_ref[side]
        for head in range(2 * heads):
            query_ref[side, head // 2, pl.ds((head % 2) * rows, rows), :] = rotated(
                raw_ref[head], cos_table, sin_table
            )
    raw = (k_own, k_other)
    rotate_keys(0, lambda side, head: raw[side][head], cos_ref, sin_ref, key_ref)
    peak_ref[...] = jnp.full_like(peak_ref, masked)
    total_ref[...] = jnp.zeros_like(total_ref)
    gather_stats(
        0, lengths_ref, spot_ref, query_ref, lambda s, h: key_ref[s, h],
        weight_ref, mark_ref, peak_ref, total_ref,
    )


def next_kernel(
    lengths_ref, spot_ref, cos_ref, sin_ref, k_own, k_other, query_ref, old_peak, old_total,
    weight_ref, mark_ref, peak_ref, total_ref, key_ref,
):
    raw = (k_own, k_other)
    rotate_keys(1, lambda side, head: raw[side][head], cos_ref, sin_ref, key_ref)
    peak_ref[...] = old_peak[...]
    total_ref[...] = old_total[...]
    gather_stats(
        1, lengths_ref, spot_ref, query_ref, lambda s, h: key_ref[s, h],
        weight_ref, mark_ref, peak_ref, total_ref,
    )


def last_kernel(
    lengths_ref, spot_ref, cos_ref, sin_ref, k_own, k_other, query_ref, old_peak, old_total,
    weight_ref, mark_ref, level_ref, squares_ref, peak_ref, total_ref, key_ref,
):
    raw = (k_own, k_other)
    rotate_keys(2, lambda side, head: raw[side][head], cos_ref, sin_ref, key_ref)
    peak_ref[...] = old_peak[...]
    total_ref[...] = old_total[...]
    gather_stats(
        2, lengths_ref, spot_ref, query_ref, lambda s, h: key_ref[s, h],
        weight_ref, mark_ref, peak_ref, total_ref,
    )
    natural = peak_ref[...] * score_scale + jnp.log(total_ref[...])
    level_ref[...] = natural * log2_e
    squares = jnp.sum(natural * natural, axis=(0, 1), keepdims=True)
    squares_ref[...] = jnp.broadcast_to(squares, squares_ref.shape)


def weighed(weight_ref, mark_ref, level_ref, value, q_side, head, heads, slot):
    scale = jnp.exp2(
        mark_ref[slot, pl.ds(head, 1), :] * unit - level_ref[pl.ds(q_side * heads + head, 1), :]
    )
    return scale * lax.dot_general(
        value, weight_ref[slot, head], TN, preferred_element_type=jnp.float32
    )


def near_kernel(
    spot_ref, level_ref, weight_0, mark_0, weight_1, mark_1, v0_own, v0_other, v1_ref, sum_ref
):
    heads = v0_own.shape[0]
    v0 = (v0_own, v0_other)
    for q_side in range(CORES):
        for head in range(heads):
            part = functools.partial(weighed, q_side=q_side, head=head, heads=heads)
            far = v1_ref[head], v1_ref[heads + head]
            sum_ref[q_side, head] = (
                part(weight_0, mark_0, level_ref, v0[q_side][head], slot=q_side)
                + part(weight_1, mark_1, level_ref, far[0], slot=2 * q_side)
                + part(weight_1, mark_1, level_ref, far[1], slot=2 * q_side + 1)
            )

    def cross(q_side, k_side, slot):
        for head in range(heads):
            sum_ref[q_side, head] += weighed(
                weight_0, mark_0, level_ref, v0[k_side][head], q_side, head, heads, slot
            )

    for q_side, k_side, slot, condition in single_slots(0, spot_ref[1])[2:]:
        guarded(condition, functools.partial(cross, q_side, k_side, slot))


def far_kernel(spot_ref, level_ref, weight_2, mark_2, v2_ref, near_ref, own_ref, other_ref, sum_ref):
    heads = near_ref.shape[1]
    for q_side in range(CORES):
        for head in range(heads):
            sum_ref[q_side, head] = near_ref[q_side, head] + weighed(
                weight_2, mark_2, level_ref, v2_ref[q_side * heads + head],
                q_side, head, heads, q_side,
            )

    def cross(q_side, k_side, slot):
        for head in range(heads):
            sum_ref[q_side, head] += weighed(
                weight_2, mark_2, level_ref, v2_ref[k_side * heads + head],
                q_side, head, heads, slot,
            )

    for q_side, k_side, slot, condition in single_slots(2, spot_ref[1])[2:]:
        guarded(condition, functools.partial(cross, q_side, k_side, slot))
    rows = own_ref.shape[1]
    for side, out_ref in enumerate((own_ref, other_ref)):
        for head in range(heads):
            for member in range(2):
                block = sum_ref[side, head, :, pl.ds(member * rows, rows)]
                out_ref[head * 2 + member] = jnp.transpose(block, (1, 0)).astype(jnp.bfloat16)


def call(kernel, out_shape, scalars, count, flops, scratch=()):
    def run(*operands):
        return pl.pallas_call(
            kernel,
            out_shape=out_shape,
            in_specs=[SMEM] * scalars + [VMEM] * (count - scalars),
            out_specs=jax.tree.map(lambda _: VMEM, out_shape),
            scratch_shapes=list(scratch),
            cost_estimate=pl.CostEstimate(flops=flops, bytes_accessed=0, transcendentals=0),
        )(*operands)

    return run


def halves(tensor, core):
    by_head = jnp.transpose(tensor, (1, 0, 2))
    part = by_head.shape[0] // CORES
    mine = lax.dynamic_slice_in_dim(by_head, core * part, part, 0)
    give = lax.dynamic_slice_in_dim(by_head, (1 - core) * part, part, 0)
    return mine, give


def after(value, *others):
    return lax.optimization_barrier((value, *others))[0]


def device_part(queries, keys, values, doc_lengths):
    rows, query_heads, width = queries.shape[1:]
    key_heads = keys.shape[2]
    heads = key_heads // CORES
    members = query_heads // key_heads
    devices = lax.axis_size(DP_SEQ)
    core = lax.axis_index("seq_2")
    chip = lax.axis_index(CHIP)
    f32, bf16 = jnp.float32, jnp.bfloat16
    shape = jax.ShapeDtypeStruct
    spot = jnp.stack([chip, core]).astype(jnp.int32)

    k_mine, k_give = halves(keys[0], core)
    k1_own = up_chip(k_mine)
    k0_other = swapped(k_give)
    k1_other = up_chip(k0_other)
    k2_own = up_chip(k1_own)
    q_mine, q_give = halves(queries[0], core)
    v_mine, v_give = halves(values[0], core)
    give = jnp.concatenate([q_give, v_give], axis=0)
    got = swapped(give)
    q_other, v0_other = got[: heads * members], got[heads * members :]

    table = shape((3 * CORES, rows, width), f32)
    cos_table, sin_table = call(table_kernel, (table, table), 2, 2, TABLE_FLOPS)(doc_lengths, spot)
    k2_other = up_chip(k1_other)
    v1 = up_chip(jnp.concatenate([v_mine, v0_other], axis=0))

    stats = shape((CORES * heads, members * rows), f32)
    q_shape = shape((CORES, heads, members * rows, width), bf16)
    key_scratch = pltpu.VMEM((CORES, heads, rows, width), bf16)

    def slots(count):
        return (
            shape((count, heads, rows, members * rows), bf16),
            shape((count, heads, members * rows), f32),
        )

    query_rot, weight_0, mark_0, peak, total = call(
        first_kernel, (q_shape, *slots(3), stats, stats), 2, 8, FIRST_FLOPS, (key_scratch,)
    )(doc_lengths, spot, cos_table, sin_table, k_mine, k0_other, q_mine, q_other)
    weight_1, mark_1, peak, total = call(
        next_kernel, (*slots(4), stats, stats), 2, 9, NEXT_FLOPS, (key_scratch,)
    )(doc_lengths, spot, cos_table, sin_table, k1_own, k1_other, query_rot, peak, total)
    weight_2, mark_2, level, squares = call(
        last_kernel,
        (*slots(3), stats, shape((16, width), f32)),
        2,
        9,
        NEXT_FLOPS,
        (pltpu.VMEM(stats.shape, f32), pltpu.VMEM(stats.shape, f32), key_scratch),
    )(doc_lengths, spot, cos_table, sin_table, k2_own, k2_other, query_rot, peak, total)
    squares = sum_over(("seq_1", "seq_2"), squares)
    v2 = up_chip(after(v1, squares))
    squares = sum_over(("dp_0", "dp_1", "seq_0"), squares)
    z_loss = squares[0, 0] / (devices * rows * query_heads)

    sum_shape = shape((CORES, heads, width, members * rows), f32)
    near = call(near_kernel, sum_shape, 1, 9, NEAR_FLOPS)(
        spot, level, weight_0, mark_0, weight_1, mark_1, v_mine, v0_other, v1
    )
    out_shape = shape((heads * members, rows, width), bf16)
    own, other = call(
        far_kernel, (out_shape, out_shape), 1, 6, NEAR_FLOPS,
        (pltpu.VMEM(sum_shape.shape, f32),),
    )(spot, level, weight_2, mark_2, v2, near)
    partner = swapped(other)
    low = jnp.where(core == 0, own, partner)
    high = jnp.where(core == 0, partner, own)
    attended = jnp.transpose(jnp.concatenate([low, high], axis=0), (1, 0, 2))
    return (attended[None], z_loss)


def sum_over(axes, part):
    count = lax.axis_size(axes)
    spread = jnp.broadcast_to(part[:1], (count, part.shape[1]))
    return jnp.sum(lax.all_to_all(spread, axes, 0, 0), axis=0, keepdims=True)


TABLE_FLOPS = 4_000_000
FIRST_FLOPS = 6_000_000
NEXT_FLOPS = 6_000_000
NEAR_FLOPS = 3_000_000


def solution(mesh):
    torus = Mesh(mesh.devices.reshape(8, 2, 2, 8, 2), ("dp_0", "dp_1", "seq_0", "seq_1", "seq_2"))
    in_specs = (P(DP, SEQ, None, None), P(DP, SEQ, None, None), P(DP, SEQ, None, None), P(DP, None))
    out_specs = (P(DP, SEQ, None, None), P())
    return jax.shard_map(
        device_part, mesh=torus, in_specs=in_specs, out_specs=out_specs, check_vma=False
    )
```

time: 164 us -> 123 us (0.75)
  the two profiles are of different devices: /device:TPU:7 before, /device:TPU:1 now
where the time goes in v1:
time: 123 us
  starting transfers between devices  44.3 us (36%)
  Pallas kernels  35.6 us (29%)
  blocking collectives  15.4 us (13%)
  waiting for transfers between devices  15.1 us (12%)
  local copies, waits for them, and re-layouts  8.1 us (7%)
  between operations  2.07 us (2%)
  other arithmetic  1.94 us (2%)
    pallas_call x6, Pallas kernels, run(): pl.pallas_call(kernel, out_shape=out_shape, in_specs=[SMEM] * scalars + [...  35.6 us
    ppermute x6, starting transfers between devices, up_chip(): lax.ppermute(block, SEQ, [(i, i + CORES) for i in range(count - CORES)])  21.5 us
    all_to_all x1, blocking collectives, sum_over(): return jnp.sum(lax.all_to_all(spread, axes, 0, 0), axis=0, keepdims=True)  15.4 us
    ppermute x3, starting transfers between devices, swapped(): return lax.ppermute(block, 'seq_2', [(0, 1), (1, 0)])  14.7 us
    all_to_all x1, waiting for transfers between devices, sum_over(): return jnp.sum(lax.all_to_all(spread, axes, 0, 0), axis=0, keepdims=True)  8.57 us
    all_to_all x1, starting transfers between devices, sum_over(): return jnp.sum(lax.all_to_all(spread, axes, 0, 0), axis=0, keepdims=True)  8.14 us
    ppermute x6, waiting for transfers between devices, up_chip(): lax.ppermute(block, SEQ, [(i, i + CORES) for i in range(count - CORES)])  4.68 us
    another operation x8, local copies, waits for them, and re-layouts  3.42 us
  transfers between devices with their start and end apart: 10, of which 5 were waited for; matrix products, arithmetic and copies ran while one was open for 3% of the time, Pallas kernels for 25%

profile of v1, /device:TPU:1, one launch (start us, length us, event | category | flops | bytes accessed | tf_op | source)
XLA Modules:
  0.0 122.6 jit_solution(4823638738322858168)
XLA Ops:
  0.6 0.0 copy-start.3
  0.6 2.3 %constant_dynamic-slice_fusion = (bf16[1,256,4,128]{3,2,1,0:T(4,128)(2,1)S(1)}, bf16[1,256,4,128]{3,2,1,0:T(4,128)(2,1)S(1)}, bf16[1,256,4,128]{3,2,1,0:T(4,128)(2,1)S(1)}, bf16[1,256,4,128]{3,2,1,0:T(4,128)(2,1)S(1)}) fusion(bf16[1,256,8,128]{3,2,1,0:T(8,128)(2,1)} %param.6, s32[]{:T(128)S(6)} %select_n.27, s32[]{:T(128)S(6)} %select_n.28, ...), kind=kLoop, calls=%fused_computation.11 | loop fusion | bytes 2097160 | tf_op jit(solution)/shard_map/dynamic-slice.7
  3.0 0.0 copy-done.3
  3.0 0.1 constant_dynamic-slice_fusion.2
  3.0 0.1 copy.35
  3.1 0.1 pad_maximum_fusion
  3.2 8.7 %collective-permute-start.5 = (bf16[12,256,128]{2,1,0:T(8,128)(2,1)S(1)}, bf16[12,256,128]{2,1,0:T(8,128)(2,1)S(1)}, u32[]{:S(2)}, u32[]{:S(2)}) collective-permute-start(bf16[12,256,128]{2,1,0:T(8,128)(2,1)S(1)} %pad_maximum_fusion), channel_id=1, source_target_pairs={{0,1},{1,0},{2,3},{3,2},{4,5},{5,4},{6,7},{7,6},{8,9},{9,8},{10,11... | collective-permute-start | bytes 2359304 | tf_op jit(solution)/shard_map/ppermute | solution.py:38
  12.0 0.0 copy-start
  12.0 1.8 %collective-permute-done.5 = bf16[12,256,128]{2,1,0:T(8,128)(2,1)S(1)} collective-permute-done((bf16[12,256,128]{2,1,0:T(8,128)(2,1)S(1)}, bf16[12,256,128]{2,1,0:T(8,128)(2,1)S(1)}, u32[]{:S(2)}, u32[]{:S(2)}) %collective-permute-start.5) | collective-permute-done | bytes 786464 | tf_op jit(solution)/shard_map/ppermute | solution.py:38
  13.9 0.0 copy-start.1
  13.9 1.3 %collective-permute-start.6 = (bf16[8,256,128]{2,1,0:T(8,128)(2,1)S(1)}, bf16[8,256,128]{2,1,0:T(8,128)(2,1)S(1)}, u32[]{:S(2)}, u32[]{:S(2)}) collective-permute-start(bf16[8,256,128]{2,1,0:T(8,128)(2,1)S(1)} %pad_maximum_fusion.1), channel_id=1, source_target_pairs={{0,2},{1,3},{2,4},{3,5},{4,6},{5,7},{6,8},{7,9},{8,10},{9,11},{10,... | collective-permute-start | bytes 1572872 | tf_op jit(solution)/shard_map/ppermute | solution.py:34
  15.3 2.3 %collective-permute-start.2 = (bf16[4,256,128]{2,1,0:T(8,128)(2,1)S(1)}, bf16[4,256,128]{2,1,0:T(8,128)(2,1)S(1)}, u32[]{:S(2)}, u32[]{:S(2)}) collective-permute-start(bf16[4,256,128]{2,1,0:T(8,128)(2,1)S(1)} %bitcast.50), channel_id=1, source_target_pairs={{0,1},{1,0},{2,3},{3,2},{4,5},{5,4},{6,7},{7,6},{8,9},{9,8},{10,11... | collective-permute-start | bytes 786440 | tf_op jit(solution)/shard_map/ppermute | solution.py:38
  17.6 0.0 copy-start.2
  17.7 1.6 %collective-permute-start = (bf16[4,256,128]{2,1,0:T(8,128)(2,1)S(1)}, bf16[4,256,128]{2,1,0:T(8,128)(2,1)S(1)}, u32[]{:S(2)}, u32[]{:S(2)}) collective-permute-start(bf16[4,256,128]{2,1,0:T(8,128)(2,1)S(1)} %bitcast.47), channel_id=1, source_target_pairs={{0,2},{1,3},{2,4},{3,5},{4,6},{5,7},{6,8},{7,9},{8,10},{9,11},{10,... | collective-permute-start | bytes 786440 | tf_op jit(solution)/shard_map/ppermute | solution.py:34
  19.3 0.0 collective-permute-done.2.k_other
  19.3 0.0 copy-start.7
  19.3 4.7 %collective-permute-start.3 = (bf16[4,256,128]{2,1,0:T(8,128)(2,1)S(1)}, bf16[4,256,128]{2,1,0:T(8,128)(2,1)}, u32[]{:S(2)}, u32[]{:S(2)}) collective-permute-start(bf16[4,256,128]{2,1,0:T(8,128)(2,1)S(1)} %collective-permute-done.2.k_other), channel_id=1, source_target_pairs={{0,2},{1,3},{2,4},{3,5},{4,6},{5,7},{6,8},{7,9},{8,10},{9,11},{10,... | collective-permute-start | bytes 786440 | tf_op jit(solution)/shard_map/ppermute | solution.py:34
  24.0 2.4 %collective-permute-done.6.v1_ref = bf16[8,256,128]{2,1,0:T(8,128)(2,1)S(1)} collective-permute-done((bf16[8,256,128]{2,1,0:T(8,128)(2,1)S(1)}, bf16[8,256,128]{2,1,0:T(8,128)(2,1)S(1)}, u32[]{:S(2)}, u32[]{:S(2)}) %collective-permute-start.6) | collective-permute-done | bytes 524320 | tf_op jit(solution)/shard_map/ppermute | solution.py:34
  26.4 0.0 copy-start.4
  26.4 4.1 %collective-permute-start.7 = (bf16[8,256,128]{2,1,0:T(8,128)(2,1)S(1)}, bf16[8,256,128]{2,1,0:T(8,128)(2,1)S(1)}, u32[]{:S(2)}, u32[]{:S(2)}) collective-permute-start(bf16[8,256,128]{2,1,0:T(8,128)(2,1)S(1)} %collective-permute-done.6.v1_ref), channel_id=1, source_target_pairs={{0,2},{1,3},{2,4},{3,5},{4,6},{5,7},{6,8},{7,9},{8,10},{9,11},{10,... | collective-permute-start | bytes 1572872 | tf_op jit(solution)/shard_map/ppermute | solution.py:34
  30.5 1.5 %collective-permute-done.k_own = bf16[4,256,128]{2,1,0:T(8,128)(2,1)S(1)} collective-permute-done((bf16[4,256,128]{2,1,0:T(8,128)(2,1)S(1)}, bf16[4,256,128]{2,1,0:T(8,128)(2,1)S(1)}, u32[]{:S(2)}, u32[]{:S(2)}) %collective-permute-start) | collective-permute-done | bytes 262176 | tf_op jit(solution)/shard_map/ppermute | solution.py:34
  32.0 0.0 copy-done.7
  32.0 0.0 copy-start.6
  32.0 4.8 %collective-permute-start.1 = (bf16[4,256,128]{2,1,0:T(8,128)(2,1)S(1)}, bf16[4,256,128]{2,1,0:T(8,128)(2,1)}, u32[]{:S(2)}, u32[]{:S(2)}) collective-permute-start(bf16[4,256,128]{2,1,0:T(8,128)(2,1)S(1)} %collective-permute-done.k_own), channel_id=1, source_target_pairs={{0,2},{1,3},{2,4},{3,5},{4,6},{5,7},{6,8},{7,9},{8,10},{9,11},{10,... | collective-permute-start | bytes 786440 | tf_op jit(solution)/shard_map/ppermute | solution.py:34
  36.9 0.8 collective-permute-done.3.k_other
  37.6 4.9 %collective-permute-start.4 = (bf16[4,256,128]{2,1,0:T(8,128)(2,1)}, bf16[4,256,128]{2,1,0:T(8,128)(2,1)}, u32[]{:S(2)}, u32[]{:S(2)}) collective-permute-start(bf16[4,256,128]{2,1,0:T(8,128)(2,1)} %collective-permute-done.3.k_other), channel_id=1, source_target_pairs={{0,2},{1,3},{2,4},{3,5},{4,6},{5,7},{6,8},{7,9},{8,10},{9,11},{10,... | collective-permute-start | bytes 786440 | tf_op jit(solution)/shard_map/ppermute | solution.py:34
  42.6 0.9 copy.36
  43.4 0.6 pad_add_fusion.spot_ref
  44.0 3.8 %shard_map.59 = (f32[6,256,128]{2,1,0:T(8,128)}, f32[6,256,128]{2,1,0:T(8,128)}) custom-call(s32[1,8]{1,0:T(1,128)} %lengths_ref.7, s32[2]{0:T(128)} %pad_add_fusion.spot_ref), custom_call_target="tpu_custom_call" | custom-call | flops 4000000 | tf_op jit(solution)/shard_map/pallas_call | solution.py:285
  47.9 0.9 slice.19.q_other
  48.8 0.0 copy-done.2
  48.8 7.3 %shard_map.60 = (bf16[2,4,512,128]{3,2,1,0:T(8,128)(2,1)}, bf16[3,4,256,512]{3,2,1,0:T(8,128)(2,1)}, f32[3,4,512]{2,1,0:T(4,128)}, f32[8,512]{1,0:T(8,128)}, f32[8,512]{1,0:T(8,128)}) custom-call(s32[1,8]{1,0:T(1,128)} %lengths_ref.7, s32[2]{0:T(128)} %pad_add_fusion.spot_ref, f32[6,256,128]{2,1,0:T(8,128)} %get-tuple-element.19.cos_ref, ...), custom_call_target="tpu_custom_call" | custom-call | flops 6000000 | tf_op jit(solution)/shard_map/pallas_call | solution.py:285
  56.0 0.0 copy-done
  56.0 0.0 copy-done.1
  56.0 0.0 copy-done.6
  56.1 7.3 %shard_map.61 = (bf16[4,4,256,512]{3,2,1,0:T(8,128)(2,1)}, f32[4,4,512]{2,1,0:T(4,128)}, f32[8,512]{1,0:T(8,128)}, f32[8,512]{1,0:T(8,128)}) custom-call(s32[1,8]{1,0:T(1,128)} %lengths_ref.7, s32[2]{0:T(128)} %pad_add_fusion.spot_ref, f32[6,256,128]{2,1,0:T(8,128)} %get-tuple-element.19.cos_ref, f32[6,256,128]{2,1,0:T(8,128)} %get-tuple-element.20.sin_ref, ...), custom_call_target="tpu_custom_call" | custom-call | flops 6000000 | tf_op jit(solution)/shard_map/pallas_call | solution.py:285
  63.3 0.0 copy-done.4
  63.3 0.0 collective-permute-done.1.k_own
  63.3 0.0 collective-permute-done.4.k_other
  63.4 6.4 %shard_map.62 = (bf16[3,4,256,512]{3,2,1,0:T(8,128)(2,1)}, f32[3,4,512]{2,1,0:T(4,128)}, f32[8,512]{1,0:T(8,128)}, f32[16,128]{1,0:T(8,128)}) custom-call(s32[1,8]{1,0:T(1,128)} %lengths_ref.7, s32[2]{0:T(128)} %pad_add_fusion.spot_ref, f32[6,256,128]{2,1,0:T(8,128)} %get-tuple-element.19.cos_ref, f32[6,256,128]{2,1,0:T(8,128)} %get-tuple-element.20.sin_ref, ...), custom_call_target="tpu_custom_call" | custom-call | flops 6000000 | tf_op jit(solution)/shard_map/pallas_call | solution.py:285
  69.7 6.1 %shard_map.63.near_ref = f32[2,4,128,512]{3,2,1,0:T(8,128)} custom-call(s32[2]{0:T(128)} %pad_add_fusion.spot_ref, f32[8,512]{1,0:T(8,128)} %get-tuple-element.26.level_ref, bf16[3,4,256,512]{3,2,1,0:T(8,128)(2,1)} %get-tuple-element.29.weight_0, f32[3,4,512]{2,1,0:T(4,128)} %get-tuple-element.30.mark_0, ...), custom_call_target="tpu_custom_call" | custom-call | flops 3000000 | tf_op jit(solution)/shard_map/pallas_call | solution.py:285
  75.8 0.0 collective-permute-done.7.v2_ref
  75.8 0.0 copy-start.5
  75.8 0.8 copy-done.5
  76.6 4.7 %shard_map.64 = (bf16[8,256,128]{2,1,0:T(8,128)(2,1)}, bf16[8,256,128]{2,1,0:T(8,128)(2,1)}) custom-call(s32[2]{0:T(128)} %pad_add_fusion.spot_ref, f32[8,512]{1,0:T(8,128)} %get-tuple-element.26.level_ref, bf16[3,4,256,512]{3,2,1,0:T(8,128)(2,1)} %get-tuple-element.27.weight_2, f32[3,4,512]{2,1,0:T(4,128)} %get-tuple-element.28.mark_2, ...), custom_call_target="tpu_custom_call" | custom-call | flops 3000000 | tf_op jit(solution)/shard_map/pallas_call | solution.py:285
  81.3 3.6 %collective-permute-start.8 = (bf16[8,256,128]{2,1,0:T(8,128)(2,1)}, bf16[8,256,128]{2,1,0:T(8,128)(2,1)S(1)}, u32[]{:S(2)}, u32[]{:S(2)}) collective-permute-start(bf16[8,256,128]{2,1,0:T(8,128)(2,1)} %get-tuple-element.34), channel_id=1, source_target_pairs={{0,1},{1,0},{2,3},{3,2},{4,5},{5,4},{6,7},{7,6},{8,9},{9,8},{10,11... | collective-permute-start | bytes 1572872 | tf_op jit(solution)/shard_map/ppermute | solution.py:38
  85.0 0.7 slice_bitcast_fusion
  85.7 15.4 %all_to_all.12 = f32[16,1,128]{2,1,0:T(1,128)S(1)} all-to-all(f32[16,1,128]{2,1,0:T(1,128)S(1)} %broadcast_in_dim.18), channel_id=1, replica_groups=mesh['dp_0'=8,'dp_1'=2,'seq_0'=2,'seq_1'=8,'seq_2'=2] {'seq_1','seq_2'}, dimensions={0} | all-to-all | bytes 16384 | tf_op jit(solution)/shard_map/all_to_all | solution.py:385
  101.2 0.6 broadcast_in_dim.19
  101.8 8.1 %all-to-all-start.1 = ((f32[32,1,128]{2,1,0:T(1,128)}), f32[32,1,128]{2,1,0:T(1,128)S(1)}, u32[]{:S(2)}, u32[]{:S(2)}) async-start(f32[32,1,128]{2,1,0:T(1,128)} %broadcast_in_dim.19), calls=%async_computation.1 | async-start | bytes 32768 | tf_op jit(solution)/shard_map/all_to_all | solution.py:385
  109.9 8.6 %all-to-all-done.1 = f32[32,1,128]{2,1,0:T(1,128)S(1)} async-done(((f32[32,1,128]{2,1,0:T(1,128)}), f32[32,1,128]{2,1,0:T(1,128)S(1)}, u32[]{:S(2)}, u32[]{:S(2)}) %all-to-all-start.1) | async-done | bytes 16416 | tf_op jit(solution)/shard_map/all_to_all | solution.py:385
  118.6 0.0 collective-permute-done.8
  118.6 1.1 broadcast_select_fusion.1
  119.7 0.1 maximum_bitcast_fusion
  119.8 1.6 %copy.28 = bf16[1,256,16,128]{3,2,1,0:T(8,128)(2,1)} copy(bf16[1,256,16,128]{3,1,2,0:T(8,128)(2,1)S(1)} %maximum_bitcast_fusion) | data formatting | bytes 2097152
  (9 shorter events, 0.3 us)
Async XLA Ops:
  0.6 2.3 %copy-start.3 = (bf16[1,256,16,128]{3,2,1,0:T(8,128)(2,1)S(1)}, bf16[1,256,16,128]{3,2,1,0:T(8,128)(2,1)}, u32[]{:S(2)}) copy-start(bf16[1,256,16,128]{3,2,1,0:T(8,128)(2,1)} %param.4) | copy-start | bytes 3145732
  3.2 10.6 %collective-permute-start.5 = (bf16[12,256,128]{2,1,0:T(8,128)(2,1)S(1)}, bf16[12,256,128]{2,1,0:T(8,128)(2,1)S(1)}, u32[]{:S(2)}, u32[]{:S(2)}) collective-permute-start(bf16[12,256,128]{2,1,0:T(8,128)(2,1)S(1)} %pad_maximum_fusion), channel_id=1, source_target_pairs={{0,1},{1,0},{2,3},{3,2},{4,5},{5,4},{6,7},{7,6},{8,9},{9,8},{10,11... | collective-permute-start | bytes 2359304 | tf_op jit(solution)/shard_map/ppermute | solution.py:38
  12.0 44.0 %copy-start = (bf16[1,256,4,128]{3,1,2,0:T(8,128)(2,1)}, bf16[1,256,4,128]{3,1,2,0:T(8,128)(2,1)S(1)}, u32[]{:S(2)}) copy-start(bf16[1,256,4,128]{3,1,2,0:T(8,128)(2,1)S(1)} %copy.37) | copy-start | bytes 786436
  13.9 42.2 %copy-start.1 = (bf16[4,256,128]{2,1,0:T(8,128)(2,1)}, bf16[4,256,128]{2,1,0:T(8,128)(2,1)S(1)}, u32[]{:S(2)}) copy-start(bf16[4,256,128]{2,1,0:T(8,128)(2,1)S(1)} %slice.20.v0_other) | copy-start | bytes 786436
  13.9 12.5 %collective-permute-start.6 = (bf16[8,256,128]{2,1,0:T(8,128)(2,1)S(1)}, bf16[8,256,128]{2,1,0:T(8,128)(2,1)S(1)}, u32[]{:S(2)}, u32[]{:S(2)}) collective-permute-start(bf16[8,256,128]{2,1,0:T(8,128)(2,1)S(1)} %pad_maximum_fusion.1), channel_id=1, source_target_pairs={{0,2},{1,3},{2,4},{3,5},{4,6},{5,7},{6,8},{7,9},{8,10},{9,11},{10,... | collective-permute-start | bytes 1572872 | tf_op jit(solution)/shard_map/ppermute | solution.py:34
  15.3 4.0 %collective-permute-start.2 = (bf16[4,256,128]{2,1,0:T(8,128)(2,1)S(1)}, bf16[4,256,128]{2,1,0:T(8,128)(2,1)S(1)}, u32[]{:S(2)}, u32[]{:S(2)}) collective-permute-start(bf16[4,256,128]{2,1,0:T(8,128)(2,1)S(1)} %bitcast.50), channel_id=1, source_target_pairs={{0,1},{1,0},{2,3},{3,2},{4,5},{5,4},{6,7},{7,6},{8,9},{9,8},{10,11... | collective-permute-start | bytes 786440 | tf_op jit(solution)/shard_map/ppermute | solution.py:38
  17.6 31.1 %copy-start.2 = (bf16[1,256,4,128]{3,1,2,0:T(8,128)(2,1)}, bf16[1,256,4,128]{3,1,2,0:T(8,128)(2,1)S(1)}, u32[]{:S(2)}) copy-start(bf16[1,256,4,128]{3,1,2,0:T(8,128)(2,1)S(1)} %copy.40) | copy-start | bytes 786436
  17.7 14.4 %collective-permute-start = (bf16[4,256,128]{2,1,0:T(8,128)(2,1)S(1)}, bf16[4,256,128]{2,1,0:T(8,128)(2,1)S(1)}, u32[]{:S(2)}, u32[]{:S(2)}) collective-permute-start(bf16[4,256,128]{2,1,0:T(8,128)(2,1)S(1)} %bitcast.47), channel_id=1, source_target_pairs={{0,2},{1,3},{2,4},{3,5},{4,6},{5,7},{6,8},{7,9},{8,10},{9,11},{10,... | collective-permute-start | bytes 786440 | tf_op jit(solution)/shard_map/ppermute | solution.py:34
  19.3 12.7 %copy-start.7 = (bf16[4,256,128]{2,1,0:T(8,128)(2,1)}, bf16[4,256,128]{2,1,0:T(8,128)(2,1)S(1)}, u32[]{:S(2)}) copy-start(bf16[4,256,128]{2,1,0:T(8,128)(2,1)S(1)} %collective-permute-done.2.k_other) | copy-start | bytes 786436
  19.3 18.3 %collective-permute-start.3 = (bf16[4,256,128]{2,1,0:T(8,128)(2,1)S(1)}, bf16[4,256,128]{2,1,0:T(8,128)(2,1)}, u32[]{:S(2)}, u32[]{:S(2)}) collective-permute-start(bf16[4,256,128]{2,1,0:T(8,128)(2,1)S(1)} %collective-permute-done.2.k_other), channel_id=1, source_target_pairs={{0,2},{1,3},{2,4},{3,5},{4,6},{5,7},{6,8},{7,9},{8,10},{9,11},{10,... | collective-permute-start | bytes 786440 | tf_op jit(solution)/shard_map/ppermute | solution.py:34
  26.4 36.9 %copy-start.4 = (bf16[8,256,128]{2,1,0:T(8,128)(2,1)}, bf16[8,256,128]{2,1,0:T(8,128)(2,1)S(1)}, u32[]{:S(2)}) copy-start(bf16[8,256,128]{2,1,0:T(8,128)(2,1)S(1)} %collective-permute-done.6.v1_ref) | copy-start | bytes 1572868
  26.4 49.4 %collective-permute-start.7 = (bf16[8,256,128]{2,1,0:T(8,128)(2,1)S(1)}, bf16[8,256,128]{2,1,0:T(8,128)(2,1)S(1)}, u32[]{:S(2)}, u32[]{:S(2)}) collective-permute-start(bf16[8,256,128]{2,1,0:T(8,128)(2,1)S(1)} %collective-permute-done.6.v1_ref), channel_id=1, source_target_pairs={{0,2},{1,3},{2,4},{3,5},{4,6},{5,7},{6,8},{7,9},{8,10},{9,11},{10,... | collective-permute-start | bytes 1572872 | tf_op jit(solution)/shard_map/ppermute | solution.py:34
  32.0 24.0 %copy-start.6 = (bf16[4,256,128]{2,1,0:T(8,128)(2,1)}, bf16[4,256,128]{2,1,0:T(8,128)(2,1)S(1)}, u32[]{:S(2)}) copy-start(bf16[4,256,128]{2,1,0:T(8,128)(2,1)S(1)} %collective-permute-done.k_own) | copy-start | bytes 786436
  32.0 31.3 %collective-permute-start.1 = (bf16[4,256,128]{2,1,0:T(8,128)(2,1)S(1)}, bf16[4,256,128]{2,1,0:T(8,128)(2,1)}, u32[]{:S(2)}, u32[]{:S(2)}) collective-permute-start(bf16[4,256,128]{2,1,0:T(8,128)(2,1)S(1)} %collective-permute-done.k_own), channel_id=1, source_target_pairs={{0,2},{1,3},{2,4},{3,5},{4,6},{5,7},{6,8},{7,9},{8,10},{9,11},{10,... | collective-permute-start | bytes 786440 | tf_op jit(solution)/shard_map/ppermute | solution.py:34
  37.6 25.7 %collective-permute-start.4 = (bf16[4,256,128]{2,1,0:T(8,128)(2,1)}, bf16[4,256,128]{2,1,0:T(8,128)(2,1)}, u32[]{:S(2)}, u32[]{:S(2)}) collective-permute-start(bf16[4,256,128]{2,1,0:T(8,128)(2,1)} %collective-permute-done.3.k_other), channel_id=1, source_target_pairs={{0,2},{1,3},{2,4},{3,5},{4,6},{5,7},{6,8},{7,9},{8,10},{9,11},{10,... | collective-permute-start | bytes 786440 | tf_op jit(solution)/shard_map/ppermute | solution.py:34
  75.8 0.8 copy-start.5
  81.3 37.2 %collective-permute-start.8 = (bf16[8,256,128]{2,1,0:T(8,128)(2,1)}, bf16[8,256,128]{2,1,0:T(8,128)(2,1)S(1)}, u32[]{:S(2)}, u32[]{:S(2)}) collective-permute-start(bf16[8,256,128]{2,1,0:T(8,128)(2,1)} %get-tuple-element.34), channel_id=1, source_target_pairs={{0,1},{1,0},{2,3},{3,2},{4,5},{5,4},{6,7},{7,6},{8,9},{9,8},{10,11... | collective-permute-start | bytes 1572872 | tf_op jit(solution)/shard_map/ppermute | solution.py:38
  101.8 16.7 %all-to-all-start.1 = ((f32[32,1,128]{2,1,0:T(1,128)}), f32[32,1,128]{2,1,0:T(1,128)S(1)}, u32[]{:S(2)}, u32[]{:S(2)}) async-start(f32[32,1,128]{2,1,0:T(1,128)} %broadcast_in_dim.19), calls=%async_computation.1 | async-start | bytes 32768 | tf_op jit(solution)/shard_map/all_to_all | solution.py:385

commit v2 on v1

v2 whole, which is shorter than its diff:
```python
import functools
import math

import jax
import jax.numpy as jnp
from jax import lax
from jax.experimental import pallas as pl
from jax.experimental.pallas import tpu as pltpu
from jax.sharding import Mesh
from jax.sharding import PartitionSpec as P

WINDOW = 1024
SEQ = ("seq_0", "seq_1", "seq_2")
CHIP = ("seq_0", "seq_1")
DP_SEQ = ("dp_0", "dp_1", "seq_0", "seq_1", "seq_2")
DP = ("dp_0", "dp_1")
CORES = 2


rope_base = 500000.0
score_scale = 1.0 / 12.0
masked = -1e30
log2_e = 1.0 / math.log(2.0)
unit = score_scale * log2_e

VMEM = pl.BlockSpec(memory_space=pltpu.VMEM)
SMEM = pl.BlockSpec(memory_space=pltpu.SMEM)
HBM = pl.BlockSpec(memory_space=pltpu.HBM)
NT = (((1,), (1,)), ((), ()))
TN = (((0,), (0,)), ((), ()))


def up_chip(block, chips=1):
    count = lax.axis_size(SEQ)
    step = chips * CORES
    return lax.ppermute(block, SEQ, [(i, i + step) for i in range(count - step)])


def swapped(block):
    return lax.ppermute(block, "seq_2", [(0, 1), (1, 0)])


def rotated(block, cos_table, sin_table):
    wide = block.astype(jnp.float32)
    half = wide.shape[-1] // 2
    return (wide * cos_table + pltpu.roll(wide, half, 1) * sin_table).astype(jnp.bfloat16)


def doc_ends(lengths_ref):
    ends = [lengths_ref[0, 0]]
    for i in range(1, lengths_ref.shape[1]):
        ends.append(ends[-1] + lengths_ref[0, i])
    return ends


def doc_start(ends, at, low):
    for end in ends:
        low = jnp.maximum(low, jnp.where(at >= end, end, 0))
    return low


def block_start(spot_ref, rows, group, parity):
    core = spot_ref[1]
    place = core if parity == 0 else 1 - core
    return ((spot_ref[0] - group) * CORES + place) * rows


def single_slots(group, core):
    flip = core if group == 0 else 1 - core
    return [(0, 0, 0, None), (1, 1, 1, None), (0, 1, 2, flip == 1), (1, 0, 2, flip == 0)]


def guarded(condition, body):
    if condition is None:
        body()
    else:
        pl.when(condition)(body)


def table_kernel(lengths_ref, spot_ref, cos_ref, sin_ref):
    rows, width = cos_ref.shape[1:]
    half = width // 2
    pairs = rows // 2
    ends = doc_ends(lengths_ref)
    lane = lax.broadcasted_iota(jnp.int32, (pairs, width), 1)
    upper = lane >= half
    slot = jnp.where(upper, lane - half, lane).astype(jnp.float32)
    frequency = jnp.exp2(slot * (-2.0 * math.log2(rope_base) / width))
    sign = jnp.where(upper, 1.0, -1.0)
    for index in range(cos_ref.shape[0]):
        begin = block_start(spot_ref, rows, index // CORES, index % CORES)
        at = begin + lax.broadcasted_iota(jnp.int32, (pairs, width), 0)
        at = at + jnp.where(upper, pairs, 0)
        places = at - doc_start(ends, at, jnp.zeros_like(at))
        angles = places.astype(jnp.float32) * frequency
        for out_ref, table, factor in (
            (cos_ref, jnp.cos(angles), None),
            (sin_ref, jnp.sin(angles), sign),
        ):
            turned = pltpu.roll(table, half, 1)
            first = jnp.where(upper, turned, table)
            second = jnp.where(upper, table, turned)
            if factor is not None:
                first = first * factor
                second = second * factor
            out_ref[index, pl.ds(0, pairs), :] = first
            out_ref[index, pl.ds(pairs, pairs), :] = second


def bias_of(ends, spot_ref, rows, group, q_side, k_side):
    query_at = block_start(spot_ref, rows, 0, q_side) + lax.broadcasted_iota(
        jnp.int32, (1, rows), 1
    )
    key_at = block_start(spot_ref, rows, group, k_side) + lax.broadcasted_iota(
        jnp.int32, (rows, rows), 0
    )
    low = doc_start(ends, query_at, jnp.maximum(query_at - (WINDOW - 1), 0))
    bias = jnp.where((key_at >= low) & (key_at <= query_at), 0.0, masked)
    return jnp.concatenate([bias, bias], axis=1)


def gather_stats(
    group, lengths_ref, spot_ref, query_ref, key_of, weight_ref, mark_ref, peak_ref, total_ref,
    stage_ref, sent,
):
    heads = query_ref.shape[1]
    rows = weight_ref.shape[2]
    ends = doc_ends(lengths_ref)

    def copy_out(slot, head):
        return pltpu.make_async_copy(
            stage_ref.at[slot, head], weight_ref.at[slot, head], sent.at[slot, head]
        )

    def visit(q_side, sides):
        biases = [bias_of(ends, spot_ref, rows, group, q_side, k_side) for k_side, _ in sides]

        def scored(head):
            return [
                lax.dot_general(
                    key_of(k_side, head),
                    query_ref[q_side, head],
                    NT,
                    preferred_element_type=jnp.float32,
                )
                + bias
                for (k_side, _), bias in zip(sides, biases)
            ]

        for head in range(heads):
            parts = scored(head)
            row = pl.ds(q_side * heads + head, 1)
            old_peak = peak_ref[row, :]
            new_peak = old_peak
            for scores in parts:
                new_peak = jnp.maximum(new_peak, jnp.max(scores, axis=0, keepdims=True))
            total = total_ref[row, :] * jnp.exp2((old_peak - new_peak) * unit)
            for (_, slot), scores in zip(sides, parts):
                weights = jnp.exp2((scores - new_peak) * unit)
                total = total + jnp.sum(weights, axis=0, keepdims=True)
                stage_ref[slot, head] = weights.astype(jnp.bfloat16)
                mark_ref[slot, pl.ds(head, 1), :] = new_peak
            peak_ref[row, :] = new_peak
            total_ref[row, :] = total
            for _, slot in sides:
                copy_out(slot, head).start()

    if group == 1:
        visit(0, [(0, 0), (1, 1)])
        visit(1, [(0, 2), (1, 3)])
    else:
        for q_side, k_side, slot, condition in single_slots(group, spot_ref[1]):
            guarded(condition, functools.partial(visit, q_side, [(k_side, slot)]))

    def wait_all():
        for slot in range(weight_ref.shape[0]):
            for head in range(heads):
                copy_out(slot, head).wait()

    return wait_all


def rotate_keys(group, raw, cos_ref, sin_ref, key_ref):
    for side in range(CORES):
        cos_table = cos_ref[group * CORES + side]
        sin_table = sin_ref[group * CORES + side]
        for head in range(key_ref.shape[1]):
            key_ref[side, head] = rotated(raw(side, head), cos_table, sin_table)


def first_kernel(
    lengths_ref, spot_ref, cos_ref, sin_ref, k_all, k_other, q_all, v_all, got_ref,
    query_ref, value_ref, weight_ref, mark_ref, peak_ref, total_ref, key_ref, stage_ref, sent,
):
    heads, rows = k_other.shape[:2]
    core = spot_ref[1]
    for side in range(CORES):
        cos_table = cos_ref[side]
        sin_table = sin_ref[side]
        for head in range(2 * heads):
            raw = q_all[core * 2 * heads + head] if side == 0 else got_ref[head]
            query_ref[side, head // 2, pl.ds((head % 2) * rows, rows), :] = rotated(
                raw, cos_table, sin_table
            )

    def raw_key(side, head):
        return k_all[core * heads + head] if side == 0 else k_other[head]

    for head in range(heads):
        value_ref[head] = v_all[core * heads + head]
        value_ref[heads + head] = got_ref[2 * heads + head]
    rotate_keys(0, raw_key, cos_ref, sin_ref, key_ref)
    peak_ref[...] = jnp.full_like(peak_ref, masked)
    total_ref[...] = jnp.zeros_like(total_ref)
    gather_stats(
        0, lengths_ref, spot_ref, query_ref, lambda s, h: key_ref[s, h],
        weight_ref, mark_ref, peak_ref, total_ref, stage_ref, sent,
    )()


def rest_kernel(
    lengths_ref, spot_ref, cos_ref, sin_ref, k1_own, k1_other, k2_own, k2_other, query_ref,
    old_peak, old_total,
    weight_1, mark_1, weight_2, mark_2, level_ref, squares_ref,
    peak_ref, total_ref, key_1, stage_1, sent_1, key_2, stage_2, sent_2,
):
    peak_ref[...] = old_peak[...]
    total_ref[...] = old_total[...]
    waits = []
    for group, raw, key_ref, weight_ref, mark_ref, stage_ref, sent in (
        (1, (k1_own, k1_other), key_1, weight_1, mark_1, stage_1, sent_1),
        (2, (k2_own, k2_other), key_2, weight_2, mark_2, stage_2, sent_2),
    ):
        rotate_keys(group, lambda side, head: raw[side][head], cos_ref, sin_ref, key_ref)
        waits.append(
            gather_stats(
                group, lengths_ref, spot_ref, query_ref, lambda s, h: key_ref[s, h],
                weight_ref, mark_ref, peak_ref, total_ref, stage_ref, sent,
            )
        )
    natural = peak_ref[...] * score_scale + jnp.log(total_ref[...])
    level_ref[...] = natural * log2_e
    squares = jnp.sum(natural * natural, axis=(0, 1), keepdims=True)
    squares_ref[...] = jnp.broadcast_to(squares, squares_ref.shape)
    for wait_all in waits:
        wait_all()


def fetch(weight_ref, held_ref, ready):
    def copy(slot):
        return pltpu.make_async_copy(weight_ref.at[slot], held_ref.at[slot], ready.at[slot, 0])

    return copy


def weighed(weight_ref, mark_ref, level_ref, value, q_side, head, heads, slot):
    scale = jnp.exp2(
        mark_ref[slot, pl.ds(head, 1), :] * unit - level_ref[pl.ds(q_side * heads + head, 1), :]
    )
    return scale * lax.dot_general(
        value, weight_ref[slot, head], TN, preferred_element_type=jnp.float32
    )


def near_kernel(
    spot_ref, level_ref, weight_0, mark_0, weight_1, mark_1, v0_ref, v1_ref, sum_ref,
    held_0, held_1, ready_0, ready_1,
):
    heads = sum_ref.shape[1]
    copies_0 = fetch(weight_0, held_0, ready_0)
    copies_1 = fetch(weight_1, held_1, ready_1)
    for copy in (
        copies_0(0), copies_1(0), copies_1(1), copies_0(1), copies_1(2), copies_1(3), copies_0(2)
    ):
        copy.start()
    for q_side in range(CORES):
        for copy in (copies_0(q_side), copies_1(2 * q_side), copies_1(2 * q_side + 1)):
            copy.wait()
        for head in range(heads):
            part = functools.partial(weighed, q_side=q_side, head=head, heads=heads)
            sum_ref[q_side, head] = (
                part(held_0, mark_0, level_ref, v0_ref[q_side * heads + head], slot=q_side)
                + part(held_1, mark_1, level_ref, v1_ref[head], slot=2 * q_side)
                + part(held_1, mark_1, level_ref, v1_ref[heads + head], slot=2 * q_side + 1)
            )
    copies_0(2).wait()

    def cross(q_side, k_side, slot):
        for head in range(heads):
            sum_ref[q_side, head] += weighed(
                held_0, mark_0, level_ref, v0_ref[k_side * heads + head], q_side, head, heads, slot
            )

    for q_side, k_side, slot, condition in single_slots(0, spot_ref[1])[2:]:
        guarded(condition, functools.partial(cross, q_side, k_side, slot))


def far_kernel(
    side, spot_ref, level_ref, weight_2, mark_2, v2_ref, near_ref, out_ref,
    sum_ref, held, ready,
):
    heads = near_ref.shape[1]
    copies = fetch(weight_2, held, ready)
    cross_here = [entry for entry in single_slots(2, spot_ref[1])[2:] if entry[0] == side]
    for slot in (2, side):
        copies(slot).start()
    sum_ref[...] = near_ref[side]
    copies(2).wait()

    def cross(k_side, slot):
        for head in range(heads):
            sum_ref[head] += weighed(
                held, mark_2, level_ref, v2_ref[k_side * heads + head], side, head, heads, slot
            )

    for _, k_side, slot, condition in cross_here:
        guarded(condition, functools.partial(cross, k_side, slot))
    rows = out_ref.shape[1]
    copies(side).wait()
    for head in range(heads):
        block = sum_ref[head] + weighed(
            held, mark_2, level_ref, v2_ref[side * heads + head], side, head, heads, side
        )
        turned = jnp.transpose(block, (1, 0)).astype(jnp.bfloat16)
        out_ref[head * 2] = turned[:rows]
        out_ref[head * 2 + 1] = turned[rows:]


def call(kernel, out_shape, scalars, count, flops, scratch=(), far_in=(), far_out=()):
    def run(*operands):
        return pl.pallas_call(
            kernel,
            out_shape=out_shape,
            in_specs=[SMEM] * scalars
            + [HBM if i in far_in else VMEM for i in range(scalars, count)],
            out_specs=tuple(
                HBM if i in far_out else VMEM for i in range(len(out_shape))
            ),
            scratch_shapes=list(scratch),
            cost_estimate=pl.CostEstimate(flops=flops, bytes_accessed=0, transcendentals=0),
            compiler_params=pltpu.CompilerParams(vmem_limit_bytes=VMEM_LIMIT),
        )(*operands)

    return run


def by_head(tensor):
    return lax.optimization_barrier(jnp.transpose(tensor, (1, 0, 2)))


def half_of(tensor, core):
    part = tensor.shape[0] // CORES
    return jnp.where(core == 0, tensor[:part], tensor[part:])


def device_part(queries, keys, values, doc_lengths):
    rows, query_heads, width = queries.shape[1:]
    key_heads = keys.shape[2]
    heads = key_heads // CORES
    members = query_heads // key_heads
    devices = lax.axis_size(DP_SEQ)
    core = lax.axis_index("seq_2")
    chip = lax.axis_index(CHIP)
    f32, bf16 = jnp.float32, jnp.bfloat16
    shape = jax.ShapeDtypeStruct
    spot = jnp.stack([chip, core]).astype(jnp.int32)

    k_all = by_head(keys[0])
    k1_own = up_chip(half_of(k_all, core))
    k0_other = swapped(half_of(k_all, 1 - core))
    k1_other = up_chip(k0_other)
    k2_own = up_chip(k1_own)
    q_all = by_head(queries[0])
    v_all = by_head(values[0])
    give = jnp.concatenate([half_of(q_all, 1 - core), half_of(v_all, 1 - core)], axis=0)
    got = swapped(give)

    table = shape((3 * CORES, rows, width), f32)
    cos_table, sin_table = call(table_kernel, (table, table), 2, 2, TABLE_FLOPS)(doc_lengths, spot)
    k2_other = up_chip(k1_other)

    stats = shape((CORES * heads, members * rows), f32)
    q_shape = shape((CORES, heads, members * rows, width), bf16)
    key_scratch = pltpu.VMEM((CORES, heads, rows, width), bf16)

    def slots(count):
        return (
            pltpu.HBM((count, heads, rows, members * rows), bf16),
            shape((count, heads, members * rows), f32),
        )

    def staged(count):
        return (
            key_scratch,
            pltpu.VMEM((count, heads, rows, members * rows), bf16),
            pltpu.SemaphoreType.DMA((count, heads)),
        )

    v_shape = shape((CORES * heads, rows, width), bf16)
    query_rot, v0, weight_0, mark_0, peak, total = call(
        first_kernel, (q_shape, v_shape, *slots(3), stats, stats), 2, 9, FIRST_FLOPS,
        staged(3), far_out=(2,),
    )(doc_lengths, spot, cos_table, sin_table, k_all, k0_other, q_all, v_all, got)
    v1 = up_chip(v0)
    v2 = up_chip(v1)
    weight_1, mark_1, weight_2, mark_2, level, squares = call(
        rest_kernel,
        (*slots(4), *slots(3), stats, shape((16, width), f32)),
        2,
        11,
        NEXT_FLOPS,
        (
            pltpu.VMEM(stats.shape, f32), pltpu.VMEM(stats.shape, f32),
            *staged(4), *staged(3),
        ),
        far_out=(0, 2),
    )(
        doc_lengths, spot, cos_table, sin_table, k1_own, k1_other, k2_own, k2_other, query_rot,
        peak, total,
    )
    squares = sum_over(("seq_1", "seq_2"), squares)
    squares = sum_over(("dp_0", "dp_1", "seq_0"), squares)
    z_loss = squares[0, 0] / (devices * rows * query_heads)

    weight_0, weight_1, weight_2 = (
        pltpu.with_memory_space_constraint(array, pltpu.HBM)
        for array in (weight_0, weight_1, weight_2)
    )
    sum_shape = shape((CORES, heads, width, members * rows), f32)
    (near,) = call(
        near_kernel, (sum_shape,), 1, 8, NEAR_FLOPS,
        (*staged(3)[1:2], *staged(4)[1:2], *staged(3)[2:], *staged(4)[2:]),
        far_in=(2, 4),
    )(spot, level, weight_0, mark_0, weight_1, mark_1, v0, v1)
    out_shape = shape((heads * members, rows, width), bf16)
    own, other = (
        call(
            functools.partial(far_kernel, side), (out_shape,), 1, 6, NEAR_FLOPS,
            (pltpu.VMEM(sum_shape.shape[1:], f32), *staged(3)[1:]),
            far_in=(2,),
        )(spot, level, weight_2, mark_2, v2, near)[0]
        for side in range(2)
    )
    partner = swapped(other)
    low = jnp.where(core == 0, own, partner)
    high = jnp.where(core == 0, partner, own)
    attended = jnp.transpose(jnp.concatenate([low, high], axis=0), (1, 0, 2))
    return (attended[None], z_loss)


def sum_over(axes, part):
    count = lax.axis_size(axes)
    spread = jnp.broadcast_to(part[:1], (count, part.shape[1]))
    return jnp.sum(lax.all_to_all(spread, axes, 0, 0), axis=0, keepdims=True)


VMEM_LIMIT = 20 * 1024 * 1024
TABLE_FLOPS = 4_000_000
FIRST_FLOPS = 6_000_000
NEXT_FLOPS = 6_000_000
NEAR_FLOPS = 3_000_000


def solution(mesh):
    torus = Mesh(mesh.devices.reshape(8, 2, 2, 8, 2), ("dp_0", "dp_1", "seq_0", "seq_1", "seq_2"))
    in_specs = (P(DP, SEQ, None, None), P(DP, SEQ, None, None), P(DP, SEQ, None, None), P(DP, None))
    out_specs = (P(DP, SEQ, None, None), P())
    return jax.shard_map(
        device_part, mesh=torus, in_specs=in_specs, out_specs=out_specs, check_vma=False
    )
```

time: 123 us -> 130 us (1.057)
  blocking collectives: 15.4 us -> 34.1 us
  waiting for transfers between devices: 15.1 us -> 26.8 us
  starting transfers between devices: 44.3 us -> 32.8 us
  Pallas kernels: 35.6 us -> 24.8 us
  local copies, waits for them, and re-layouts: 8.1 us -> 5.4 us
    ppermute x6, waiting for transfers between devices: 4.68 us -> 26.8 us  [up_chip(): lax.ppermute(block, SEQ, [(i, i + step) for i in range(count - step)])]
    all_to_all x1 -> x2, blocking collectives: 15.4 us -> 34.1 us  [sum_over(): return jnp.sum(lax.all_to_all(spread, axes, 0, 0), axis=0, keepdims=True)]
    pallas_call x6, Pallas kernels: 35.6 us -> 24.8 us  [run(): pl.pallas_call(kernel, out_shape=out_shape, in_specs=[SMEM] * scalars + [...]
    all_to_all x1 -> x0, waiting for transfers between devices: 8.57 us -> none  [sum_over(): return jnp.sum(lax.all_to_all(spread, axes, 0, 0), axis=0, keepdims=True)]
    all_to_all x1 -> x0, starting transfers between devices: 8.14 us -> none  [sum_over(): return jnp.sum(lax.all_to_all(spread, axes, 0, 0), axis=0, keepdims=True)]
    another operation x8 -> x0, local copies, waits for them, and re-layouts: 3.42 us -> none
    unnamed x17 -> x6, local copies, waits for them, and re-layouts: 2.47 us -> 5.38 us
    ppermute x6, starting transfers between devices: 21.5 us -> 19.2 us  [up_chip(): lax.ppermute(block, SEQ, [(i, i + step) for i in range(count - step)])]
  transfers between devices with their start and end apart: 10 -> 9, of which waited for: 5 -> 5; matrix products, arithmetic and copies ran while one was open for 3% -> 2% of each run, Pallas kernels for 25% -> 13%
where the time goes in v2:
time: 130 us; the launch traced here: 129 us
  blocking collectives  34.1 us (26%)
  starting transfers between devices  32.8 us (25%)
  waiting for transfers between devices  26.8 us (21%)
  Pallas kernels  24.8 us (19%)
  local copies, waits for them, and re-layouts  5.4 us (4%)
  other arithmetic  3.1 us (2%)
  between operations  2.03 us (2%)
    all_to_all x2, blocking collectives, sum_over(): return jnp.sum(lax.all_to_all(spread, axes, 0, 0), axis=0, keepdims=True)  34.1 us
    ppermute x6, waiting for transfers between devices, up_chip(): lax.ppermute(block, SEQ, [(i, i + step) for i in range(count - step)])  26.8 us
    pallas_call x6, Pallas kernels, run(): pl.pallas_call(kernel, out_shape=out_shape, in_specs=[SMEM] * scalars + [...  24.8 us
    ppermute x6, starting transfers between devices, up_chip(): lax.ppermute(block, SEQ, [(i, i + step) for i in range(count - step)])  19.2 us
    ppermute x3, starting transfers between devices, swapped(): return lax.ppermute(block, 'seq_2', [(0, 1), (1, 0)])  13.6 us
    unnamed x6, local copies, waits for them, and re-layouts  5.38 us
  transfers between devices with their start and end apart: 9, of which 5 were waited for; matrix products, arithmetic and copies ran while one was open for 2% of the time, Pallas kernels for 13%

profile of v2, /device:TPU:1, one launch (start us, length us, event | category | flops | bytes accessed | tf_op | source)
XLA Modules:
  0.0 129.0 jit_solution(18065908017468481030)
XLA Ops:
  0.6 1.5 %copy.23 = bf16[1,256,16,128]{3,1,2,0:T(8,128)(2,1)S(1)} copy(bf16[1,256,16,128]{3,2,1,0:T(8,128)(2,1)} %param.4) | data formatting | bytes 2097152 | tf_op args[0]
  2.1 1.1 copy.24
  3.2 0.0 copy-start
  3.3 0.1 slice_select_fusion
  3.4 0.9 pad_maximum_fusion
  4.3 8.7 %collective-permute-start.5 = (bf16[12,256,128]{2,1,0:T(8,128)(2,1)}, bf16[12,256,128]{2,1,0:T(8,128)(2,1)S(1)}, u32[]{:S(2)}, u32[]{:S(2)}) collective-permute-start(bf16[12,256,128]{2,1,0:T(8,128)(2,1)} %pad_maximum_fusion), channel_id=1, source_target_pairs={{0,1},{1,0},{2,3},{3,2},{4,5},{5,4},{6,7},{7,6},{8,9},{9,8},{10,11... | collective-permute-start | bytes 2359304 | tf_op jit(solution)/shard_map/ppermute | solution.py:40
  13.1 1.1 copy.25
  14.2 0.7 broadcast_select_fusion.2
  14.9 1.9 %collective-permute-start.1 = (bf16[4,256,128]{2,1,0:T(8,128)(2,1)}, bf16[4,256,128]{2,1,0:T(8,128)(2,1)S(1)}, u32[]{:S(2)}, u32[]{:S(2)}) collective-permute-start(bf16[4,256,128]{2,1,0:T(8,128)(2,1)} %get-tuple-element.38), channel_id=1, source_target_pairs={{0,1},{1,0},{2,3},{3,2},{4,5},{5,4},{6,7},{7,6},{8,9},{9,8},{10,11... | collective-permute-start | bytes 786440 | tf_op jit(solution)/shard_map/ppermute | solution.py:40
  16.8 0.1 pad_add_fusion.spot_ref
  16.9 0.0 copy-done
  16.9 2.6 %shard_map.59 = (f32[6,256,128]{2,1,0:T(8,128)S(1)}, f32[6,256,128]{2,1,0:T(8,128)S(1)}) custom-call(s32[1,8]{1,0:T(1,128)S(1)} %copy-done, s32[2]{0:T(128)S(1)} %pad_add_fusion.spot_ref), custom_call_target="tpu_custom_call" | custom-call | flops 4000000 | tf_op jit(solution)/shard_map/pallas_call | solution.py:331
  19.5 0.0 collective-permute-done.1.k_other
  19.5 0.0 collective-permute-done.5.got_ref
  19.5 4.8 %shard_map.60 = (bf16[2,4,512,128]{3,2,1,0:T(8,128)(2,1)S(1)}, bf16[8,256,128]{2,1,0:T(8,128)(2,1)S(1)}, bf16[3,4,256,512]{3,2,1,0:T(8,128)(2,1)}, f32[3,4,512]{...) custom-call(s32[1,8]{1,0:T(1,128)S(1)} %copy-done, s32[2]{0:T(128)S(1)} %pad_add_fusion.spot_ref, ...), custom_call_target="tpu_custom_call" | custom-call | flops 6000000 | tf_op jit(solution)/shard_map/pallas_call | solution.py:331
  24.3 1.3 %collective-permute-start.6 = (bf16[8,256,128]{2,1,0:T(8,128)(2,1)S(1)}, bf16[8,256,128]{2,1,0:T(8,128)(2,1)S(1)}, u32[]{:S(2)}, u32[]{:S(2)}) collective-permute-start(bf16[8,256,128]{2,1,0:T(8,128)(2,1)S(1)} %get-tuple-element.24.v0_ref), channel_id=1, source_target_pairs={{0,2},{1,3},{2,4},{3,5},{4,6},{5,7},{6,8},{7,9},{8,10},{9,11},{10,... | collective-permute-start | bytes 1572872 | tf_op jit(solution)/shard_map/ppermute | solution.py:36
  25.6 1.3 %collective-permute-start = (bf16[4,256,128]{2,1,0:T(8,128)(2,1)S(1)}, bf16[4,256,128]{2,1,0:T(8,128)(2,1)S(1)}, u32[]{:S(2)}, u32[]{:S(2)}) collective-permute-start(bf16[4,256,128]{2,1,0:T(8,128)(2,1)S(1)} %get-tuple-element.39), channel_id=1, source_target_pairs={{0,2},{1,3},{2,4},{3,5},{4,6},{5,7},{6,8},{7,9},{8,10},{9,11},{10,... | collective-permute-start | bytes 786440 | tf_op jit(solution)/shard_map/ppermute | solution.py:36
  27.0 4.0 %collective-permute-start.2 = (bf16[4,256,128]{2,1,0:T(8,128)(2,1)S(1)}, bf16[4,256,128]{2,1,0:T(8,128)(2,1)S(1)}, u32[]{:S(2)}, u32[]{:S(2)}) collective-permute-start(bf16[4,256,128]{2,1,0:T(8,128)(2,1)S(1)} %collective-permute-done.1.k_other), channel_id=1, source_target_pairs={{0,2},{1,3},{2,4},{3,5},{4,6},{5,7},{6,8},{7,9},{8,10},{9,11},{10,... | collective-permute-start | bytes 786440 | tf_op jit(solution)/shard_map/ppermute | solution.py:36
  31.0 5.7 %collective-permute-done.6.v1_ref = bf16[8,256,128]{2,1,0:T(8,128)(2,1)S(1)} collective-permute-done((bf16[8,256,128]{2,1,0:T(8,128)(2,1)S(1)}, bf16[8,256,128]{2,1,0:T(8,128)(2,1)S(1)}, u32[]{:S(2)}, u32[]{:S(2)}) %collective-permute-start.6) | collective-permute-done | bytes 524320 | tf_op jit(solution)/shard_map/ppermute | solution.py:36
  36.7 4.1 %collective-permute-start.7 = (bf16[8,256,128]{2,1,0:T(8,128)(2,1)S(1)}, bf16[8,256,128]{2,1,0:T(8,128)(2,1)S(1)}, u32[]{:S(2)}, u32[]{:S(2)}) collective-permute-start(bf16[8,256,128]{2,1,0:T(8,128)(2,1)S(1)} %collective-permute-done.6.v1_ref), channel_id=1, source_target_pairs={{0,2},{1,3},{2,4},{3,5},{4,6},{5,7},{6,8},{7,9},{8,10},{9,11},{10,... | collective-permute-start | bytes 1572872 | tf_op jit(solution)/shard_map/ppermute | solution.py:36
  40.8 1.5 %collective-permute-done.k1_own = bf16[4,256,128]{2,1,0:T(8,128)(2,1)S(1)} collective-permute-done((bf16[4,256,128]{2,1,0:T(8,128)(2,1)S(1)}, bf16[4,256,128]{2,1,0:T(8,128)(2,1)S(1)}, u32[]{:S(2)}, u32[]{:S(2)}) %collective-permute-start) | collective-permute-done | bytes 262176 | tf_op jit(solution)/shard_map/ppermute | solution.py:36
  42.3 4.1 %collective-permute-start.3 = (bf16[4,256,128]{2,1,0:T(8,128)(2,1)S(1)}, bf16[4,256,128]{2,1,0:T(8,128)(2,1)S(1)}, u32[]{:S(2)}, u32[]{:S(2)}) collective-permute-start(bf16[4,256,128]{2,1,0:T(8,128)(2,1)S(1)} %collective-permute-done.k1_own), channel_id=1, source_target_pairs={{0,2},{1,3},{2,4},{3,5},{4,6},{5,7},{6,8},{7,9},{8,10},{9,11},{10,... | collective-permute-start | bytes 786440 | tf_op jit(solution)/shard_map/ppermute | solution.py:36
  46.4 1.5 %collective-permute-done.2.k1_other = bf16[4,256,128]{2,1,0:T(8,128)(2,1)S(1)} collective-permute-done((bf16[4,256,128]{2,1,0:T(8,128)(2,1)S(1)}, bf16[4,256,128]{2,1,0:T(8,128)(2,1)S(1)}, u32[]{:S(2)}, u32[]{:S(2)}) %collective-permute-start.2) | collective-permute-done | bytes 262176 | tf_op jit(solution)/shard_map/ppermute | solution.py:36
  47.9 4.3 %collective-permute-start.4 = (bf16[4,256,128]{2,1,0:T(8,128)(2,1)S(1)}, bf16[4,256,128]{2,1,0:T(8,128)(2,1)S(1)}, u32[]{:S(2)}, u32[]{:S(2)}) collective-permute-start(bf16[4,256,128]{2,1,0:T(8,128)(2,1)S(1)} %collective-permute-done.2.k1_other), channel_id=1, source_target_pairs={{0,2},{1,3},{2,4},{3,5},{4,6},{5,7},{6,8},{7,9},{8,10},{9,11},{10,... | collective-permute-start | bytes 786440 | tf_op jit(solution)/shard_map/ppermute | solution.py:36
  52.2 12.6 %collective-permute-done.3.k2_own = bf16[4,256,128]{2,1,0:T(8,128)(2,1)S(1)} collective-permute-done((bf16[4,256,128]{2,1,0:T(8,128)(2,1)S(1)}, bf16[4,256,128]{2,1,0:T(8,128)(2,1)S(1)}, u32[]{:S(2)}, u32[]{:S(2)}) %collective-permute-start.3) | collective-permute-done | bytes 262176 | tf_op jit(solution)/shard_map/ppermute | solution.py:36
  64.7 5.6 %collective-permute-done.4.k2_other = bf16[4,256,128]{2,1,0:T(8,128)(2,1)S(1)} collective-permute-done((bf16[4,256,128]{2,1,0:T(8,128)(2,1)S(1)}, bf16[4,256,128]{2,1,0:T(8,128)(2,1)S(1)}, u32[]{:S(2)}, u32[]{:S(2)}) %collective-permute-start.4) | collective-permute-done | bytes 262176 | tf_op jit(solution)/shard_map/ppermute | solution.py:36
  70.4 7.6 %shard_map.61 = (bf16[4,4,256,512]{3,2,1,0:T(8,128)(2,1)}, f32[4,4,512]{2,1,0:T(4,128)S(1)}, bf16[3,4,256,512]{3,2,1,0:T(8,128)(2,1)}, f32[3,4,512]{2,1,0:T(4,12...) custom-call(s32[1,8]{1,0:T(1,128)S(1)} %copy-done, s32[2]{0:T(128)S(1)} %pad_add_fusion.spot_ref, ...), custom_call_target="tpu_custom_call" | custom-call | flops 6000000 | tf_op jit(solution)/shard_map/pallas_call | solution.py:331
  78.0 4.6 %shard_map.62.near_ref = f32[2,4,128,512]{3,2,1,0:T(8,128)S(1)} custom-call(s32[2]{0:T(128)S(1)} %pad_add_fusion.spot_ref, f32[8,512]{1,0:T(8,128)S(1)} %get-tuple-element.21.level_ref, bf16[3,4,256,512]{3,2,1,0:T(8,128)(2,1)} %get-tuple-element.25.weight_0, f32[3,4,512]{2,1,0:T(4,128)S(1)} %get-tuple-element.26.mark_0, ...), custom_call_target="tpu_custom_call" | custom-call | flops 3000000 | tf_op jit(solution)/shard_map/pallas_call | solution.py:331
  82.6 0.0 collective-permute-done.7.v2_ref
  82.6 2.6 %shard_map.64 = bf16[8,256,128]{2,1,0:T(8,128)(2,1)S(1)} custom-call(s32[2]{0:T(128)S(1)} %pad_add_fusion.spot_ref, f32[8,512]{1,0:T(8,128)S(1)} %get-tuple-element.21.level_ref, bf16[3,4,256,512]{3,2,1,0:T(8,128)(2,1)} %get-tuple-element.22.weight_2, f32[3,4,512]{2,1,0:T(4,128)S(1)} %get-tuple-element.23.mark_2, ...), custom_call_target="tpu_custom_call" | custom-call | flops 3000000 | tf_op jit(solution)/shard_map/pallas_call | solution.py:331
  85.2 3.0 %collective-permute-start.8 = (bf16[8,256,128]{2,1,0:T(8,128)(2,1)S(1)}, bf16[8,256,128]{2,1,0:T(8,128)(2,1)}, u32[]{:S(2)}, u32[]{:S(2)}) collective-permute-start(bf16[8,256,128]{2,1,0:T(8,128)(2,1)S(1)} %shard_map.64), channel_id=1, source_target_pairs={{0,1},{1,0},{2,3},{3,2},{4,5},{5,4},{6,7},{7,6},{8,9},{9,8},{10,11... | collective-permute-start | bytes 1572872 | tf_op jit(solution)/shard_map/ppermute | solution.py:40
  88.2 15.9 %all_to_all.12 = f32[16,1,128]{2,1,0:T(1,128)S(1)} all-to-all(f32[16,1,128]{2,1,0:T(1,128)S(1)} %broadcast_in_dim.18), channel_id=1, replica_groups=mesh['dp_0'=8,'dp_1'=2,'seq_0'=2,'seq_1'=8,'seq_2'=2] {'seq_1','seq_2'}, dimensions={0} | all-to-all | bytes 16384 | tf_op jit(solution)/shard_map/all_to_all | solution.py:454
  104.2 18.1 %all_to_all.13 = f32[32,1,128]{2,1,0:T(1,128)S(1)} all-to-all(f32[32,1,128]{2,1,0:T(1,128)S(1)} %broadcast_in_dim.19), channel_id=1, replica_groups=mesh['dp_0'=8,'dp_1'=2,'seq_0'=2,'seq_1'=8,'seq_2'=2] {'dp_0','dp_1','se..., dimensions={0} | all-to-all | bytes 32768 | tf_op jit(solution)/shard_map/all_to_all | solution.py:454
  122.4 2.6 %shard_map.63 = bf16[8,256,128]{2,1,0:T(8,128)(2,1)S(1)} custom-call(s32[2]{0:T(128)S(1)} %pad_add_fusion.spot_ref, f32[8,512]{1,0:T(8,128)S(1)} %get-tuple-element.21.level_ref, bf16[3,4,256,512]{3,2,1,0:T(8,128)(2,1)} %get-tuple-element.22.weight_2, f32[3,4,512]{2,1,0:T(4,128)S(1)} %get-tuple-element.23.mark_2, ...), custom_call_target="tpu_custom_call" | custom-call | flops 3000000 | tf_op jit(solution)/shard_map/pallas_call | solution.py:331
  125.0 0.0 collective-permute-done.8
  125.0 1.1 broadcast_select_fusion.1
  126.1 0.1 maximum_bitcast_fusion
  126.2 1.6 %copy.19 = bf16[1,256,16,128]{3,2,1,0:T(8,128)(2,1)} copy(bf16[1,256,16,128]{3,1,2,0:T(8,128)(2,1)S(1)} %maximum_bitcast_fusion) | data formatting | bytes 2097152
  (6 shorter events, 0.1 us)
Async XLA Ops:
  3.2 13.7 %copy-start = (s32[1,8]{1,0:T(1,128)S(1)}, s32[1,8]{1,0:T(1,128)}, u32[]{:S(2)}) copy-start(s32[1,8]{1,0:T(1,128)} %lengths_ref.5) | copy-start | bytes 100
  4.3 15.2 %collective-permute-start.5 = (bf16[12,256,128]{2,1,0:T(8,128)(2,1)}, bf16[12,256,128]{2,1,0:T(8,128)(2,1)S(1)}, u32[]{:S(2)}, u32[]{:S(2)}) collective-permute-start(bf16[12,256,128]{2,1,0:T(8,128)(2,1)} %pad_maximum_fusion), channel_id=1, source_target_pairs={{0,1},{1,0},{2,3},{3,2},{4,5},{5,4},{6,7},{7,6},{8,9},{9,8},{10,11... | collective-permute-start | bytes 2359304 | tf_op jit(solution)/shard_map/ppermute | solution.py:40
  14.9 4.6 %collective-permute-start.1 = (bf16[4,256,128]{2,1,0:T(8,128)(2,1)}, bf16[4,256,128]{2,1,0:T(8,128)(2,1)S(1)}, u32[]{:S(2)}, u32[]{:S(2)}) collective-permute-start(bf16[4,256,128]{2,1,0:T(8,128)(2,1)} %get-tuple-element.38), channel_id=1, source_target_pairs={{0,1},{1,0},{2,3},{3,2},{4,5},{5,4},{6,7},{7,6},{8,9},{9,8},{10,11... | collective-permute-start | bytes 786440 | tf_op jit(solution)/shard_map/ppermute | solution.py:40
  24.3 12.3 %collective-permute-start.6 = (bf16[8,256,128]{2,1,0:T(8,128)(2,1)S(1)}, bf16[8,256,128]{2,1,0:T(8,128)(2,1)S(1)}, u32[]{:S(2)}, u32[]{:S(2)}) collective-permute-start(bf16[8,256,128]{2,1,0:T(8,128)(2,1)S(1)} %get-tuple-element.24.v0_ref), channel_id=1, source_target_pairs={{0,2},{1,3},{2,4},{3,5},{4,6},{5,7},{6,8},{7,9},{8,10},{9,11},{10,... | collective-permute-start | bytes 1572872 | tf_op jit(solution)/shard_map/ppermute | solution.py:36
  25.6 16.6 %collective-permute-start = (bf16[4,256,128]{2,1,0:T(8,128)(2,1)S(1)}, bf16[4,256,128]{2,1,0:T(8,128)(2,1)S(1)}, u32[]{:S(2)}, u32[]{:S(2)}) collective-permute-start(bf16[4,256,128]{2,1,0:T(8,128)(2,1)S(1)} %get-tuple-element.39), channel_id=1, source_target_pairs={{0,2},{1,3},{2,4},{3,5},{4,6},{5,7},{6,8},{7,9},{8,10},{9,11},{10,... | collective-permute-start | bytes 786440 | tf_op jit(solution)/shard_map/ppermute | solution.py:36
  27.0 20.9 %collective-permute-start.2 = (bf16[4,256,128]{2,1,0:T(8,128)(2,1)S(1)}, bf16[4,256,128]{2,1,0:T(8,128)(2,1)S(1)}, u32[]{:S(2)}, u32[]{:S(2)}) collective-permute-start(bf16[4,256,128]{2,1,0:T(8,128)(2,1)S(1)} %collective-permute-done.1.k_other), channel_id=1, source_target_pairs={{0,2},{1,3},{2,4},{3,5},{4,6},{5,7},{6,8},{7,9},{8,10},{9,11},{10,... | collective-permute-start | bytes 786440 | tf_op jit(solution)/shard_map/ppermute | solution.py:36
  36.7 45.9 %collective-permute-start.7 = (bf16[8,256,128]{2,1,0:T(8,128)(2,1)S(1)}, bf16[8,256,128]{2,1,0:T(8,128)(2,1)S(1)}, u32[]{:S(2)}, u32[]{:S(2)}) collective-permute-start(bf16[8,256,128]{2,1,0:T(8,128)(2,1)S(1)} %collective-permute-done.6.v1_ref), channel_id=1, source_target_pairs={{0,2},{1,3},{2,4},{3,5},{4,6},{5,7},{6,8},{7,9},{8,10},{9,11},{10,... | collective-permute-start | bytes 1572872 | tf_op jit(solution)/shard_map/ppermute | solution.py:36
  42.3 22.5 %collective-permute-start.3 = (bf16[4,256,128]{2,1,0:T(8,128)(2,1)S(1)}, bf16[4,256,128]{2,1,0:T(8,128)(2,1)S(1)}, u32[]{:S(2)}, u32[]{:S(2)}) collective-permute-start(bf16[4,256,128]{2,1,0:T(8,128)(2,1)S(1)} %collective-permute-done.k1_own), channel_id=1, source_target_pairs={{0,2},{1,3},{2,4},{3,5},{4,6},{5,7},{6,8},{7,9},{8,10},{9,11},{10,... | collective-permute-start | bytes 786440 | tf_op jit(solution)/shard_map/ppermute | solution.py:36
  47.9 22.5 %collective-permute-start.4 = (bf16[4,256,128]{2,1,0:T(8,128)(2,1)S(1)}, bf16[4,256,128]{2,1,0:T(8,128)(2,1)S(1)}, u32[]{:S(2)}, u32[]{:S(2)}) collective-permute-start(bf16[4,256,128]{2,1,0:T(8,128)(2,1)S(1)} %collective-permute-done.2.k1_other), channel_id=1, source_target_pairs={{0,2},{1,3},{2,4},{3,5},{4,6},{5,7},{6,8},{7,9},{8,10},{9,11},{10,... | collective-permute-start | bytes 786440 | tf_op jit(solution)/shard_map/ppermute | solution.py:36
  85.2 39.8 %collective-permute-start.8 = (bf16[8,256,128]{2,1,0:T(8,128)(2,1)S(1)}, bf16[8,256,128]{2,1,0:T(8,128)(2,1)}, u32[]{:S(2)}, u32[]{:S(2)}) collective-permute-start(bf16[8,256,128]{2,1,0:T(8,128)(2,1)S(1)} %shard_map.64), channel_id=1, source_target_pairs={{0,1},{1,0},{2,3},{3,2},{4,5},{5,4},{6,7},{7,6},{8,9},{9,8},{10,11... | collective-permute-start | bytes 1572872 | tf_op jit(solution)/shard_map/ppermute | solution.py:40

commit v3 on v2

--- a/solution.py
+++ b/solution.py
@@ -77,26 +77,39 @@
         pl.when(condition)(body)
 
 
-def table_kernel(lengths_ref, spot_ref, cos_ref, sin_ref):
+def cos_sin(angles):
+    turns = jnp.floor(angles * (2.0 / math.pi) + 0.5)
+    rest = ((angles - turns * 1.5703125) - turns * 4.837512969970703125e-4) - turns * 7.54978995489188216e-8
+    square = rest * rest
+    sine = (
+        (-1.9515295891e-4 * square + 8.3321608736e-3) * square - 1.6666654611e-1
+    ) * square * rest + rest
+    cosine = (
+        (2.443315711809948e-5 * square - 1.388731625493765e-3) * square + 4.166664568298827e-2
+    ) * square * square - 0.5 * square + 1.0
+    quarter = turns.astype(jnp.int32)
+    odd = (quarter & 1) == 1
+    return (
+        jnp.where(((quarter + 1) & 2) == 2, -1.0, 1.0) * jnp.where(odd, sine, cosine),
+        jnp.where((quarter & 2) == 2, -1.0, 1.0) * jnp.where(odd, cosine, sine),
+    )
+
+
+def table_kernel(lengths_ref, spot_ref, frequency_ref, cos_ref, sin_ref):
     rows, width = cos_ref.shape[1:]
     half = width // 2
     pairs = rows // 2
     ends = doc_ends(lengths_ref)
-    lane = lax.broadcasted_iota(jnp.int32, (pairs, width), 1)
-    upper = lane >= half
-    slot = jnp.where(upper, lane - half, lane).astype(jnp.float32)
-    frequency = jnp.exp2(slot * (-2.0 * math.log2(rope_base) / width))
+    upper = lax.broadcasted_iota(jnp.int32, (pairs, width), 1) >= half
     sign = jnp.where(upper, 1.0, -1.0)
+    frequency = frequency_ref[...]
     for index in range(cos_ref.shape[0]):
         begin = block_start(spot_ref, rows, index // CORES, index % CORES)
         at = begin + lax.broadcasted_iota(jnp.int32, (pairs, width), 0)
         at = at + jnp.where(upper, pairs, 0)
         places = at - doc_start(ends, at, jnp.zeros_like(at))
-        angles = places.astype(jnp.float32) * frequency
-        for out_ref, table, factor in (
-            (cos_ref, jnp.cos(angles), None),
-            (sin_ref, jnp.sin(angles), sign),
-        ):
+        cosine, sine = cos_sin(places.astype(jnp.float32) * frequency)
+        for out_ref, table, factor in ((cos_ref, cosine, None), (sin_ref, sine, sign)):
             turned = pltpu.roll(table, half, 1)
             first = jnp.where(upper, turned, table)
             second = jnp.where(upper, table, turned)
@@ -218,32 +231,37 @@
     )()
 
 
-def rest_kernel(
-    lengths_ref, spot_ref, cos_ref, sin_ref, k1_own, k1_other, k2_own, k2_other, query_ref,
-    old_peak, old_total,
-    weight_1, mark_1, weight_2, mark_2, level_ref, squares_ref,
-    peak_ref, total_ref, key_1, stage_1, sent_1, key_2, stage_2, sent_2,
-):
+def next_kernel(
+    lengths_ref, spot_ref, cos_ref, sin_ref, k_own, k_other, query_ref, old_peak, old_total,
+    weight_ref, mark_ref, peak_ref, total_ref, key_ref, stage_ref, sent,
+):
+    raw = (k_own, k_other)
+    rotate_keys(1, lambda side, head: raw[side][head], cos_ref, sin_ref, key_ref)
     peak_ref[...] = old_peak[...]
     total_ref[...] = old_total[...]
-    waits = []
-    for group, raw, key_ref, weight_ref, mark_ref, stage_ref, sent in (
-        (1, (k1_own, k1_other), key_1, weight_1, mark_1, stage_1, sent_1),
-        (2, (k2_own, k2_other), key_2, weight_2, mark_2, stage_2, sent_2),
-    ):
-        rotate_keys(group, lambda side, head: raw[side][head], cos_ref, sin_ref, key_ref)
-        waits.append(
-            gather_stats(
-                group, lengths_ref, spot_ref, query_ref, lambda s, h: key_ref[s, h],
-                weight_ref, mark_ref, peak_ref, total_ref, stage_ref, sent,
-            )
-        )
+    gather_stats(
+        1, lengths_ref, spot_ref, query_ref, lambda s, h: key_ref[s, h],
+        weight_ref, mark_ref, peak_ref, total_ref, stage_ref, sent,
+    )()
+
+
+def last_kernel(
+    lengths_ref, spot_ref, cos_ref, sin_ref, k_own, k_other, query_ref, old_peak, old_total,
+    weight_ref, mark_ref, level_ref, squares_ref, peak_ref, total_ref, key_ref, stage_ref, sent,
+):
+    raw = (k_own, k_other)
+    rotate_keys(2, lambda side, head: raw[side][head], cos_ref, sin_ref, key_ref)
+    peak_ref[...] = old_peak[...]
+    total_ref[...] = old_total[...]
+    wait_all = gather_stats(
+        2, lengths_ref, spot_ref, query_ref, lambda s, h: key_ref[s, h],
+        weight_ref, mark_ref, peak_ref, total_ref, stage_ref, sent,
+    )
     natural = peak_ref[...] * score_scale + jnp.log(total_ref[...])
     level_ref[...] = natural * log2_e
     squares = jnp.sum(natural * natural, axis=(0, 1), keepdims=True)
     squares_ref[...] = jnp.broadcast_to(squares, squares_ref.shape)
-    for wait_all in waits:
-        wait_all()
+    wait_all()
 
 
 def fetch(weight_ref, held_ref, ready):
@@ -376,7 +394,12 @@
     got = swapped(give)
 
     table = shape((3 * CORES, rows, width), f32)
-    cos_table, sin_table = call(table_kernel, (table, table), 2, 2, TABLE_FLOPS)(doc_lengths, spot)
+    lane = jnp.arange(width // 2, dtype=f32)
+    frequency = rope_base ** (-2.0 * lane / width)
+    frequency = jnp.concatenate([frequency, frequency])[None, :]
+    cos_table, sin_table = call(table_kernel, (table, table), 2, 3, TABLE_FLOPS)(
+        doc_lengths, spot, frequency
+    )
     k2_other = up_chip(k1_other)
 
     stats = shape((CORES * heads, members * rows), f32)
@@ -403,23 +426,25 @@
     )(doc_lengths, spot, cos_table, sin_table, k_all, k0_other, q_all, v_all, got)
     v1 = up_chip(v0)
     v2 = up_chip(v1)
-    weight_1, mark_1, weight_2, mark_2, level, squares = call(
-        rest_kernel,
-        (*slots(4), *slots(3), stats, shape((16, width), f32)),
+    weight_1, mark_1, peak, total = call(
+        next_kernel, (*slots(4), stats, stats), 2, 9, NEXT_FLOPS, staged(4),
+        far_out=(0,),
+    )(doc_lengths, spot, cos_table, sin_table, k1_own, k1_other, query_rot, peak, total)
+    weight_2, mark_2, level, squares = call(
+        last_kernel,
+        (*slots(3), stats, shape((lax.axis_size(("seq_1", "seq_2")), width), f32)),
         2,
-        11,
+        9,
         NEXT_FLOPS,
-        (
-            pltpu.VMEM(stats.shape, f32), pltpu.VMEM(stats.shape, f32),
-            *staged(4), *staged(3),
-        ),
-        far_out=(0, 2),
-    )(
-        doc_lengths, spot, cos_table, sin_table, k1_own, k1_other, k2_own, k2_other, query_rot,
-        peak, total,
-    )
-    squares = sum_over(("seq_1", "seq_2"), squares)
-    squares = sum_over(("dp_0", "dp_1", "seq_0"), squares)
+        (pltpu.VMEM(stats.shape, f32), pltpu.VMEM(stats.shape, f32), *staged(3)),
+        far_out=(0,),
+    )(doc_lengths, spot, cos_table, sin_table, k2_own, k2_other, query_rot, peak, total)
+    squares = lax.all_to_all(squares, ("seq_1", "seq_2"), 0, 0)
+    across = ("dp_0", "dp_1", "seq_0")
+    squares = jnp.sum(squares, axis=0, keepdims=True)
+    squares = jnp.broadcast_to(squares, (lax.axis_size(across), width))
+    squares = lax.all_to_all(squares, across, 0, 0)
+    squares = jnp.sum(squares, axis=0, keepdims=True)
     z_loss = squares[0, 0] / (devices * rows * query_heads)
 
     weight_0, weight_1, weight_2 = (
@@ -448,12 +473,6 @@
     return (attended[None], z_loss)
 
 
-def sum_over(axes, part):
-    count = lax.axis_size(axes)
-    spread = jnp.broadcast_to(part[:1], (count, part.shape[1]))
-    return jnp.sum(lax.all_to_all(spread, axes, 0, 0), axis=0, keepdims=True)
-
-
 VMEM_LIMIT = 20 * 1024 * 1024
 TABLE_FLOPS = 4_000_000
 FIRST_FLOPS = 6_000_000

time: 130 us -> 125 us (0.962)
  waiting for transfers between devices: 26.8 us -> 22.2 us
    ppermute x6, waiting for transfers between devices: 26.8 us -> 22.1 us  [up_chip(): lax.ppermute(block, SEQ, [(i, i + step) for i in range(count - step)])]
    pallas_call x6 -> x7, Pallas kernels: 24.8 us -> 25.4 us  [run(): pl.pallas_call(kernel, out_shape=out_shape, in_specs=[SMEM] * scalars + [...]
  transfers between devices with their start and end apart: 9 -> 9, of which waited for: 5 -> 5; matrix products, arithmetic and copies ran while one was open for 2% -> 2% of each run, Pallas kernels for 13% -> 14%
where the time goes in v3:
time: 125 us
  blocking collectives  34.1 us (27%)
  starting transfers between devices  32.6 us (26%)
  Pallas kernels  25.4 us (20%)
  waiting for transfers between devices  22.2 us (18%)
  local copies, waits for them, and re-layouts  5.39 us (4%)
  other arithmetic  3.21 us (3%)
  between operations  2.04 us (2%)
    pallas_call x7, Pallas kernels, run(): pl.pallas_call(kernel, out_shape=out_shape, in_specs=[SMEM] * scalars + [...  25.4 us
    ppermute x6, waiting for transfers between devices, up_chip(): lax.ppermute(block, SEQ, [(i, i + step) for i in range(count - step)])  22.1 us
    ppermute x6, starting transfers between devices, up_chip(): lax.ppermute(block, SEQ, [(i, i + step) for i in range(count - step)])  19 us
    all_to_all x1, blocking collectives, device_part(): squares = lax.all_to_all(squares, across, 0, 0)  18.1 us
    all_to_all x1, blocking collectives, device_part(): squares = lax.all_to_all(squares, ('seq_1', 'seq_2'), 0, 0)  15.9 us
    ppermute x3, starting transfers between devices, swapped(): return lax.ppermute(block, 'seq_2', [(0, 1), (1, 0)])  13.6 us
    unnamed x6, local copies, waits for them, and re-layouts  5.38 us
  transfers between devices with their start and end apart: 9, of which 5 were waited for; matrix products, arithmetic and copies ran while one was open for 2% of the time, Pallas kernels for 14%

profile of v3, /device:TPU:1, one launch (start us, length us, event | category | flops | bytes accessed | tf_op | source)
XLA Modules:
  0.0 124.8 jit_solution(6535372519231848224)
XLA Ops:
  0.6 1.5 %copy.29 = bf16[1,256,16,128]{3,1,2,0:T(8,128)(2,1)S(1)} copy(bf16[1,256,16,128]{3,2,1,0:T(8,128)(2,1)} %param.4) | data formatting | bytes 2097152 | tf_op args[0]
  2.1 1.1 copy.30
  3.2 0.0 copy-start
  3.3 0.1 slice_select_fusion
  3.4 0.9 pad_maximum_fusion
  4.3 8.7 %collective-permute-start.5 = (bf16[12,256,128]{2,1,0:T(8,128)(2,1)}, bf16[12,256,128]{2,1,0:T(8,128)(2,1)S(1)}, u32[]{:S(2)}, u32[]{:S(2)}) collective-permute-start(bf16[12,256,128]{2,1,0:T(8,128)(2,1)} %pad_maximum_fusion), channel_id=1, source_target_pairs={{0,1},{1,0},{2,3},{3,2},{4,5},{5,4},{6,7},{7,6},{8,9},{9,8},{10,11... | collective-permute-start | bytes 2359304 | tf_op jit(solution)/shard_map/ppermute | solution.py:40
  13.1 1.1 copy.31
  14.2 0.8 broadcast_select_fusion.2
  14.9 1.9 %collective-permute-start.2 = (bf16[4,256,128]{2,1,0:T(8,128)(2,1)}, bf16[4,256,128]{2,1,0:T(8,128)(2,1)S(1)}, u32[]{:S(2)}, u32[]{:S(2)}) collective-permute-start(bf16[4,256,128]{2,1,0:T(8,128)(2,1)} %get-tuple-element.44), channel_id=1, source_target_pairs={{0,1},{1,0},{2,3},{3,2},{4,5},{5,4},{6,7},{7,6},{8,9},{9,8},{10,11... | collective-permute-start | bytes 786440 | tf_op jit(solution)/shard_map/ppermute | solution.py:40
  16.9 0.1 maximum_bitcast_fusion.1.frequency_ref
  16.9 0.1 pad_add_fusion.spot_ref
  17.0 0.0 copy-done
  17.0 1.7 %shard_map.59 = (f32[6,256,128]{2,1,0:T(8,128)S(1)}, f32[6,256,128]{2,1,0:T(8,128)S(1)}) custom-call(s32[1,8]{1,0:T(1,128)S(1)} %copy-done, s32[2]{0:T(128)S(1)} %pad_add_fusion.spot_ref, f32[1,128]{1,0:T(1,128)S(1)} %maximum_bitcast_fusion.1.frequency_ref), custom_call_target="tpu_custom_call" | custom-call | flops 4000000 | tf_op jit(solution)/shard_map/pallas_call | solution.py:349
  18.7 0.0 collective-permute-done.2.k_other
  18.8 0.0 collective-permute-done.5.got_ref
  18.8 4.8 %shard_map.60 = (bf16[2,4,512,128]{3,2,1,0:T(8,128)(2,1)S(1)}, bf16[8,256,128]{2,1,0:T(8,128)(2,1)S(1)}, bf16[3,4,256,512]{3,2,1,0:T(8,128)(2,1)}, f32[3,4,512]{...) custom-call(s32[1,8]{1,0:T(1,128)S(1)} %copy-done, s32[2]{0:T(128)S(1)} %pad_add_fusion.spot_ref, ...), custom_call_target="tpu_custom_call" | custom-call | flops 6000000 | tf_op jit(solution)/shard_map/pallas_call | solution.py:349
  23.5 1.3 %collective-permute-start.6 = (bf16[8,256,128]{2,1,0:T(8,128)(2,1)S(1)}, bf16[8,256,128]{2,1,0:T(8,128)(2,1)S(1)}, u32[]{:S(2)}, u32[]{:S(2)}) collective-permute-start(bf16[8,256,128]{2,1,0:T(8,128)(2,1)S(1)} %get-tuple-element.28.v0_ref), channel_id=1, source_target_pairs={{0,2},{1,3},{2,4},{3,5},{4,6},{5,7},{6,8},{7,9},{8,10},{9,11},{10,... | collective-permute-start | bytes 1572872 | tf_op jit(solution)/shard_map/ppermute | solution.py:36
  24.9 1.3 %collective-permute-start = (bf16[4,256,128]{2,1,0:T(8,128)(2,1)S(1)}, bf16[4,256,128]{2,1,0:T(8,128)(2,1)S(1)}, u32[]{:S(2)}, u32[]{:S(2)}) collective-permute-start(bf16[4,256,128]{2,1,0:T(8,128)(2,1)S(1)} %get-tuple-element.45), channel_id=1, source_target_pairs={{0,2},{1,3},{2,4},{3,5},{4,6},{5,7},{6,8},{7,9},{8,10},{9,11},{10,... | collective-permute-start | bytes 786440 | tf_op jit(solution)/shard_map/ppermute | solution.py:36
  26.2 4.0 %collective-permute-start.3 = (bf16[4,256,128]{2,1,0:T(8,128)(2,1)S(1)}, bf16[4,256,128]{2,1,0:T(8,128)(2,1)S(1)}, u32[]{:S(2)}, u32[]{:S(2)}) collective-permute-start(bf16[4,256,128]{2,1,0:T(8,128)(2,1)S(1)} %collective-permute-done.2.k_other), channel_id=1, source_target_pairs={{0,2},{1,3},{2,4},{3,5},{4,6},{5,7},{6,8},{7,9},{8,10},{9,11},{10,... | collective-permute-start | bytes 786440 | tf_op jit(solution)/shard_map/ppermute | solution.py:36
  30.2 5.7 %collective-permute-done.6.v1_ref = bf16[8,256,128]{2,1,0:T(8,128)(2,1)S(1)} collective-permute-done((bf16[8,256,128]{2,1,0:T(8,128)(2,1)S(1)}, bf16[8,256,128]{2,1,0:T(8,128)(2,1)S(1)}, u32[]{:S(2)}, u32[]{:S(2)}) %collective-permute-start.6) | collective-permute-done | bytes 524320 | tf_op jit(solution)/shard_map/ppermute | solution.py:36
  35.9 4.1 %collective-permute-start.7 = (bf16[8,256,128]{2,1,0:T(8,128)(2,1)S(1)}, bf16[8,256,128]{2,1,0:T(8,128)(2,1)S(1)}, u32[]{:S(2)}, u32[]{:S(2)}) collective-permute-start(bf16[8,256,128]{2,1,0:T(8,128)(2,1)S(1)} %collective-permute-done.6.v1_ref), channel_id=1, source_target_pairs={{0,2},{1,3},{2,4},{3,5},{4,6},{5,7},{6,8},{7,9},{8,10},{9,11},{10,... | collective-permute-start | bytes 1572872 | tf_op jit(solution)/shard_map/ppermute | solution.py:36
  40.0 1.5 %collective-permute-done.k_own = bf16[4,256,128]{2,1,0:T(8,128)(2,1)S(1)} collective-permute-done((bf16[4,256,128]{2,1,0:T(8,128)(2,1)S(1)}, bf16[4,256,128]{2,1,0:T(8,128)(2,1)S(1)}, u32[]{:S(2)}, u32[]{:S(2)}) %collective-permute-start) | collective-permute-done | bytes 262176 | tf_op jit(solution)/shard_map/ppermute | solution.py:36
  41.5 4.1 %collective-permute-start.1 = (bf16[4,256,128]{2,1,0:T(8,128)(2,1)S(1)}, bf16[4,256,128]{2,1,0:T(8,128)(2,1)S(1)}, u32[]{:S(2)}, u32[]{:S(2)}) collective-permute-start(bf16[4,256,128]{2,1,0:T(8,128)(2,1)S(1)} %collective-permute-done.k_own), channel_id=1, source_target_pairs={{0,2},{1,3},{2,4},{3,5},{4,6},{5,7},{6,8},{7,9},{8,10},{9,11},{10,... | collective-permute-start | bytes 786440 | tf_op jit(solution)/shard_map/ppermute | solution.py:36
  45.6 1.5 %collective-permute-done.3.k_other = bf16[4,256,128]{2,1,0:T(8,128)(2,1)S(1)} collective-permute-done((bf16[4,256,128]{2,1,0:T(8,128)(2,1)S(1)}, bf16[4,256,128]{2,1,0:T(8,128)(2,1)S(1)}, u32[]{:S(2)}, u32[]{:S(2)}) %collective-permute-start.3) | collective-permute-done | bytes 262176 | tf_op jit(solution)/shard_map/ppermute | solution.py:36
  47.1 4.1 %collective-permute-start.4 = (bf16[4,256,128]{2,1,0:T(8,128)(2,1)S(1)}, bf16[4,256,128]{2,1,0:T(8,128)(2,1)S(1)}, u32[]{:S(2)}, u32[]{:S(2)}) collective-permute-start(bf16[4,256,128]{2,1,0:T(8,128)(2,1)S(1)} %collective-permute-done.3.k_other), channel_id=1, source_target_pairs={{0,2},{1,3},{2,4},{3,5},{4,6},{5,7},{6,8},{7,9},{8,10},{9,11},{10,... | collective-permute-start | bytes 786440 | tf_op jit(solution)/shard_map/ppermute | solution.py:36
  51.2 4.8 %shard_map.61 = (bf16[4,4,256,512]{3,2,1,0:T(8,128)(2,1)}, f32[4,4,512]{2,1,0:T(4,128)S(1)}, f32[8,512]{1,0:T(8,128)S(1)}, f32[8,512]{1,0:T(8,128)S(1)}) custom-call(s32[1,8]{1,0:T(1,128)S(1)} %copy-done, s32[2]{0:T(128)S(1)} %pad_add_fusion.spot_ref, f32[6,256,128]{2,1,0:T(8,128)S(1)} %get-tuple-element.18.cos_ref, ...), custom_call_target="tpu_custom_call" | custom-call | flops 6000000 | tf_op jit(solution)/shard_map/pallas_call | solution.py:349
  56.1 7.9 %collective-permute-done.1.k_own = bf16[4,256,128]{2,1,0:T(8,128)(2,1)S(1)} collective-permute-done((bf16[4,256,128]{2,1,0:T(8,128)(2,1)S(1)}, bf16[4,256,128]{2,1,0:T(8,128)(2,1)S(1)}, u32[]{:S(2)}, u32[]{:S(2)}) %collective-permute-start.1) | collective-permute-done | bytes 262176 | tf_op jit(solution)/shard_map/ppermute | solution.py:36
  64.0 5.6 %collective-permute-done.4.k_other = bf16[4,256,128]{2,1,0:T(8,128)(2,1)S(1)} collective-permute-done((bf16[4,256,128]{2,1,0:T(8,128)(2,1)S(1)}, bf16[4,256,128]{2,1,0:T(8,128)(2,1)S(1)}, u32[]{:S(2)}, u32[]{:S(2)}) %collective-permute-start.4) | collective-permute-done | bytes 262176 | tf_op jit(solution)/shard_map/ppermute | solution.py:36
  69.6 4.3 %shard_map.62 = (bf16[3,4,256,512]{3,2,1,0:T(8,128)(2,1)}, f32[3,4,512]{2,1,0:T(4,128)S(1)}, f32[8,512]{1,0:T(8,128)S(1)}, f32[16,128]{1,0:T(8,128)S(1)}) custom-call(s32[1,8]{1,0:T(1,128)S(1)} %copy-done, s32[2]{0:T(128)S(1)} %pad_add_fusion.spot_ref, f32[6,256,128]{2,1,0:T(8,128)S(1)} %get-tuple-element.18.cos_ref, ...), custom_call_target="tpu_custom_call" | custom-call | flops 6000000 | tf_op jit(solution)/shard_map/pallas_call | solution.py:349
  73.9 4.5 %shard_map.63.near_ref = f32[2,4,128,512]{3,2,1,0:T(8,128)S(1)} custom-call(s32[2]{0:T(128)S(1)} %pad_add_fusion.spot_ref, f32[8,512]{1,0:T(8,128)S(1)} %get-tuple-element.25.level_ref, bf16[3,4,256,512]{3,2,1,0:T(8,128)(2,1)} %get-tuple-element.29.weight_0, f32[3,4,512]{2,1,0:T(4,128)S(1)} %get-tuple-element.30.mark_0, ...), custom_call_target="tpu_custom_call" | custom-call | flops 3000000 | tf_op jit(solution)/shard_map/pallas_call | solution.py:349
  78.4 0.0 collective-permute-done.7.v2_ref
  78.4 2.6 %shard_map.65 = bf16[8,256,128]{2,1,0:T(8,128)(2,1)S(1)} custom-call(s32[2]{0:T(128)S(1)} %pad_add_fusion.spot_ref, f32[8,512]{1,0:T(8,128)S(1)} %get-tuple-element.25.level_ref, bf16[3,4,256,512]{3,2,1,0:T(8,128)(2,1)} %get-tuple-element.26.weight_2, f32[3,4,512]{2,1,0:T(4,128)S(1)} %get-tuple-element.27.mark_2, ...), custom_call_target="tpu_custom_call" | custom-call | flops 3000000 | tf_op jit(solution)/shard_map/pallas_call | solution.py:349
  81.1 3.0 %collective-permute-start.8 = (bf16[8,256,128]{2,1,0:T(8,128)(2,1)S(1)}, bf16[8,256,128]{2,1,0:T(8,128)(2,1)}, u32[]{:S(2)}, u32[]{:S(2)}) collective-permute-start(bf16[8,256,128]{2,1,0:T(8,128)(2,1)S(1)} %shard_map.65), channel_id=1, source_target_pairs={{0,1},{1,0},{2,3},{3,2},{4,5},{5,4},{6,7},{7,6},{8,9},{9,8},{10,11... | collective-permute-start | bytes 1572872 | tf_op jit(solution)/shard_map/ppermute | solution.py:40
  84.0 15.9 %all_to_all.15 = f32[16,1,128]{2,1,0:T(1,128)S(1)} all-to-all(f32[16,1,128]{2,1,0:T(1,128)S(1)} %bitcast.36), channel_id=1, replica_groups=mesh['dp_0'=8,'dp_1'=2,'seq_0'=2,'seq_1'=8,'seq_2'=2] {'seq_1','seq_2'}, dimensions={0} | all-to-all | bytes 16384 | tf_op jit(solution)/shard_map/all_to_all | solution.py:442
  100.0 18.1 %all_to_all.16 = f32[32,1,128]{2,1,0:T(1,128)S(1)} all-to-all(f32[32,1,128]{2,1,0:T(1,128)S(1)} %broadcast_in_dim.17), channel_id=1, replica_groups=mesh['dp_0'=8,'dp_1'=2,'seq_0'=2,'seq_1'=8,'seq_2'=2] {'dp_0','dp_1','se..., dimensions={0} | all-to-all | bytes 32768 | tf_op jit(solution)/shard_map/all_to_all | solution.py:446
  118.2 2.6 %shard_map.64 = bf16[8,256,128]{2,1,0:T(8,128)(2,1)S(1)} custom-call(s32[2]{0:T(128)S(1)} %pad_add_fusion.spot_ref, f32[8,512]{1,0:T(8,128)S(1)} %get-tuple-element.25.level_ref, bf16[3,4,256,512]{3,2,1,0:T(8,128)(2,1)} %get-tuple-element.26.weight_2, f32[3,4,512]{2,1,0:T(4,128)S(1)} %get-tuple-element.27.mark_2, ...), custom_call_target="tpu_custom_call" | custom-call | flops 3000000 | tf_op jit(solution)/shard_map/pallas_call | solution.py:349
  120.8 0.0 collective-permute-done.8
  120.8 1.1 broadcast_select_fusion.1
  121.9 0.1 maximum_bitcast_fusion
  122.0 1.6 %copy.25 = bf16[1,256,16,128]{3,2,1,0:T(8,128)(2,1)} copy(bf16[1,256,16,128]{3,1,2,0:T(8,128)(2,1)S(1)} %maximum_bitcast_fusion) | data formatting | bytes 2097152
  (5 shorter events, 0.1 us)
Async XLA Ops:
  3.2 13.8 %copy-start = (s32[1,8]{1,0:T(1,128)S(1)}, s32[1,8]{1,0:T(1,128)}, u32[]{:S(2)}) copy-start(s32[1,8]{1,0:T(1,128)} %lengths_ref.7) | copy-start | bytes 100
  4.3 14.4 %collective-permute-start.5 = (bf16[12,256,128]{2,1,0:T(8,128)(2,1)}, bf16[12,256,128]{2,1,0:T(8,128)(2,1)S(1)}, u32[]{:S(2)}, u32[]{:S(2)}) collective-permute-start(bf16[12,256,128]{2,1,0:T(8,128)(2,1)} %pad_maximum_fusion), channel_id=1, source_target_pairs={{0,1},{1,0},{2,3},{3,2},{4,5},{5,4},{6,7},{7,6},{8,9},{9,8},{10,11... | collective-permute-start | bytes 2359304 | tf_op jit(solution)/shard_map/ppermute | solution.py:40
  14.9 3.8 %collective-permute-start.2 = (bf16[4,256,128]{2,1,0:T(8,128)(2,1)}, bf16[4,256,128]{2,1,0:T(8,128)(2,1)S(1)}, u32[]{:S(2)}, u32[]{:S(2)}) collective-permute-start(bf16[4,256,128]{2,1,0:T(8,128)(2,1)} %get-tuple-element.44), channel_id=1, source_target_pairs={{0,1},{1,0},{2,3},{3,2},{4,5},{5,4},{6,7},{7,6},{8,9},{9,8},{10,11... | collective-permute-start | bytes 786440 | tf_op jit(solution)/shard_map/ppermute | solution.py:40
  23.5 12.3 %collective-permute-start.6 = (bf16[8,256,128]{2,1,0:T(8,128)(2,1)S(1)}, bf16[8,256,128]{2,1,0:T(8,128)(2,1)S(1)}, u32[]{:S(2)}, u32[]{:S(2)}) collective-permute-start(bf16[8,256,128]{2,1,0:T(8,128)(2,1)S(1)} %get-tuple-element.28.v0_ref), channel_id=1, source_target_pairs={{0,2},{1,3},{2,4},{3,5},{4,6},{5,7},{6,8},{7,9},{8,10},{9,11},{10,... | collective-permute-start | bytes 1572872 | tf_op jit(solution)/shard_map/ppermute | solution.py:36
  24.9 16.6 %collective-permute-start = (bf16[4,256,128]{2,1,0:T(8,128)(2,1)S(1)}, bf16[4,256,128]{2,1,0:T(8,128)(2,1)S(1)}, u32[]{:S(2)}, u32[]{:S(2)}) collective-permute-start(bf16[4,256,128]{2,1,0:T(8,128)(2,1)S(1)} %get-tuple-element.45), channel_id=1, source_target_pairs={{0,2},{1,3},{2,4},{3,5},{4,6},{5,7},{6,8},{7,9},{8,10},{9,11},{10,... | collective-permute-start | bytes 786440 | tf_op jit(solution)/shard_map/ppermute | solution.py:36
  26.2 20.9 %collective-permute-start.3 = (bf16[4,256,128]{2,1,0:T(8,128)(2,1)S(1)}, bf16[4,256,128]{2,1,0:T(8,128)(2,1)S(1)}, u32[]{:S(2)}, u32[]{:S(2)}) collective-permute-start(bf16[4,256,128]{2,1,0:T(8,128)(2,1)S(1)} %collective-permute-done.2.k_other), channel_id=1, source_target_pairs={{0,2},{1,3},{2,4},{3,5},{4,6},{5,7},{6,8},{7,9},{8,10},{9,11},{10,... | collective-permute-start | bytes 786440 | tf_op jit(solution)/shard_map/ppermute | solution.py:36
  35.9 42.5 %collective-permute-start.7 = (bf16[8,256,128]{2,1,0:T(8,128)(2,1)S(1)}, bf16[8,256,128]{2,1,0:T(8,128)(2,1)S(1)}, u32[]{:S(2)}, u32[]{:S(2)}) collective-permute-start(bf16[8,256,128]{2,1,0:T(8,128)(2,1)S(1)} %collective-permute-done.6.v1_ref), channel_id=1, source_target_pairs={{0,2},{1,3},{2,4},{3,5},{4,6},{5,7},{6,8},{7,9},{8,10},{9,11},{10,... | collective-permute-start | bytes 1572872 | tf_op jit(solution)/shard_map/ppermute | solution.py:36
  41.5 22.5 %collective-permute-start.1 = (bf16[4,256,128]{2,1,0:T(8,128)(2,1)S(1)}, bf16[4,256,128]{2,1,0:T(8,128)(2,1)S(1)}, u32[]{:S(2)}, u32[]{:S(2)}) collective-permute-start(bf16[4,256,128]{2,1,0:T(8,128)(2,1)S(1)} %collective-permute-done.k_own), channel_id=1, source_target_pairs={{0,2},{1,3},{2,4},{3,5},{4,6},{5,7},{6,8},{7,9},{8,10},{9,11},{10,... | collective-permute-start | bytes 786440 | tf_op jit(solution)/shard_map/ppermute | solution.py:36
  47.1 22.5 %collective-permute-start.4 = (bf16[4,256,128]{2,1,0:T(8,128)(2,1)S(1)}, bf16[4,256,128]{2,1,0:T(8,128)(2,1)S(1)}, u32[]{:S(2)}, u32[]{:S(2)}) collective-permute-start(bf16[4,256,128]{2,1,0:T(8,128)(2,1)S(1)} %collective-permute-done.3.k_other), channel_id=1, source_target_pairs={{0,2},{1,3},{2,4},{3,5},{4,6},{5,7},{6,8},{7,9},{8,10},{9,11},{10,... | collective-permute-start | bytes 786440 | tf_op jit(solution)/shard_map/ppermute | solution.py:36
  81.1 39.8 %collective-permute-start.8 = (bf16[8,256,128]{2,1,0:T(8,128)(2,1)S(1)}, bf16[8,256,128]{2,1,0:T(8,128)(2,1)}, u32[]{:S(2)}, u32[]{:S(2)}) collective-permute-start(bf16[8,256,128]{2,1,0:T(8,128)(2,1)S(1)} %shard_map.65), channel_id=1, source_target_pairs={{0,1},{1,0},{2,3},{3,2},{4,5},{5,4},{6,7},{7,6},{8,9},{9,8},{10,11... | collective-permute-start | bytes 1572872 | tf_op jit(solution)/shard_map/ppermute | solution.py:40

commit v4 on v3

--- a/solution.py
+++ b/solution.py
@@ -281,10 +281,11 @@
 
 
 def near_kernel(
-    spot_ref, level_ref, weight_0, mark_0, weight_1, mark_1, v0_ref, v1_ref, sum_ref,
+    spot_ref, level_ref, weight_0, mark_0, weight_1, mark_1, v0_ref, v1_ref, own_ref, other_ref,
     held_0, held_1, ready_0, ready_1,
 ):
-    heads = sum_ref.shape[1]
+    heads = own_ref.shape[0]
+    sums = (own_ref, other_ref)
     copies_0 = fetch(weight_0, held_0, ready_0)
     copies_1 = fetch(weight_1, held_1, ready_1)
     for copy in (
@@ -296,7 +297,7 @@
             copy.wait()
         for head in range(heads):
             part = functools.partial(weighed, q_side=q_side, head=head, heads=heads)
-            sum_ref[q_side, head] = (
+            sums[q_side][head] = (
                 part(held_0, mark_0, level_ref, v0_ref[q_side * heads + head], slot=q_side)
                 + part(held_1, mark_1, level_ref, v1_ref[head], slot=2 * q_side)
                 + part(held_1, mark_1, level_ref, v1_ref[heads + head], slot=2 * q_side + 1)
@@ -305,7 +306,7 @@
 
     def cross(q_side, k_side, slot):
         for head in range(heads):
-            sum_ref[q_side, head] += weighed(
+            sums[q_side][head] += weighed(
                 held_0, mark_0, level_ref, v0_ref[k_side * heads + head], q_side, head, heads, slot
             )
 
@@ -314,34 +315,48 @@
 
 
 def far_kernel(
-    side, spot_ref, level_ref, weight_2, mark_2, v2_ref, near_ref, out_ref,
-    sum_ref, held, ready,
+    side, spot_ref, level_ref, weight_2, mark_2, v2_ref, near_ref, out_ref, sum_ref, held, ready
 ):
-    heads = near_ref.shape[1]
+    heads, rows = near_ref.shape[0], out_ref.shape[1]
     copies = fetch(weight_2, held, ready)
-    cross_here = [entry for entry in single_slots(2, spot_ref[1])[2:] if entry[0] == side]
-    for slot in (2, side):
-        copies(slot).start()
-    sum_ref[...] = near_ref[side]
-    copies(2).wait()
-
-    def cross(k_side, slot):
-        for head in range(heads):
-            sum_ref[head] += weighed(
-                held, mark_2, level_ref, v2_ref[k_side * heads + head], side, head, heads, slot
-            )
-
-    for _, k_side, slot, condition in cross_here:
-        guarded(condition, functools.partial(cross, k_side, slot))
-    rows = out_ref.shape[1]
+    crossed = spot_ref[1] == side
+    copies(side).start()
+
+    @pl.when(crossed)
+    def _():
+        copies(2).start()
+
     copies(side).wait()
-    for head in range(heads):
-        block = sum_ref[head] + weighed(
+
+    def summed(head):
+        return near_ref[head] + weighed(
             held, mark_2, level_ref, v2_ref[side * heads + head], side, head, heads, side
         )
+
+    def write(head, block):
         turned = jnp.transpose(block, (1, 0)).astype(jnp.bfloat16)
         out_ref[head * 2] = turned[:rows]
         out_ref[head * 2 + 1] = turned[rows:]
+
+    @pl.when(crossed)
+    def _():
+        for head in range(heads):
+            sum_ref[head] = summed(head)
+        copies(2).wait()
+        for head in range(heads):
+            write(
+                head,
+                sum_ref[head]
+                + weighed(
+                    held, mark_2, level_ref, v2_ref[(1 - side) * heads + head],
+                    side, head, heads, 2,
+                ),
+            )
+
+    @pl.when(jnp.logical_not(crossed))
+    def _():
+        for head in range(heads):
+            write(head, summed(head))
 
 
 def call(kernel, out_shape, scalars, count, flops, scratch=(), far_in=(), far_out=()):
@@ -451,9 +466,9 @@
         pltpu.with_memory_space_constraint(array, pltpu.HBM)
         for array in (weight_0, weight_1, weight_2)
     )
-    sum_shape = shape((CORES, heads, width, members * rows), f32)
-    (near,) = call(
-        near_kernel, (sum_shape,), 1, 8, NEAR_FLOPS,
+    sum_shape = shape((heads, width, members * rows), f32)
+    near = call(
+        near_kernel, (sum_shape, sum_shape), 1, 8, NEAR_FLOPS,
         (*staged(3)[1:2], *staged(4)[1:2], *staged(3)[2:], *staged(4)[2:]),
         far_in=(2, 4),
     )(spot, level, weight_0, mark_0, weight_1, mark_1, v0, v1)
@@ -461,9 +476,9 @@
     own, other = (
         call(
             functools.partial(far_kernel, side), (out_shape,), 1, 6, NEAR_FLOPS,
-            (pltpu.VMEM(sum_shape.shape[1:], f32), *staged(3)[1:]),
+            (pltpu.VMEM(sum_shape.shape, f32), *staged(3)[1:]),
             far_in=(2,),
-        )(spot, level, weight_2, mark_2, v2, near)[0]
+        )(spot, level, weight_2, mark_2, v2, near[side])[0]
         for side in range(2)
     )
     partner = swapped(other)

time: 125 us -> 124 us (level)
  the two profiles are of different devices: /device:TPU:1 before, /device:TPU:2 now
where the time goes in v4:
time: 124 us; the launch traced here: 123 us
  blocking collectives  37.9 us (31%)
  starting transfers between devices  32.3 us (26%)
  Pallas kernels  24.9 us (20%)
  waiting for transfers between devices  18.4 us (15%)
  local copies, waits for them, and re-layouts  5.39 us (4%)
  other arithmetic  2.17 us (2%)
  between operations  2.05 us (2%)
    ppermute x6, starting transfers between devices, up_chip(): lax.ppermute(block, SEQ, [(i, i + step) for i in range(count - step)])  26 us
    pallas_call x7, Pallas kernels, run(): pl.pallas_call(kernel, out_shape=out_shape, in_specs=[SMEM] * scalars + [...  24.9 us
    all_to_all x1, blocking collectives, device_part(): squares = lax.all_to_all(squares, ('seq_1', 'seq_2'), 0, 0)  19.2 us
    all_to_all x1, blocking collectives, device_part(): squares = lax.all_to_all(squares, across, 0, 0)  18.6 us
    ppermute x6, waiting for transfers between devices, up_chip(): lax.ppermute(block, SEQ, [(i, i + step) for i in range(count - step)])  18.4 us
    ppermute x3, starting transfers between devices, swapped(): return lax.ppermute(block, 'seq_2', [(0, 1), (1, 0)])  6.22 us
    unnamed x6, local copies, waits for them, and re-layouts  5.38 us
  transfers between devices with their start and end apart: 9, of which 5 were waited for; matrix products, arithmetic and copies ran while one was open for 2% of the time, Pallas kernels for 15%

profile of v4, /device:TPU:2, one launch (start us, length us, event | category | flops | bytes accessed | tf_op | source)
XLA Modules:
  0.0 123.1 jit_solution(8012404843699449567)
XLA Ops:
  0.6 1.5 %copy.29 = bf16[1,256,16,128]{3,1,2,0:T(8,128)(2,1)S(1)} copy(bf16[1,256,16,128]{3,2,1,0:T(8,128)(2,1)} %param.4) | data formatting | bytes 2097152 | tf_op args[0]
  2.1 1.1 copy.30
  3.2 0.0 copy-start
  3.3 0.1 slice_select_fusion
  3.4 0.9 pad_maximum_fusion
  4.3 1.9 %collective-permute-start.5 = (bf16[12,256,128]{2,1,0:T(8,128)(2,1)}, bf16[12,256,128]{2,1,0:T(8,128)(2,1)S(1)}, u32[]{:S(2)}, u32[]{:S(2)}) collective-permute-start(bf16[12,256,128]{2,1,0:T(8,128)(2,1)} %pad_maximum_fusion), channel_id=1, source_target_pairs={{0,1},{1,0},{2,3},{3,2},{4,5},{5,4},{6,7},{7,6},{8,9},{9,8},{10,11... | collective-permute-start | bytes 2359304 | tf_op jit(solution)/shard_map/ppermute | solution.py:40
  6.2 1.1 copy.31
  7.4 0.7 broadcast_select_fusion.2
  8.1 2.4 %collective-permute-start.2 = (bf16[4,256,128]{2,1,0:T(8,128)(2,1)}, bf16[4,256,128]{2,1,0:T(8,128)(2,1)S(1)}, u32[]{:S(2)}, u32[]{:S(2)}) collective-permute-start(bf16[4,256,128]{2,1,0:T(8,128)(2,1)} %get-tuple-element.48), channel_id=1, source_target_pairs={{0,1},{1,0},{2,3},{3,2},{4,5},{5,4},{6,7},{7,6},{8,9},{9,8},{10,11... | collective-permute-start | bytes 786440 | tf_op jit(solution)/shard_map/ppermute | solution.py:40
  10.5 0.1 maximum_bitcast_fusion.1.frequency_ref
  10.6 0.1 pad_add_fusion.spot_ref
  10.7 0.0 copy-done
  10.7 1.7 %shard_map.59 = (f32[6,256,128]{2,1,0:T(8,128)S(1)}, f32[6,256,128]{2,1,0:T(8,128)S(1)}) custom-call(s32[1,8]{1,0:T(1,128)S(1)} %copy-done, s32[2]{0:T(128)S(1)} %pad_add_fusion.spot_ref, f32[1,128]{1,0:T(1,128)S(1)} %maximum_bitcast_fusion.1.frequency_ref), custom_call_target="tpu_custom_call" | custom-call | flops 4000000 | tf_op jit(solution)/shard_map/pallas_call | solution.py:364
  12.4 0.0 collective-permute-done.2.k_other
  12.4 0.0 collective-permute-done.5.got_ref
  12.4 4.7 %shard_map.60 = (bf16[2,4,512,128]{3,2,1,0:T(8,128)(2,1)S(1)}, bf16[8,256,128]{2,1,0:T(8,128)(2,1)S(1)}, bf16[3,4,256,512]{3,2,1,0:T(8,128)(2,1)}, f32[3,4,512]{...) custom-call(s32[1,8]{1,0:T(1,128)S(1)} %copy-done, s32[2]{0:T(128)S(1)} %pad_add_fusion.spot_ref, ...), custom_call_target="tpu_custom_call" | custom-call | flops 6000000 | tf_op jit(solution)/shard_map/pallas_call | solution.py:364
  17.1 4.3 %collective-permute-start.6 = (bf16[8,256,128]{2,1,0:T(8,128)(2,1)S(1)}, bf16[8,256,128]{2,1,0:T(8,128)(2,1)S(1)}, u32[]{:S(2)}, u32[]{:S(2)}) collective-permute-start(bf16[8,256,128]{2,1,0:T(8,128)(2,1)S(1)} %get-tuple-element.30.v0_ref), channel_id=1, source_target_pairs={{0,2},{1,3},{2,4},{3,5},{4,6},{5,7},{6,8},{7,9},{8,10},{9,11},{10,... | collective-permute-start | bytes 1572872 | tf_op jit(solution)/shard_map/ppermute | solution.py:36
  21.4 4.3 %collective-permute-start = (bf16[4,256,128]{2,1,0:T(8,128)(2,1)S(1)}, bf16[4,256,128]{2,1,0:T(8,128)(2,1)S(1)}, u32[]{:S(2)}, u32[]{:S(2)}) collective-permute-start(bf16[4,256,128]{2,1,0:T(8,128)(2,1)S(1)} %get-tuple-element.49), channel_id=1, source_target_pairs={{0,2},{1,3},{2,4},{3,5},{4,6},{5,7},{6,8},{7,9},{8,10},{9,11},{10,... | collective-permute-start | bytes 786440 | tf_op jit(solution)/shard_map/ppermute | solution.py:36
  25.7 4.3 %collective-permute-start.3 = (bf16[4,256,128]{2,1,0:T(8,128)(2,1)S(1)}, bf16[4,256,128]{2,1,0:T(8,128)(2,1)S(1)}, u32[]{:S(2)}, u32[]{:S(2)}) collective-permute-start(bf16[4,256,128]{2,1,0:T(8,128)(2,1)S(1)} %collective-permute-done.2.k_other), channel_id=1, source_target_pairs={{0,2},{1,3},{2,4},{3,5},{4,6},{5,7},{6,8},{7,9},{8,10},{9,11},{10,... | collective-permute-start | bytes 786440 | tf_op jit(solution)/shard_map/ppermute | solution.py:36
  30.0 3.7 %collective-permute-done.6.v1_ref = bf16[8,256,128]{2,1,0:T(8,128)(2,1)S(1)} collective-permute-done((bf16[8,256,128]{2,1,0:T(8,128)(2,1)S(1)}, bf16[8,256,128]{2,1,0:T(8,128)(2,1)S(1)}, u32[]{:S(2)}, u32[]{:S(2)}) %collective-permute-start.6) | collective-permute-done | bytes 524320 | tf_op jit(solution)/shard_map/ppermute | solution.py:36
  33.7 4.4 %collective-permute-start.7 = (bf16[8,256,128]{2,1,0:T(8,128)(2,1)S(1)}, bf16[8,256,128]{2,1,0:T(8,128)(2,1)S(1)}, u32[]{:S(2)}, u32[]{:S(2)}) collective-permute-start(bf16[8,256,128]{2,1,0:T(8,128)(2,1)S(1)} %collective-permute-done.6.v1_ref), channel_id=1, source_target_pairs={{0,2},{1,3},{2,4},{3,5},{4,6},{5,7},{6,8},{7,9},{8,10},{9,11},{10,... | collective-permute-start | bytes 1572872 | tf_op jit(solution)/shard_map/ppermute | solution.py:36
  38.1 1.2 collective-permute-done.k_own
  39.3 4.4 %collective-permute-start.1 = (bf16[4,256,128]{2,1,0:T(8,128)(2,1)S(1)}, bf16[4,256,128]{2,1,0:T(8,128)(2,1)S(1)}, u32[]{:S(2)}, u32[]{:S(2)}) collective-permute-start(bf16[4,256,128]{2,1,0:T(8,128)(2,1)S(1)} %collective-permute-done.k_own), channel_id=1, source_target_pairs={{0,2},{1,3},{2,4},{3,5},{4,6},{5,7},{6,8},{7,9},{8,10},{9,11},{10,... | collective-permute-start | bytes 786440 | tf_op jit(solution)/shard_map/ppermute | solution.py:36
  43.7 1.2 collective-permute-done.3.k_other
  44.9 4.4 %collective-permute-start.4 = (bf16[4,256,128]{2,1,0:T(8,128)(2,1)S(1)}, bf16[4,256,128]{2,1,0:T(8,128)(2,1)S(1)}, u32[]{:S(2)}, u32[]{:S(2)}) collective-permute-start(bf16[4,256,128]{2,1,0:T(8,128)(2,1)S(1)} %collective-permute-done.3.k_other), channel_id=1, source_target_pairs={{0,2},{1,3},{2,4},{3,5},{4,6},{5,7},{6,8},{7,9},{8,10},{9,11},{10,... | collective-permute-start | bytes 786440 | tf_op jit(solution)/shard_map/ppermute | solution.py:36
  49.3 4.8 %shard_map.61 = (bf16[4,4,256,512]{3,2,1,0:T(8,128)(2,1)}, f32[4,4,512]{2,1,0:T(4,128)S(1)}, f32[8,512]{1,0:T(8,128)S(1)}, f32[8,512]{1,0:T(8,128)S(1)}) custom-call(s32[1,8]{1,0:T(1,128)S(1)} %copy-done, s32[2]{0:T(128)S(1)} %pad_add_fusion.spot_ref, f32[6,256,128]{2,1,0:T(8,128)S(1)} %get-tuple-element.20.cos_ref, ...), custom_call_target="tpu_custom_call" | custom-call | flops 6000000 | tf_op jit(solution)/shard_map/pallas_call | solution.py:364
  54.2 7.6 %collective-permute-done.1.k_own = bf16[4,256,128]{2,1,0:T(8,128)(2,1)S(1)} collective-permute-done((bf16[4,256,128]{2,1,0:T(8,128)(2,1)S(1)}, bf16[4,256,128]{2,1,0:T(8,128)(2,1)S(1)}, u32[]{:S(2)}, u32[]{:S(2)}) %collective-permute-start.1) | collective-permute-done | bytes 262176 | tf_op jit(solution)/shard_map/ppermute | solution.py:36
  61.8 4.7 %collective-permute-done.4.k_other = bf16[4,256,128]{2,1,0:T(8,128)(2,1)S(1)} collective-permute-done((bf16[4,256,128]{2,1,0:T(8,128)(2,1)S(1)}, bf16[4,256,128]{2,1,0:T(8,128)(2,1)S(1)}, u32[]{:S(2)}, u32[]{:S(2)}) %collective-permute-start.4) | collective-permute-done | bytes 262176 | tf_op jit(solution)/shard_map/ppermute | solution.py:36
  66.5 4.2 %shard_map.62 = (bf16[3,4,256,512]{3,2,1,0:T(8,128)(2,1)}, f32[3,4,512]{2,1,0:T(4,128)S(1)}, f32[8,512]{1,0:T(8,128)S(1)}, f32[16,128]{1,0:T(8,128)S(1)}) custom-call(s32[1,8]{1,0:T(1,128)S(1)} %copy-done, s32[2]{0:T(128)S(1)} %pad_add_fusion.spot_ref, f32[6,256,128]{2,1,0:T(8,128)S(1)} %get-tuple-element.20.cos_ref, ...), custom_call_target="tpu_custom_call" | custom-call | flops 6000000 | tf_op jit(solution)/shard_map/pallas_call | solution.py:364
  70.7 4.5 %shard_map.63 = (f32[4,128,512]{2,1,0:T(8,128)S(1)}, f32[4,128,512]{2,1,0:T(8,128)S(1)}) custom-call(s32[2]{0:T(128)S(1)} %pad_add_fusion.spot_ref, f32[8,512]{1,0:T(8,128)S(1)} %get-tuple-element.27.level_ref, bf16[3,4,256,512]{3,2,1,0:T(8,128)(2,1)} %get-tuple-element.31.weight_0, f32[3,4,512]{2,1,0:T(4,128)S(1)} %get-tuple-element.32.mark_0, ...), custom_call_target="tpu_custom_call" | custom-call | flops 3000000 | tf_op jit(solution)/shard_map/pallas_call | solution.py:364
  75.3 0.0 collective-permute-done.7.v2_ref
  75.3 2.3 %shard_map.65 = bf16[8,256,128]{2,1,0:T(8,128)(2,1)S(1)} custom-call(s32[2]{0:T(128)S(1)} %pad_add_fusion.spot_ref, f32[8,512]{1,0:T(8,128)S(1)} %get-tuple-element.27.level_ref, bf16[3,4,256,512]{3,2,1,0:T(8,128)(2,1)} %get-tuple-element.28.weight_2, f32[3,4,512]{2,1,0:T(4,128)S(1)} %get-tuple-element.29.mark_2, ...), custom_call_target="tpu_custom_call" | custom-call | flops 3000000 | tf_op jit(solution)/shard_map/pallas_call | solution.py:364
  77.6 1.9 %collective-permute-start.8 = (bf16[8,256,128]{2,1,0:T(8,128)(2,1)S(1)}, bf16[8,256,128]{2,1,0:T(8,128)(2,1)S(1)}, u32[]{:S(2)}, u32[]{:S(2)}) collective-permute-start(bf16[8,256,128]{2,1,0:T(8,128)(2,1)S(1)} %shard_map.65), channel_id=1, source_target_pairs={{0,1},{1,0},{2,3},{3,2},{4,5},{5,4},{6,7},{7,6},{8,9},{9,8},{10,11... | collective-permute-start | bytes 1572872 | tf_op jit(solution)/shard_map/ppermute | solution.py:40
  79.5 19.2 %all_to_all.15 = f32[16,1,128]{2,1,0:T(1,128)S(1)} all-to-all(f32[16,1,128]{2,1,0:T(1,128)S(1)} %bitcast.36), channel_id=1, replica_groups=mesh['dp_0'=8,'dp_1'=2,'seq_0'=2,'seq_1'=8,'seq_2'=2] {'seq_1','seq_2'}, dimensions={0} | all-to-all | bytes 16384 | tf_op jit(solution)/shard_map/all_to_all | solution.py:457
  98.8 18.6 %all_to_all.16 = f32[32,1,128]{2,1,0:T(1,128)S(1)} all-to-all(f32[32,1,128]{2,1,0:T(1,128)S(1)} %broadcast_in_dim.17), channel_id=1, replica_groups=mesh['dp_0'=8,'dp_1'=2,'seq_0'=2,'seq_1'=8,'seq_2'=2] {'dp_0','dp_1','se..., dimensions={0} | all-to-all | bytes 32768 | tf_op jit(solution)/shard_map/all_to_all | solution.py:461
  117.5 2.6 %shard_map.64 = bf16[8,256,128]{2,1,0:T(8,128)(2,1)S(1)} custom-call(s32[2]{0:T(128)S(1)} %pad_add_fusion.spot_ref, f32[8,512]{1,0:T(8,128)S(1)} %get-tuple-element.27.level_ref, bf16[3,4,256,512]{3,2,1,0:T(8,128)(2,1)} %get-tuple-element.28.weight_2, f32[3,4,512]{2,1,0:T(4,128)S(1)} %get-tuple-element.29.mark_2, ...), custom_call_target="tpu_custom_call" | custom-call | flops 3000000 | tf_op jit(solution)/shard_map/pallas_call | solution.py:364
  120.1 0.0 collective-permute-done.8
  120.1 0.1 broadcast_select_fusion.1
  120.2 0.1 maximum_bitcast_fusion
  120.3 1.6 %copy.25 = bf16[1,256,16,128]{3,2,1,0:T(8,128)(2,1)} copy(bf16[1,256,16,128]{3,1,2,0:T(8,128)(2,1)S(1)} %maximum_bitcast_fusion) | data formatting | bytes 2097152
  (5 shorter events, 0.1 us)
Async XLA Ops:
  3.2 7.4 %copy-start = (s32[1,8]{1,0:T(1,128)S(1)}, s32[1,8]{1,0:T(1,128)}, u32[]{:S(2)}) copy-start(s32[1,8]{1,0:T(1,128)} %lengths_ref.7) | copy-start | bytes 100
  4.3 8.1 %collective-permute-start.5 = (bf16[12,256,128]{2,1,0:T(8,128)(2,1)}, bf16[12,256,128]{2,1,0:T(8,128)(2,1)S(1)}, u32[]{:S(2)}, u32[]{:S(2)}) collective-permute-start(bf16[12,256,128]{2,1,0:T(8,128)(2,1)} %pad_maximum_fusion), channel_id=1, source_target_pairs={{0,1},{1,0},{2,3},{3,2},{4,5},{5,4},{6,7},{7,6},{8,9},{9,8},{10,11... | collective-permute-start | bytes 2359304 | tf_op jit(solution)/shard_map/ppermute | solution.py:40
  8.1 4.3 %collective-permute-start.2 = (bf16[4,256,128]{2,1,0:T(8,128)(2,1)}, bf16[4,256,128]{2,1,0:T(8,128)(2,1)S(1)}, u32[]{:S(2)}, u32[]{:S(2)}) collective-permute-start(bf16[4,256,128]{2,1,0:T(8,128)(2,1)} %get-tuple-element.48), channel_id=1, source_target_pairs={{0,1},{1,0},{2,3},{3,2},{4,5},{5,4},{6,7},{7,6},{8,9},{9,8},{10,11... | collective-permute-start | bytes 786440 | tf_op jit(solution)/shard_map/ppermute | solution.py:40
  17.1 16.6 %collective-permute-start.6 = (bf16[8,256,128]{2,1,0:T(8,128)(2,1)S(1)}, bf16[8,256,128]{2,1,0:T(8,128)(2,1)S(1)}, u32[]{:S(2)}, u32[]{:S(2)}) collective-permute-start(bf16[8,256,128]{2,1,0:T(8,128)(2,1)S(1)} %get-tuple-element.30.v0_ref), channel_id=1, source_target_pairs={{0,2},{1,3},{2,4},{3,5},{4,6},{5,7},{6,8},{7,9},{8,10},{9,11},{10,... | collective-permute-start | bytes 1572872 | tf_op jit(solution)/shard_map/ppermute | solution.py:36
  21.4 17.9 %collective-permute-start = (bf16[4,256,128]{2,1,0:T(8,128)(2,1)S(1)}, bf16[4,256,128]{2,1,0:T(8,128)(2,1)S(1)}, u32[]{:S(2)}, u32[]{:S(2)}) collective-permute-start(bf16[4,256,128]{2,1,0:T(8,128)(2,1)S(1)} %get-tuple-element.49), channel_id=1, source_target_pairs={{0,2},{1,3},{2,4},{3,5},{4,6},{5,7},{6,8},{7,9},{8,10},{9,11},{10,... | collective-permute-start | bytes 786440 | tf_op jit(solution)/shard_map/ppermute | solution.py:36
  25.7 19.2 %collective-permute-start.3 = (bf16[4,256,128]{2,1,0:T(8,128)(2,1)S(1)}, bf16[4,256,128]{2,1,0:T(8,128)(2,1)S(1)}, u32[]{:S(2)}, u32[]{:S(2)}) collective-permute-start(bf16[4,256,128]{2,1,0:T(8,128)(2,1)S(1)} %collective-permute-done.2.k_other), channel_id=1, source_target_pairs={{0,2},{1,3},{2,4},{3,5},{4,6},{5,7},{6,8},{7,9},{8,10},{9,11},{10,... | collective-permute-start | bytes 786440 | tf_op jit(solution)/shard_map/ppermute | solution.py:36
  33.7 41.6 %collective-permute-start.7 = (bf16[8,256,128]{2,1,0:T(8,128)(2,1)S(1)}, bf16[8,256,128]{2,1,0:T(8,128)(2,1)S(1)}, u32[]{:S(2)}, u32[]{:S(2)}) collective-permute-start(bf16[8,256,128]{2,1,0:T(8,128)(2,1)S(1)} %collective-permute-done.6.v1_ref), channel_id=1, source_target_pairs={{0,2},{1,3},{2,4},{3,5},{4,6},{5,7},{6,8},{7,9},{8,10},{9,11},{10,... | collective-permute-start | bytes 1572872 | tf_op jit(solution)/shard_map/ppermute | solution.py:36
  39.3 22.5 %collective-permute-start.1 = (bf16[4,256,128]{2,1,0:T(8,128)(2,1)S(1)}, bf16[4,256,128]{2,1,0:T(8,128)(2,1)S(1)}, u32[]{:S(2)}, u32[]{:S(2)}) collective-permute-start(bf16[4,256,128]{2,1,0:T(8,128)(2,1)S(1)} %collective-permute-done.k_own), channel_id=1, source_target_pairs={{0,2},{1,3},{2,4},{3,5},{4,6},{5,7},{6,8},{7,9},{8,10},{9,11},{10,... | collective-permute-start | bytes 786440 | tf_op jit(solution)/shard_map/ppermute | solution.py:36
  44.9 21.5 %collective-permute-start.4 = (bf16[4,256,128]{2,1,0:T(8,128)(2,1)S(1)}, bf16[4,256,128]{2,1,0:T(8,128)(2,1)S(1)}, u32[]{:S(2)}, u32[]{:S(2)}) collective-permute-start(bf16[4,256,128]{2,1,0:T(8,128)(2,1)S(1)} %collective-permute-done.3.k_other), channel_id=1, source_target_pairs={{0,2},{1,3},{2,4},{3,5},{4,6},{5,7},{6,8},{7,9},{8,10},{9,11},{10,... | collective-permute-start | bytes 786440 | tf_op jit(solution)/shard_map/ppermute | solution.py:36
  77.6 42.5 %collective-permute-start.8 = (bf16[8,256,128]{2,1,0:T(8,128)(2,1)S(1)}, bf16[8,256,128]{2,1,0:T(8,128)(2,1)S(1)}, u32[]{:S(2)}, u32[]{:S(2)}) collective-permute-start(bf16[8,256,128]{2,1,0:T(8,128)(2,1)S(1)} %shard_map.65), channel_id=1, source_target_pairs={{0,1},{1,0},{2,3},{3,2},{4,5},{5,4},{6,7},{7,6},{8,9},{9,8},{10,11... | collective-permute-start | bytes 1572872 | tf_op jit(solution)/shard_map/ppermute | solution.py:40

commit v5 on v4

--- a/solution.py
+++ b/solution.py
@@ -320,15 +320,23 @@
     heads, rows = near_ref.shape[0], out_ref.shape[1]
     copies = fetch(weight_2, held, ready)
     crossed = spot_ref[1] == side
-    copies(side).start()
+    lead, rest = pl.ds(0, 1), pl.ds(1, heads - 1)
+    firsts = [
+        pltpu.make_async_copy(
+            weight_2.at[side, part], held.at[side, part], ready.at[side, place]
+        )
+        for place, part in enumerate((lead, rest))
+    ]
+    for copy in firsts:
+        copy.start()
 
     @pl.when(crossed)
     def _():
         copies(2).start()
 
-    copies(side).wait()
-
     def summed(head):
+        if head < 2:
+            firsts[head].wait()
         return near_ref[head] + weighed(
             held, mark_2, level_ref, v2_ref[side * heads + head], side, head, heads, side
         )

time: 124 us -> 124 us (level)
  no operation moved by 1% of the time
where the time goes in v5:
time: 124 us; the launch traced here: 123 us
  blocking collectives  37.9 us (31%)
  starting transfers between devices  32.3 us (26%)
  Pallas kernels  24.9 us (20%)
  waiting for transfers between devices  18.4 us (15%)
  local copies, waits for them, and re-layouts  5.39 us (4%)
  other arithmetic  2.17 us (2%)
  between operations  2.05 us (2%)
    ppermute x6, starting transfers between devices, up_chip(): lax.ppermute(block, SEQ, [(i, i + step) for i in range(count - step)])  26 us
    pallas_call x7, Pallas kernels, run(): pl.pallas_call(kernel, out_shape=out_shape, in_specs=[SMEM] * scalars + [...  24.9 us
    all_to_all x1, blocking collectives, device_part(): squares = lax.all_to_all(squares, ('seq_1', 'seq_2'), 0, 0)  19.2 us
    all_to_all x1, blocking collectives, device_part(): squares = lax.all_to_all(squares, across, 0, 0)  18.6 us
    ppermute x6, waiting for transfers between devices, up_chip(): lax.ppermute(block, SEQ, [(i, i + step) for i in range(count - step)])  18.4 us
    ppermute x3, starting transfers between devices, swapped(): return lax.ppermute(block, 'seq_2', [(0, 1), (1, 0)])  6.22 us
    unnamed x6, local copies, waits for them, and re-layouts  5.38 us
  transfers between devices with their start and end apart: 9, of which 5 were waited for; matrix products, arithmetic and copies ran while one was open for 2% of the time, Pallas kernels for 15%

profile of v5, /device:TPU:2, one launch (start us, length us, event | category | flops | bytes accessed | tf_op | source)
XLA Modules:
  0.0 123.0 jit_solution(13073415524300261018)
XLA Ops:
  0.6 1.5 %copy.29 = bf16[1,256,16,128]{3,1,2,0:T(8,128)(2,1)S(1)} copy(bf16[1,256,16,128]{3,2,1,0:T(8,128)(2,1)} %param.4) | data formatting | bytes 2097152 | tf_op args[0]
  2.1 1.1 copy.30
  3.2 0.0 copy-start
  3.3 0.1 slice_select_fusion
  3.4 0.9 pad_maximum_fusion
  4.3 1.9 %collective-permute-start.5 = (bf16[12,256,128]{2,1,0:T(8,128)(2,1)}, bf16[12,256,128]{2,1,0:T(8,128)(2,1)S(1)}, u32[]{:S(2)}, u32[]{:S(2)}) collective-permute-start(bf16[12,256,128]{2,1,0:T(8,128)(2,1)} %pad_maximum_fusion), channel_id=1, source_target_pairs={{0,1},{1,0},{2,3},{3,2},{4,5},{5,4},{6,7},{7,6},{8,9},{9,8},{10,11... | collective-permute-start | bytes 2359304 | tf_op jit(solution)/shard_map/ppermute | solution.py:40
  6.2 1.1 copy.31
  7.4 0.7 broadcast_select_fusion.2
  8.1 2.4 %collective-permute-start.2 = (bf16[4,256,128]{2,1,0:T(8,128)(2,1)}, bf16[4,256,128]{2,1,0:T(8,128)(2,1)S(1)}, u32[]{:S(2)}, u32[]{:S(2)}) collective-permute-start(bf16[4,256,128]{2,1,0:T(8,128)(2,1)} %get-tuple-element.48), channel_id=1, source_target_pairs={{0,1},{1,0},{2,3},{3,2},{4,5},{5,4},{6,7},{7,6},{8,9},{9,8},{10,11... | collective-permute-start | bytes 786440 | tf_op jit(solution)/shard_map/ppermute | solution.py:40
  10.5 0.1 maximum_bitcast_fusion.1.frequency_ref
  10.6 0.1 pad_add_fusion.spot_ref
  10.7 0.0 copy-done
  10.7 1.7 %shard_map.59 = (f32[6,256,128]{2,1,0:T(8,128)S(1)}, f32[6,256,128]{2,1,0:T(8,128)S(1)}) custom-call(s32[1,8]{1,0:T(1,128)S(1)} %copy-done, s32[2]{0:T(128)S(1)} %pad_add_fusion.spot_ref, f32[1,128]{1,0:T(1,128)S(1)} %maximum_bitcast_fusion.1.frequency_ref), custom_call_target="tpu_custom_call" | custom-call | flops 4000000 | tf_op jit(solution)/shard_map/pallas_call | solution.py:372
  12.4 0.0 collective-permute-done.2.k_other
  12.4 0.0 collective-permute-done.5.got_ref
  12.4 4.7 %shard_map.60 = (bf16[2,4,512,128]{3,2,1,0:T(8,128)(2,1)S(1)}, bf16[8,256,128]{2,1,0:T(8,128)(2,1)S(1)}, bf16[3,4,256,512]{3,2,1,0:T(8,128)(2,1)}, f32[3,4,512]{...) custom-call(s32[1,8]{1,0:T(1,128)S(1)} %copy-done, s32[2]{0:T(128)S(1)} %pad_add_fusion.spot_ref, ...), custom_call_target="tpu_custom_call" | custom-call | flops 6000000 | tf_op jit(solution)/shard_map/pallas_call | solution.py:372
  17.1 4.3 %collective-permute-start.6 = (bf16[8,256,128]{2,1,0:T(8,128)(2,1)S(1)}, bf16[8,256,128]{2,1,0:T(8,128)(2,1)S(1)}, u32[]{:S(2)}, u32[]{:S(2)}) collective-permute-start(bf16[8,256,128]{2,1,0:T(8,128)(2,1)S(1)} %get-tuple-element.30.v0_ref), channel_id=1, source_target_pairs={{0,2},{1,3},{2,4},{3,5},{4,6},{5,7},{6,8},{7,9},{8,10},{9,11},{10,... | collective-permute-start | bytes 1572872 | tf_op jit(solution)/shard_map/ppermute | solution.py:36
  21.4 4.3 %collective-permute-start = (bf16[4,256,128]{2,1,0:T(8,128)(2,1)S(1)}, bf16[4,256,128]{2,1,0:T(8,128)(2,1)S(1)}, u32[]{:S(2)}, u32[]{:S(2)}) collective-permute-start(bf16[4,256,128]{2,1,0:T(8,128)(2,1)S(1)} %get-tuple-element.49), channel_id=1, source_target_pairs={{0,2},{1,3},{2,4},{3,5},{4,6},{5,7},{6,8},{7,9},{8,10},{9,11},{10,... | collective-permute-start | bytes 786440 | tf_op jit(solution)/shard_map/ppermute | solution.py:36
  25.7 4.3 %collective-permute-start.3 = (bf16[4,256,128]{2,1,0:T(8,128)(2,1)S(1)}, bf16[4,256,128]{2,1,0:T(8,128)(2,1)S(1)}, u32[]{:S(2)}, u32[]{:S(2)}) collective-permute-start(bf16[4,256,128]{2,1,0:T(8,128)(2,1)S(1)} %collective-permute-done.2.k_other), channel_id=1, source_target_pairs={{0,2},{1,3},{2,4},{3,5},{4,6},{5,7},{6,8},{7,9},{8,10},{9,11},{10,... | collective-permute-start | bytes 786440 | tf_op jit(solution)/shard_map/ppermute | solution.py:36
  30.0 3.7 %collective-permute-done.6.v1_ref = bf16[8,256,128]{2,1,0:T(8,128)(2,1)S(1)} collective-permute-done((bf16[8,256,128]{2,1,0:T(8,128)(2,1)S(1)}, bf16[8,256,128]{2,1,0:T(8,128)(2,1)S(1)}, u32[]{:S(2)}, u32[]{:S(2)}) %collective-permute-start.6) | collective-permute-done | bytes 524320 | tf_op jit(solution)/shard_map/ppermute | solution.py:36
  33.7 4.4 %collective-permute-start.7 = (bf16[8,256,128]{2,1,0:T(8,128)(2,1)S(1)}, bf16[8,256,128]{2,1,0:T(8,128)(2,1)S(1)}, u32[]{:S(2)}, u32[]{:S(2)}) collective-permute-start(bf16[8,256,128]{2,1,0:T(8,128)(2,1)S(1)} %collective-permute-done.6.v1_ref), channel_id=1, source_target_pairs={{0,2},{1,3},{2,4},{3,5},{4,6},{5,7},{6,8},{7,9},{8,10},{9,11},{10,... | collective-permute-start | bytes 1572872 | tf_op jit(solution)/shard_map/ppermute | solution.py:36
  38.1 1.2 collective-permute-done.k_own
  39.3 4.4 %collective-permute-start.1 = (bf16[4,256,128]{2,1,0:T(8,128)(2,1)S(1)}, bf16[4,256,128]{2,1,0:T(8,128)(2,1)S(1)}, u32[]{:S(2)}, u32[]{:S(2)}) collective-permute-start(bf16[4,256,128]{2,1,0:T(8,128)(2,1)S(1)} %collective-permute-done.k_own), channel_id=1, source_target_pairs={{0,2},{1,3},{2,4},{3,5},{4,6},{5,7},{6,8},{7,9},{8,10},{9,11},{10,... | collective-permute-start | bytes 786440 | tf_op jit(solution)/shard_map/ppermute | solution.py:36
  43.7 1.2 collective-permute-done.3.k_other
  44.9 4.4 %collective-permute-start.4 = (bf16[4,256,128]{2,1,0:T(8,128)(2,1)S(1)}, bf16[4,256,128]{2,1,0:T(8,128)(2,1)S(1)}, u32[]{:S(2)}, u32[]{:S(2)}) collective-permute-start(bf16[4,256,128]{2,1,0:T(8,128)(2,1)S(1)} %collective-permute-done.3.k_other), channel_id=1, source_target_pairs={{0,2},{1,3},{2,4},{3,5},{4,6},{5,7},{6,8},{7,9},{8,10},{9,11},{10,... | collective-permute-start | bytes 786440 | tf_op jit(solution)/shard_map/ppermute | solution.py:36
  49.3 4.8 %shard_map.61 = (bf16[4,4,256,512]{3,2,1,0:T(8,128)(2,1)}, f32[4,4,512]{2,1,0:T(4,128)S(1)}, f32[8,512]{1,0:T(8,128)S(1)}, f32[8,512]{1,0:T(8,128)S(1)}) custom-call(s32[1,8]{1,0:T(1,128)S(1)} %copy-done, s32[2]{0:T(128)S(1)} %pad_add_fusion.spot_ref, f32[6,256,128]{2,1,0:T(8,128)S(1)} %get-tuple-element.20.cos_ref, ...), custom_call_target="tpu_custom_call" | custom-call | flops 6000000 | tf_op jit(solution)/shard_map/pallas_call | solution.py:372
  54.2 7.6 %collective-permute-done.1.k_own = bf16[4,256,128]{2,1,0:T(8,128)(2,1)S(1)} collective-permute-done((bf16[4,256,128]{2,1,0:T(8,128)(2,1)S(1)}, bf16[4,256,128]{2,1,0:T(8,128)(2,1)S(1)}, u32[]{:S(2)}, u32[]{:S(2)}) %collective-permute-start.1) | collective-permute-done | bytes 262176 | tf_op jit(solution)/shard_map/ppermute | solution.py:36
  61.8 4.7 %collective-permute-done.4.k_other = bf16[4,256,128]{2,1,0:T(8,128)(2,1)S(1)} collective-permute-done((bf16[4,256,128]{2,1,0:T(8,128)(2,1)S(1)}, bf16[4,256,128]{2,1,0:T(8,128)(2,1)S(1)}, u32[]{:S(2)}, u32[]{:S(2)}) %collective-permute-start.4) | collective-permute-done | bytes 262176 | tf_op jit(solution)/shard_map/ppermute | solution.py:36
  66.5 4.2 %shard_map.62 = (bf16[3,4,256,512]{3,2,1,0:T(8,128)(2,1)}, f32[3,4,512]{2,1,0:T(4,128)S(1)}, f32[8,512]{1,0:T(8,128)S(1)}, f32[16,128]{1,0:T(8,128)S(1)}) custom-call(s32[1,8]{1,0:T(1,128)S(1)} %copy-done, s32[2]{0:T(128)S(1)} %pad_add_fusion.spot_ref, f32[6,256,128]{2,1,0:T(8,128)S(1)} %get-tuple-element.20.cos_ref, ...), custom_call_target="tpu_custom_call" | custom-call | flops 6000000 | tf_op jit(solution)/shard_map/pallas_call | solution.py:372
  70.7 4.5 %shard_map.63 = (f32[4,128,512]{2,1,0:T(8,128)S(1)}, f32[4,128,512]{2,1,0:T(8,128)S(1)}) custom-call(s32[2]{0:T(128)S(1)} %pad_add_fusion.spot_ref, f32[8,512]{1,0:T(8,128)S(1)} %get-tuple-element.27.level_ref, bf16[3,4,256,512]{3,2,1,0:T(8,128)(2,1)} %get-tuple-element.31.weight_0, f32[3,4,512]{2,1,0:T(4,128)S(1)} %get-tuple-element.32.mark_0, ...), custom_call_target="tpu_custom_call" | custom-call | flops 3000000 | tf_op jit(solution)/shard_map/pallas_call | solution.py:372
  75.3 0.0 collective-permute-done.7.v2_ref
  75.3 2.3 %shard_map.65 = bf16[8,256,128]{2,1,0:T(8,128)(2,1)S(1)} custom-call(s32[2]{0:T(128)S(1)} %pad_add_fusion.spot_ref, f32[8,512]{1,0:T(8,128)S(1)} %get-tuple-element.27.level_ref, bf16[3,4,256,512]{3,2,1,0:T(8,128)(2,1)} %get-tuple-element.28.weight_2, f32[3,4,512]{2,1,0:T(4,128)S(1)} %get-tuple-element.29.mark_2, ...), custom_call_target="tpu_custom_call" | custom-call | flops 3000000 | tf_op jit(solution)/shard_map/pallas_call | solution.py:372
  77.5 1.9 %collective-permute-start.8 = (bf16[8,256,128]{2,1,0:T(8,128)(2,1)S(1)}, bf16[8,256,128]{2,1,0:T(8,128)(2,1)S(1)}, u32[]{:S(2)}, u32[]{:S(2)}) collective-permute-start(bf16[8,256,128]{2,1,0:T(8,128)(2,1)S(1)} %shard_map.65), channel_id=1, source_target_pairs={{0,1},{1,0},{2,3},{3,2},{4,5},{5,4},{6,7},{7,6},{8,9},{9,8},{10,11... | collective-permute-start | bytes 1572872 | tf_op jit(solution)/shard_map/ppermute | solution.py:40
  79.5 19.2 %all_to_all.15 = f32[16,1,128]{2,1,0:T(1,128)S(1)} all-to-all(f32[16,1,128]{2,1,0:T(1,128)S(1)} %bitcast.36), channel_id=1, replica_groups=mesh['dp_0'=8,'dp_1'=2,'seq_0'=2,'seq_1'=8,'seq_2'=2] {'seq_1','seq_2'}, dimensions={0} | all-to-all | bytes 16384 | tf_op jit(solution)/shard_map/all_to_all | solution.py:465
  98.7 18.6 %all_to_all.16 = f32[32,1,128]{2,1,0:T(1,128)S(1)} all-to-all(f32[32,1,128]{2,1,0:T(1,128)S(1)} %broadcast_in_dim.17), channel_id=1, replica_groups=mesh['dp_0'=8,'dp_1'=2,'seq_0'=2,'seq_1'=8,'seq_2'=2] {'dp_0','dp_1','se..., dimensions={0} | all-to-all | bytes 32768 | tf_op jit(solution)/shard_map/all_to_all | solution.py:469
  117.4 2.6 %shard_map.64 = bf16[8,256,128]{2,1,0:T(8,128)(2,1)S(1)} custom-call(s32[2]{0:T(128)S(1)} %pad_add_fusion.spot_ref, f32[8,512]{1,0:T(8,128)S(1)} %get-tuple-element.27.level_ref, bf16[3,4,256,512]{3,2,1,0:T(8,128)(2,1)} %get-tuple-element.28.weight_2, f32[3,4,512]{2,1,0:T(4,128)S(1)} %get-tuple-element.29.mark_2, ...), custom_call_target="tpu_custom_call" | custom-call | flops 3000000 | tf_op jit(solution)/shard_map/pallas_call | solution.py:372
  120.0 0.0 collective-permute-done.8
  120.1 0.1 broadcast_select_fusion.1
  120.1 0.1 maximum_bitcast_fusion
  120.2 1.6 %copy.25 = bf16[1,256,16,128]{3,2,1,0:T(8,128)(2,1)} copy(bf16[1,256,16,128]{3,1,2,0:T(8,128)(2,1)S(1)} %maximum_bitcast_fusion) | data formatting | bytes 2097152
  (5 shorter events, 0.1 us)
Async XLA Ops:
  3.2 7.4 %copy-start = (s32[1,8]{1,0:T(1,128)S(1)}, s32[1,8]{1,0:T(1,128)}, u32[]{:S(2)}) copy-start(s32[1,8]{1,0:T(1,128)} %lengths_ref.7) | copy-start | bytes 100
  4.3 8.1 %collective-permute-start.5 = (bf16[12,256,128]{2,1,0:T(8,128)(2,1)}, bf16[12,256,128]{2,1,0:T(8,128)(2,1)S(1)}, u32[]{:S(2)}, u32[]{:S(2)}) collective-permute-start(bf16[12,256,128]{2,1,0:T(8,128)(2,1)} %pad_maximum_fusion), channel_id=1, source_target_pairs={{0,1},{1,0},{2,3},{3,2},{4,5},{5,4},{6,7},{7,6},{8,9},{9,8},{10,11... | collective-permute-start | bytes 2359304 | tf_op jit(solution)/shard_map/ppermute | solution.py:40
  8.1 4.3 %collective-permute-start.2 = (bf16[4,256,128]{2,1,0:T(8,128)(2,1)}, bf16[4,256,128]{2,1,0:T(8,128)(2,1)S(1)}, u32[]{:S(2)}, u32[]{:S(2)}) collective-permute-start(bf16[4,256,128]{2,1,0:T(8,128)(2,1)} %get-tuple-element.48), channel_id=1, source_target_pairs={{0,1},{1,0},{2,3},{3,2},{4,5},{5,4},{6,7},{7,6},{8,9},{9,8},{10,11... | collective-permute-start | bytes 786440 | tf_op jit(solution)/shard_map/ppermute | solution.py:40
  17.1 16.6 %collective-permute-start.6 = (bf16[8,256,128]{2,1,0:T(8,128)(2,1)S(1)}, bf16[8,256,128]{2,1,0:T(8,128)(2,1)S(1)}, u32[]{:S(2)}, u32[]{:S(2)}) collective-permute-start(bf16[8,256,128]{2,1,0:T(8,128)(2,1)S(1)} %get-tuple-element.30.v0_ref), channel_id=1, source_target_pairs={{0,2},{1,3},{2,4},{3,5},{4,6},{5,7},{6,8},{7,9},{8,10},{9,11},{10,... | collective-permute-start | bytes 1572872 | tf_op jit(solution)/shard_map/ppermute | solution.py:36
  21.4 17.9 %collective-permute-start = (bf16[4,256,128]{2,1,0:T(8,128)(2,1)S(1)}, bf16[4,256,128]{2,1,0:T(8,128)(2,1)S(1)}, u32[]{:S(2)}, u32[]{:S(2)}) collective-permute-start(bf16[4,256,128]{2,1,0:T(8,128)(2,1)S(1)} %get-tuple-element.49), channel_id=1, source_target_pairs={{0,2},{1,3},{2,4},{3,5},{4,6},{5,7},{6,8},{7,9},{8,10},{9,11},{10,... | collective-permute-start | bytes 786440 | tf_op jit(solution)/shard_map/ppermute | solution.py:36
  25.7 19.2 %collective-permute-start.3 = (bf16[4,256,128]{2,1,0:T(8,128)(2,1)S(1)}, bf16[4,256,128]{2,1,0:T(8,128)(2,1)S(1)}, u32[]{:S(2)}, u32[]{:S(2)}) collective-permute-start(bf16[4,256,128]{2,1,0:T(8,128)(2,1)S(1)} %collective-permute-done.2.k_other), channel_id=1, source_target_pairs={{0,2},{1,3},{2,4},{3,5},{4,6},{5,7},{6,8},{7,9},{8,10},{9,11},{10,... | collective-permute-start | bytes 786440 | tf_op jit(solution)/shard_map/ppermute | solution.py:36
  33.7 41.6 %collective-permute-start.7 = (bf16[8,256,128]{2,1,0:T(8,128)(2,1)S(1)}, bf16[8,256,128]{2,1,0:T(8,128)(2,1)S(1)}, u32[]{:S(2)}, u32[]{:S(2)}) collective-permute-start(bf16[8,256,128]{2,1,0:T(8,128)(2,1)S(1)} %collective-permute-done.6.v1_ref), channel_id=1, source_target_pairs={{0,2},{1,3},{2,4},{3,5},{4,6},{5,7},{6,8},{7,9},{8,10},{9,11},{10,... | collective-permute-start | bytes 1572872 | tf_op jit(solution)/shard_map/ppermute | solution.py:36
  39.3 22.5 %collective-permute-start.1 = (bf16[4,256,128]{2,1,0:T(8,128)(2,1)S(1)}, bf16[4,256,128]{2,1,0:T(8,128)(2,1)S(1)}, u32[]{:S(2)}, u32[]{:S(2)}) collective-permute-start(bf16[4,256,128]{2,1,0:T(8,128)(2,1)S(1)} %collective-permute-done.k_own), channel_id=1, source_target_pairs={{0,2},{1,3},{2,4},{3,5},{4,6},{5,7},{6,8},{7,9},{8,10},{9,11},{10,... | collective-permute-start | bytes 786440 | tf_op jit(solution)/shard_map/ppermute | solution.py:36
  44.9 21.5 %collective-permute-start.4 = (bf16[4,256,128]{2,1,0:T(8,128)(2,1)S(1)}, bf16[4,256,128]{2,1,0:T(8,128)(2,1)S(1)}, u32[]{:S(2)}, u32[]{:S(2)}) collective-permute-start(bf16[4,256,128]{2,1,0:T(8,128)(2,1)S(1)} %collective-permute-done.3.k_other), channel_id=1, source_target_pairs={{0,2},{1,3},{2,4},{3,5},{4,6},{5,7},{6,8},{7,9},{8,10},{9,11},{10,... | collective-permute-start | bytes 786440 | tf_op jit(solution)/shard_map/ppermute | solution.py:36
  77.5 42.5 %collective-permute-start.8 = (bf16[8,256,128]{2,1,0:T(8,128)(2,1)S(1)}, bf16[8,256,128]{2,1,0:T(8,128)(2,1)S(1)}, u32[]{:S(2)}, u32[]{:S(2)}) collective-permute-start(bf16[8,256,128]{2,1,0:T(8,128)(2,1)S(1)} %shard_map.65), channel_id=1, source_target_pairs={{0,1},{1,0},{2,3},{3,2},{4,5},{5,4},{6,7},{7,6},{8,9},{9,8},{10,11... | collective-permute-start | bytes 1572872 | tf_op jit(solution)/shard_map/ppermute | solution.py:40
